TPU v7x, 32 devices: a whole 2x2x4 slice. The times are simulated.
32 devices in a mesh: fsdp: 4 (over y, x), expert: 8 (over z, core).
Axes of the slice: x: 2, y: 2, z: 4, core: 2. Of those that a mesh axis runs over, the one named last changes fastest.
Arguments:
- block_input: bfloat16 [8, 512, 2048], P('expert', 'fsdp'), may hold values from -6 to 6
- cotangent: bfloat16 [8, 512, 2048], P('expert', 'fsdp'), may hold values from -6 to 6
- w_query: bfloat16 [2048, 2048], P(None, 'fsdp'), may hold values from -0.125 to 0.125
- w_key: bfloat16 [2048, 2048], P(None, 'fsdp'), may hold values from -0.125 to 0.125
- w_value: bfloat16 [2048, 2048], P(None, 'fsdp'), may hold values from -0.125 to 0.125
- w_output: bfloat16 [2048, 2048], P('fsdp'), may hold values from -0.75 to 0.75
- q_gain: float32 [2048], P('fsdp'), may hold values from 0.7 to 1.3
- k_gain: float32 [2048], P('fsdp'), may hold values from 0.7 to 1.3
- attn_gain: float32 [2048], replicated, may hold values from 0.1 to 1.9
- mlp_gain: float32 [2048], replicated, may hold values from 0.1 to 1.9
- w_router: bfloat16 [2048, 16], replicated, may hold values from -0.125 to 0.125
- w_gate: bfloat16 [16, 2048, 1024], P('expert', None, 'fsdp'), may hold values from -0.125 to 0.125
- w_up: bfloat16 [16, 2048, 1024], P('expert', None, 'fsdp'), may hold values from -0.125 to 0.125
- w_down: bfloat16 [16, 1024, 2048], P('expert', 'fsdp'), may hold values from -0.5 to 0.5
- segments: int32 [8, 512], P('expert', 'fsdp'), may hold values from 0 to 1, as said below
- routes: int32 [8, 512, 8], P('expert', 'fsdp'), may hold values from 0 to 15, all different within a row; in each aligned block of 128 rows (0 to 127, 128 to 255, ..., all dimensions but the last counted through in order) at most 96 rows name the same one
- capacity: int32 [16], replicated, may hold values from 48 to 96
Outputs:
- block_output: bfloat16 [8, 512, 2048], P('expert', 'fsdp')
- grad_input: float32 [8, 512, 2048], P('expert', 'fsdp')
- grad_query: float32 [2048, 2048], P(None, 'fsdp')
- grad_key: float32 [2048, 2048], P(None, 'fsdp')
- grad_value: float32 [2048, 2048], P(None, 'fsdp')
- grad_w_output: float32 [2048, 2048], P('fsdp')
- grad_q_gain: float32 [2048], P('fsdp')
- grad_k_gain: float32 [2048], P('fsdp')
- grad_attn_gain: float32 [2048], replicated
- grad_mlp_gain: float32 [2048], replicated
- grad_router: float32 [2048, 16], replicated
- grad_gate: float32 [16, 2048, 1024], P('expert', None, 'fsdp')
- grad_up: float32 [16, 2048, 1024], P('expert', None, 'fsdp')
- grad_down: float32 [16, 1024, 2048], P('expert', 'fsdp')
Inputs may be any that keep to these rules, and one draw needn't show every extreme that they name: `segments`: segment ids start at 0 and never fall along the rows of a group; each group holds exactly 2 sequences. `routes`: each token names 8 different experts; among the tokens of one device no expert is named more than 96 times.
All inputs are finite; a program needn't handle non-finite values.
Results may differ from a plain program's by a relative error of at most 0.017.
Values may be sent and summed in bfloat16 or wider, within the bound.
A program may use at most 384 MiB of HBM per device.

v0:
```python
import jax
import jax.numpy as jnp
from jax import lax
from jax.sharding import PartitionSpec as P

HEAD_DIM = 128
TOP = 8


epsilon = 1e-05
rope_base = 10000.0
precise = lax.Precision.HIGHEST


def rope_tables(seg_ids, head_dim):
    length = seg_ids.shape[0]
    ordinal = lax.iota(jnp.int32, length)
    earlier = (seg_ids[:, None] == seg_ids[None, :]) & (ordinal[None, :] < ordinal[:, None])
    places = jnp.sum(earlier.astype(jnp.int32), axis=1).astype(jnp.float32)
    half_dim = head_dim // 2
    inv_freq = rope_base ** (
        -(lax.iota(jnp.int32, half_dim).astype(jnp.float32) * (2.0 / head_dim))
    )
    angles = places[:, None] * inv_freq[None, :]
    angles = jnp.concatenate([angles, angles], axis=1)
    return (jnp.cos(angles), jnp.sin(angles))


def rotate_half(values):
    half_dim = values.shape[-1] // 2
    return jnp.concatenate([-values[..., half_dim:], values[..., :half_dim]], axis=-1)


def rotate_back(values):
    half_dim = values.shape[-1] // 2
    return jnp.concatenate([values[..., half_dim:], -values[..., :half_dim]], axis=-1)


def apply_rope(values, cosine, sine_table):
    return values * cosine[:, None, :] + rotate_half(values) * sine_table[:, None, :]


def rope_grad(grads_in, cosine, sine_table):
    return grads_in * cosine[:, None, :] + rotate_back(grads_in * sine_table[:, None, :])


def across_heads(pair_sums):
    return lax.psum((pair_sums[0], pair_sums[1]), "fsdp")


def share_rows(term_fn, own_rows):
    return lax.psum_scatter(
        term_fn(jnp.int32(0), own_rows * lax.axis_size("fsdp")),
        "fsdp",
        scatter_dimension=0,
        tiled=True,
    )


def to_owner(block_rows):
    return lax.all_to_all(block_rows, "expert", split_axis=0, concat_axis=0, tiled=True)


def from_owner(block_rows):
    return lax.all_to_all(block_rows, "expert", split_axis=0, concat_axis=0, tiled=True)


def shard_gather(block_rows):
    return lax.all_gather(block_rows, "fsdp", axis=0, tiled=True)


def owner_sum(term_fn, sources):
    own_rows = sources // lax.axis_size("fsdp")
    return lax.psum_scatter(
        term_fn(jnp.int32(0), own_rows * lax.axis_size("fsdp")),
        "fsdp",
        scatter_dimension=0,
        tiled=True,
    )


def head_scores(q_heads, k_heads, allowed):
    scores = jnp.einsum(
        "thd,shd->hts", q_heads, k_heads, preferred_element_type=jnp.float32
    ) * HEAD_DIM ** (-0.5)
    return jnp.where(allowed[None], scores, -1e30)


def on_device(
    block_input,
    cotangent,
    w_query,
    w_key,
    w_value,
    w_output,
    q_gain,
    k_gain,
    attn_gain,
    mlp_gain,
    w_router,
    w_gate,
    w_up,
    w_down,
    segments,
    routes,
    capacity,
):
    tok_count = block_input.shape[1]
    model_width = block_input.shape[2]
    experts = w_router.shape[1]
    local_experts = w_gate.shape[0]
    slot_count = tok_count * TOP * 3 // (2 * experts)
    pair_count = tok_count * TOP
    zero_row = jnp.zeros((1, model_width), jnp.bfloat16)
    flat_in = block_input[0].astype(jnp.float32)
    scale_one = lax.rsqrt(jnp.mean(flat_in * flat_in, axis=1, keepdims=True) + epsilon)
    normed_one = flat_in * scale_one
    first_rows = (normed_one * attn_gain).astype(jnp.bfloat16)
    group_rows, group_segs = (
        lax.all_gather(first_rows, "fsdp", axis=0, tiled=True),
        lax.all_gather(segments[0], "fsdp", axis=0, tiled=True),
    )
    group_len = group_rows.shape[0]
    heads_here = w_query.shape[1] // HEAD_DIM
    query_rows = jnp.dot(group_rows, w_query, preferred_element_type=jnp.float32)
    key_rows = jnp.dot(group_rows, w_key, preferred_element_type=jnp.float32)
    value_rows = jnp.dot(group_rows, w_value, preferred_element_type=jnp.float32).astype(
        jnp.bfloat16
    )
    square_sums = across_heads(
        (jnp.sum(query_rows * query_rows, axis=1), jnp.sum(key_rows * key_rows, axis=1))
    )
    q_scale = lax.rsqrt(square_sums[0][:, None] / model_width + epsilon)
    k_scale = lax.rsqrt(square_sums[1][:, None] / model_width + epsilon)
    cosine, sine_table = rope_tables(group_segs, HEAD_DIM)
    head_shape = (group_len, heads_here, HEAD_DIM)
    q_heads = apply_rope(
        (query_rows * q_scale * q_gain).reshape(head_shape), cosine, sine_table
    ).astype(jnp.bfloat16)
    k_heads = apply_rope(
        (key_rows * k_scale * k_gain).reshape(head_shape), cosine, sine_table
    ).astype(jnp.bfloat16)
    v_heads = value_rows.reshape(head_shape)
    ordinal = lax.iota(jnp.int32, group_len)
    allowed = (group_segs[:, None] == group_segs[None, :]) & (ordinal[None, :] <= ordinal[:, None])
    scores = head_scores(q_heads, k_heads, allowed)
    row_top = jnp.max(scores, axis=2, keepdims=True)
    log_total = row_top + jnp.log(jnp.sum(jnp.exp(scores - row_top), axis=2, keepdims=True))
    attn_weights = jnp.exp(scores - log_total)
    mixed_heads = jnp.einsum(
        "hts,shd->thd",
        attn_weights.astype(jnp.bfloat16),
        v_heads,
        preferred_element_type=jnp.float32,
    )
    attn_rows = mixed_heads.reshape(group_len, heads_here * HEAD_DIM).astype(jnp.bfloat16)

    def mixed_term(start, length):
        return jnp.dot(attn_rows, w_output, preferred_element_type=jnp.float32)

    mixed_rows = share_rows(mixed_term, tok_count)
    second_in = flat_in + mixed_rows
    scale_two = lax.rsqrt(jnp.mean(second_in * second_in, axis=1, keepdims=True) + epsilon)
    normed_two = second_in * scale_two
    second_rows = (normed_two * mlp_gain).astype(jnp.bfloat16)
    logits = jnp.dot(second_rows, w_router, preferred_element_type=jnp.float32)
    chosen = routes[0]
    expert_ids = lax.iota(jnp.int32, experts)
    chosen_hot = (chosen[:, :, None] == expert_ids[None, None, :]).astype(jnp.float32)
    routed = jnp.sum(chosen_hot * logits[:, None, :], axis=2)
    gate_wts = jax.nn.softmax(routed, axis=1)
    pair_hot = chosen_hot.reshape(pair_count, experts).astype(jnp.int32)
    earlier_hits = jnp.cumsum(pair_hot, axis=0) - pair_hot
    ranking = jnp.sum(earlier_hits * pair_hot, axis=1)
    cap_pair = jnp.sum(pair_hot * capacity[None, :], axis=1)
    is_kept = ranking < cap_pair
    pair_route = chosen.reshape(pair_count)
    slot_place = jnp.where(is_kept, pair_route * slot_count + ranking, experts * slot_count)
    pair_ids = lax.iota(jnp.int32, pair_count)
    slot_pair = (
        jnp.full((experts * slot_count,), pair_count, jnp.int32)
        .at[slot_place]
        .set(pair_ids, mode="drop")
    )
    padded = jnp.concatenate([second_rows, zero_row], axis=0)
    outgoing = padded[slot_pair // TOP].reshape(experts, slot_count, model_width)
    arrived = shard_gather(to_owner(outgoing))
    gate_w, up_w, down_w = (w_gate, w_up, w_down)
    owner_rows = arrived.reshape(-1, local_experts, slot_count, model_width)
    sources = owner_rows.shape[0]
    gate_act = jnp.einsum("sjcd,jdh->sjch", owner_rows, gate_w, preferred_element_type=jnp.float32)
    up_act = jnp.einsum("sjcd,jdh->sjch", owner_rows, up_w, preferred_element_type=jnp.float32)
    sig_gate = jax.nn.sigmoid(gate_act)
    silu_gate = gate_act * sig_gate
    hidden = (silu_gate * up_act).astype(jnp.bfloat16)

    def down_term(start, length):
        return jnp.einsum("sjch,jhd->sjcd", hidden, down_w, preferred_element_type=jnp.float32)

    produced = owner_sum(down_term, sources)
    returned = from_owner(produced.astype(jnp.bfloat16).reshape(-1, slot_count, model_width))
    slot_rows = jnp.concatenate(
        [returned.reshape(experts * slot_count, model_width), zero_row], axis=0
    )
    pair_rows = slot_rows[slot_place].reshape(tok_count, TOP, model_width).astype(jnp.float32)
    kept_mask = is_kept.reshape(tok_count, TOP).astype(jnp.float32)
    gate_kept = gate_wts * kept_mask
    moe_rows = jnp.sum(gate_kept[:, :, None] * pair_rows, axis=1)
    final_rows = second_in + moe_rows
    block_output = final_rows.astype(jnp.bfloat16)[None]
    grad_out = cotangent[0].astype(jnp.float32)
    grad_gate_k = jnp.sum(pair_rows * grad_out[:, None, :], axis=2) * kept_mask
    grad_routed = gate_wts * (grad_gate_k - jnp.sum(gate_wts * grad_gate_k, axis=1, keepdims=True))
    grad_logits = jnp.sum(chosen_hot * grad_routed[:, :, None], axis=1)
    router_grad = jnp.dot(second_rows.astype(jnp.float32).T, grad_logits, precision=precise)
    grad_second = jnp.dot(grad_logits, w_router.astype(jnp.float32).T, precision=precise)
    pair_grads = (
        (gate_kept[:, :, None] * grad_out[:, None, :])
        .astype(jnp.bfloat16)
        .reshape(pair_count, model_width)
    )
    pair_grads = jnp.concatenate([pair_grads, zero_row], axis=0)
    slot_grads = pair_grads[slot_pair].reshape(experts, slot_count, model_width)
    grad_blocks = shard_gather(to_owner(slot_grads)).reshape(
        -1, local_experts, slot_count, model_width
    )
    grad_hidden = jnp.einsum(
        "sjcd,jhd->sjch", grad_blocks, down_w, preferred_element_type=jnp.float32
    )
    grad_down_w = jnp.einsum(
        "sjch,sjcd->jhd", hidden, grad_blocks, preferred_element_type=jnp.float32
    )
    grad_gate_in = (grad_hidden * up_act * sig_gate * (1.0 + gate_act * (1.0 - sig_gate))).astype(
        jnp.bfloat16
    )
    grad_up_in = (grad_hidden * silu_gate).astype(jnp.bfloat16)
    grad_gate_w = jnp.einsum(
        "sjcd,sjch->jdh", owner_rows, grad_gate_in, preferred_element_type=jnp.float32
    )
    grad_up_w = jnp.einsum(
        "sjcd,sjch->jdh", owner_rows, grad_up_in, preferred_element_type=jnp.float32
    )

    def back_term(start, length):
        from_gate = jnp.einsum(
            "sjch,jdh->sjcd", grad_gate_in, gate_w, preferred_element_type=jnp.float32
        )
        from_up = jnp.einsum("sjch,jdh->sjcd", grad_up_in, up_w, preferred_element_type=jnp.float32)
        return from_gate + from_up

    grad_slots = from_owner(
        owner_sum(back_term, sources).astype(jnp.bfloat16).reshape(-1, slot_count, model_width)
    )
    back_rows = jnp.concatenate(
        [grad_slots.reshape(experts * slot_count, model_width), zero_row], axis=0
    )
    grad_second = grad_second + jnp.sum(
        back_rows[slot_place].reshape(tok_count, TOP, model_width).astype(jnp.float32), axis=1
    )
    mlp_gain_grad = jnp.sum(grad_second * normed_two, axis=0)
    grad_normed_two = grad_second * mlp_gain
    grad_mid = grad_out + scale_two * (
        grad_normed_two - normed_two * jnp.mean(grad_normed_two * normed_two, axis=1, keepdims=True)
    )
    group_grad = lax.all_gather(grad_mid.astype(jnp.bfloat16), "fsdp", axis=0, tiled=True)
    out_grad = jnp.einsum("ti,td->id", attn_rows, group_grad, preferred_element_type=jnp.float32)
    grad_attn = (
        jnp.einsum("td,id->ti", group_grad, w_output, preferred_element_type=jnp.float32)
        .astype(jnp.bfloat16)
        .reshape(head_shape)
    )
    scores_again = head_scores(q_heads, k_heads, allowed)
    weights_again = jnp.exp(scores_again - log_total)
    grad_values = jnp.einsum(
        "hts,thd->shd",
        weights_again.astype(jnp.bfloat16),
        grad_attn,
        preferred_element_type=jnp.float32,
    )
    grad_weights = jnp.einsum(
        "thd,shd->hts", grad_attn, v_heads, preferred_element_type=jnp.float32
    )
    inner_sum = jnp.sum(weights_again * grad_weights, axis=2, keepdims=True)
    grad_scores = (weights_again * (grad_weights - inner_sum)).astype(jnp.bfloat16)
    grad_q_heads = jnp.einsum(
        "hts,shd->thd", grad_scores, k_heads, preferred_element_type=jnp.float32
    ) * HEAD_DIM ** (-0.5)
    grad_k_heads = jnp.einsum(
        "hts,thd->shd", grad_scores, q_heads, preferred_element_type=jnp.float32
    ) * HEAD_DIM ** (-0.5)
    grad_q_normed = rope_grad(grad_q_heads, cosine, sine_table).reshape(group_len, -1)
    grad_k_normed = rope_grad(grad_k_heads, cosine, sine_table).reshape(group_len, -1)
    q_gain_grad = jnp.sum(grad_q_normed * query_rows * q_scale, axis=0)
    k_gain_grad = jnp.sum(grad_k_normed * key_rows * k_scale, axis=0)
    inner_q = grad_q_normed * q_gain
    inner_k = grad_k_normed * k_gain
    inner_sums = across_heads(
        (jnp.sum(inner_q * query_rows, axis=1), jnp.sum(inner_k * key_rows, axis=1))
    )
    grad_query_rows = (
        q_scale
        * (inner_q - query_rows * q_scale * q_scale * (inner_sums[0][:, None] / model_width))
    ).astype(jnp.bfloat16)
    grad_key_rows = (
        k_scale * (inner_k - key_rows * k_scale * k_scale * (inner_sums[1][:, None] / model_width))
    ).astype(jnp.bfloat16)
    grad_value_rows = grad_values.reshape(group_len, -1).astype(jnp.bfloat16)
    query_grad = jnp.einsum(
        "td,ti->di", group_rows, grad_query_rows, preferred_element_type=jnp.float32
    )
    key_grad = jnp.einsum(
        "td,ti->di", group_rows, grad_key_rows, preferred_element_type=jnp.float32
    )
    value_grad = jnp.einsum(
        "td,ti->di", group_rows, grad_value_rows, preferred_element_type=jnp.float32
    )

    def input_term(start, length):
        from_q = jnp.einsum(
            "ti,di->td", grad_query_rows, w_query, preferred_element_type=jnp.float32
        )
        from_k = jnp.einsum("ti,di->td", grad_key_rows, w_key, preferred_element_type=jnp.float32)
        from_v = jnp.einsum(
            "ti,di->td", grad_value_rows, w_value, preferred_element_type=jnp.float32
        )
        return from_q + from_k + from_v

    grad_first = share_rows(input_term, tok_count)
    attn_gain_grad = jnp.sum(grad_first * normed_one, axis=0)
    grad_normed_one = grad_first * attn_gain
    grad_x = grad_mid + scale_one * (
        grad_normed_one - normed_one * jnp.mean(grad_normed_one * normed_one, axis=1, keepdims=True)
    )
    mixer = lax.psum(
        (query_grad, key_grad, value_grad, out_grad, q_gain_grad, k_gain_grad), "expert"
    )
    shared = lax.psum((attn_gain_grad, mlp_gain_grad, router_grad), ("fsdp", "expert"))
    return (
        block_output,
        grad_x[None],
        mixer[0],
        mixer[1],
        mixer[2],
        mixer[3],
        mixer[4],
        mixer[5],
        shared[0],
        shared[1],
        shared[2],
        grad_gate_w,
        grad_up_w,
        grad_down_w,
    )


def solution(mesh):
    placed = (
        P("expert", "fsdp", None),
        P("expert", "fsdp", None),
        P(None, "fsdp"),
        P(None, "fsdp"),
        P(None, "fsdp"),
        P("fsdp", None),
        P("fsdp"),
        P("fsdp"),
        P(),
        P(),
        P(),
        P("expert", None, "fsdp"),
        P("expert", None, "fsdp"),
        P("expert", "fsdp", None),
        P("expert", "fsdp"),
        P("expert", "fsdp", None),
        P(),
    )
    return jax.shard_map(
        on_device,
        mesh=mesh,
        in_specs=placed,
        out_specs=(
            P("expert", "fsdp", None),
            P("expert", "fsdp", None),
            P(None, "fsdp"),
            P(None, "fsdp"),
            P(None, "fsdp"),
            P("fsdp", None),
            P("fsdp"),
            P("fsdp"),
            P(),
            P(),
            P(),
            P("expert", None, "fsdp"),
            P("expert", None, "fsdp"),
            P("expert", "fsdp", None),
        ),
        check_vma=False,
    )
```

profile of v0, /device:TPU:0, one launch (start us, length us, event | category | flops | bytes accessed | tf_op | source)
XLA Modules:
  0.0 5057.8 jit_solution(2037723887730777735)
XLA Ops:
  11.3 9.5 all-gather
  23.1 26.2 all-gather.6.cloned.1.call-done
  49.3 3.7 multiply_reduce_fusion.6
  55.3 9.0 all-reduce.11
  78.7 4.5 reduce-window.6
  84.4 4.3 scatter_custom_fusion
  88.8 42.0 reduce-scatter.9.cloned.1.call-done
  134.2 7.2 gather_fusion
  141.3 144.3 %all_to_all.20 = bf16[16,96,2048]{2,1,0:T(8,128)(2,1)} all-to-all(bf16[16,96,2048]{2,1,0:T(8,128)(2,1)} %bitcast.227), channel_id=1, replica_groups=mesh['fsdp'=4,'expert'=8] {'expert'}, dimensions={0} | all-to-all | bytes 12582912 | tf_op jit(solution)/shard_map/all_to_all | solution.py:61
  293.8 16.6 gather_fusion.2
  310.4 144.9 %all_to_all.21 = bf16[16,96,2048]{2,1,0:T(8,128)(2,1)} all-to-all(bf16[16,96,2048]{2,1,0:T(8,128)(2,1)} %bitcast.228), channel_id=1, replica_groups=mesh['fsdp'=4,'expert'=8] {'expert'}, dimensions={0} | all-to-all | bytes 12582912 | tf_op jit(solution)/shard_map/all_to_all | solution.py:61
  457.2 54.1 %all-gather.8.cloned.1.call-done = bf16[64,96,2048]{2,1,0:T(8,128)(2,1)} async-done(((bf16[16,96,2048]{2,1,0:T(8,128)(2,1)}), bf16[64,96,2048]{2,1,0:T(8,128)(2,1)}) %all-gather.8.cloned.1.call-update) | async-done | bytes 25165840 | tf_op jit(solution)/shard_map/all_gather | solution.py:69
  511.3 14.9 fusion.4
  526.3 15.8 fusion.6
  542.1 198.6 %all-gather.10.cloned.1.call-done = bf16[64,96,2048]{2,1,0:T(8,128)(2,1)} async-done(((bf16[16,96,2048]{2,1,0:T(8,128)(2,1)}), bf16[64,96,2048]{2,1,0:T(8,128)(2,1)}) %all-gather.10.cloned.1.call-update) | async-done | bytes 25165840 | tf_op jit(solution)/shard_map/all_gather | solution.py:69
  740.6 19.9 fusion.14
  760.6 21.6 fusion.29
  782.2 34.5 add_bitcast_fusion
  816.7 21.2 convolution_bitcast_fusion
  837.9 3289.4 %all-reduce.19 = (bf16[32,2,96,2048]{3,2,0,1:T(8,128)(2,1)}, bf16[32,2,96,2048]{3,2,0,1:T(8,128)(2,1)}) all-reduce(f32[32,2,96,2048]{3,2,0,1:T(8,128)} %convolution_bitcast_fusion, f32[32,2,96,2048]{3,2,0,1:T(8,128)} %add_bitcast_fusion), channel_id=4, replica_groups=mesh['fsdp'=4,'expert'=8] {'fsdp'}, use_global_device_ids=true, to_apply=%region_18.19.clone | all-reduce | flops 25165824 | bytes 150994944
  4127.3 3.4 constant_dynamic-slice_fusion
  4133.9 5.2 all-to-all-start.3
  4139.1 3.4 constant_dynamic-slice_fusion.1
  4145.7 132.3 %all-to-all-done.3 = bf16[16,96,2048]{2,1,0:T(8,128)(2,1)} async-done(((bf16[16,96,2048]{2,1,0:T(8,128)(2,1)}), bf16[16,96,2048]{2,1,0:T(8,128)(2,1)}, u32[]{:S(2)}, u32[]{:S(2)}) %all-to-all-start.3) | async-done | bytes 6291488 | tf_op jit(solution)/shard_map/all_to_all | solution.py:65
  4278.0 4.9 all-to-all-start.1
  4283.1 6.6 concatenate.41
  4289.7 12.4 gather_fusion.3
  4302.1 6.0 convert_reduce_fusion
  4308.1 113.8 %all-to-all-done.1 = bf16[16,96,2048]{2,1,0:T(8,128)(2,1)} async-done(((bf16[16,96,2048]{2,1,0:T(8,128)(2,1)}), bf16[16,96,2048]{2,1,0:T(8,128)(2,1)}, u32[]{:S(2)}, u32[]{:S(2)}) %all-to-all-start.1) | async-done | bytes 6291488 | tf_op jit(solution)/shard_map/all_to_all | solution.py:65
  4421.8 6.6 concatenate.39
  4428.4 12.5 gather_fusion.1
  4441.0 6.0 fusion.9
  4450.7 34.7 all-gather.12.cloned.1.call-done
  4485.4 3.7 convolution_convert_fusion
  4497.7 8.9 all-reduce.9
  4513.5 3.4 add_add_fusion
  4519.4 5.2 fusion.77
  4524.6 3.3 fusion.75
  4527.9 3.3 fusion.74
  4531.2 3.3 fusion.76
  4534.6 14.5 fusion.20
  4549.1 16.8 convolution_bitcast_fusion.1
  4565.9 17.4 convolution_bitcast_fusion.2
  4583.3 14.6 all-reduce.7
  4599.6 37.0 all-reduce.6
  4639.8 60.5 %all-reduce.16.cloned.1.call-done = f32[2048,16]{0,1:T(8,128)} async-done(((f32[2048,16]{0,1:T(8,128)}), f32[2048,16]{0,1:T(8,128)}) %all-reduce.16.cloned.1.call-update) | async-done | bytes 131088 | tf_op jit(solution)/shard_map/psum | solution.py:337
  4700.3 335.3 %all-reduce.18.cloned.1.call-done = (f32[2048,512]{1,0:T(8,128)}, f32[2048,512]{1,0:T(8,128)}, f32[2048,512]{1,0:T(8,128)}, f32[512,2048]{1,0:T(8,128)}) async-done(((f32[2048,512]{1,0:T(8,128)}, f32[2048,512]{1,0:T(8,128)}, f32[2048,512]{1,0:T(8,128)}, f32[512,2048]{1,0:T(8,128)}), (f32[2048,512]{1,0:T(8,128)}, f32[2048,512]{1,0:T(8,128)}, f32[2048,512]{1,0:T(8,128)}, ...) | async-done | bytes 16777232 | tf_op jit(solution)/shard_map/psum | solution.py:334
  5035.6 4.8 copy.187
  (272 shorter events, 79.4 us)
Async XLA Ops:
  7.2 733.5 %copy-start = (bf16[2,256,2048]{2,1,0:T(8,128)(2,1)S(1)}, bf16[2,256,2048]{2,1,0:T(8,128)(2,1)}, u32[]{:S(2)}) copy-start(bf16[2,256,2048]{2,1,0:T(8,128)(2,1)} %param.30) | copy-start | bytes 6291460
  7.2 42.1 all-gather.6.cloned.1.call-start
  11.2 119.5 %reduce-scatter.9.cloned.1.call-start = ((), (), s32[]{:S(2)}) async-start(), calls=%async_computation.7 | async-start | bytes 5242880 | tf_op jit(solution)/shard_map/reduce_scatter | solution.py:52
  23.1 49.3 copy-start.19
  53.0 12.9 copy-start.13
  53.0 11.3 copy-start.66
  55.3 10.7 copy-start.68
  66.9 4.1 copy-start.39
  67.9 4.4 copy-start.2
  77.9 5.8 copy-start.78
  77.9 52.8 %copy-start.9 = (bf16[1,128,2048]{2,1,0:T(8,128)(2,1)S(1)}, bf16[1,128,2048]{2,1,0:T(8,128)(2,1)}, u32[]{:S(2)}) copy-start(bf16[1,128,2048]{2,1,0:T(8,128)(2,1)} %param.17) | copy-start | bytes 1572868
  77.9 55.2 %copy-start.52 = (f32[2048]{0:T(1024)S(1)}, f32[2048]{0:T(1024)}, u32[]{:S(2)}) copy-start(f32[2048]{0:T(1024)} %param.26) | copy-start | bytes 24580
  78.0 433.4 %all-gather.8.cloned.1.call-start = ((), (), s32[]{:S(2)}) async-start(), calls=%async_computation.8 | async-start | bytes 31457280 | tf_op jit(solution)/shard_map/all_gather | solution.py:69
  132.2 9.1 copy-start.74
  285.6 455.0 %all-gather.10.cloned.1.call-start = ((), (), s32[]{:S(2)}) async-start(), calls=%async_computation.9 | async-start | bytes 31457280 | tf_op jit(solution)/shard_map/all_gather | solution.py:69
  285.8 8.0 copy-start.70
  287.0 6.8 copy-start.16
  289.4 4.4 copy-start.58
  511.3 14.9 copy-start.34
  4133.9 144.1 %all-to-all-start.3 = ((bf16[16,96,2048]{2,1,0:T(8,128)(2,1)}), bf16[16,96,2048]{2,1,0:T(8,128)(2,1)}, u32[]{:S(2)}, u32[]{:S(2)}) async-start(bf16[16,96,2048]{2,1,0:T(8,128)(2,1)} %bitcast.226), calls=%async_computation.4 | async-start | bytes 12582912 | tf_op jit(solution)/shard_map/all_to_all | solution.py:65
  4278.0 4.9 copy-start.73
  4278.0 5.0 copy-start.72
  4278.0 143.8 %all-to-all-start.1 = ((bf16[16,96,2048]{2,1,0:T(8,128)(2,1)}), bf16[16,96,2048]{2,1,0:T(8,128)(2,1)}, u32[]{:S(2)}, u32[]{:S(2)}) async-start(bf16[16,96,2048]{2,1,0:T(8,128)(2,1)} %bitcast.225), calls=%async_computation.2 | async-start | bytes 12582912 | tf_op jit(solution)/shard_map/all_to_all | solution.py:65
  4282.9 202.5 %all-gather.12.cloned.1.call-start = ((), (), s32[]{:S(2)}) async-start(), calls=%async_computation.10 | async-start | bytes 2621440 | tf_op jit(solution)/shard_map/all_gather | solution.py:265
  4428.4 12.5 copy-start.17
  4440.9 6.1 copy-start.59
  4440.9 6.1 copy-start.71
  4440.9 6.2 copy-start.61
  4440.9 6.2 copy-start.8
  4440.9 6.2 copy-start.51
  4440.9 6.2 copy-start.53
  4441.0 6.2 copy-start.75
  4441.0 8.3 copy-start.25
  4449.3 39.8 copy-start.11
  4450.4 38.7 copy-start.20
  4450.4 38.7 copy-start.57
  4450.4 147.5 %reduce-scatter.11.cloned.1.call-start = ((), (), s32[]{:S(2)}) async-start(), calls=%async_computation.11 | async-start | bytes 5242880 | tf_op jit(solution)/shard_map/reduce_scatter | solution.py:52
  4516.9 7.7 copy-start.6
  4516.9 183.4 %all-reduce.16.cloned.1.call-start = ((), (), s32[]{:S(2)}) async-start(), calls=%async_computation.12 | async-start | bytes 262144 | tf_op jit(solution)/shard_map/psum | solution.py:337
  4519.3 516.3 %all-reduce.18.cloned.1.call-start = ((), (), s32[]{:S(2)}) async-start(), calls=%async_computation.13 | async-start | bytes 33554432 | tf_op jit(solution)/shard_map/psum | solution.py:334
  4519.4 5.2 copy-start.24
  4565.9 32.0 copy-start.10
  4565.9 32.0 copy-start.55
  4565.9 32.0 copy-start.77
  4565.9 70.7 %copy-start.12 = (f32[128,2048]{1,0:T(8,128)S(1)}, f32[128,2048]{1,0:T(8,128)}, u32[]{:S(2)}) copy-start(f32[128,2048]{1,0:T(8,128)} %copy-done.11) | copy-start | bytes 3145732
  4565.9 70.7 %copy-start.26 = (bf16[1,128,2048]{2,1,0:T(8,128)(2,1)S(1)}, bf16[1,128,2048]{2,1,0:T(8,128)(2,1)}, u32[]{:S(2)}) copy-start(bf16[1,128,2048]{2,1,0:T(8,128)(2,1)} %param.18) | copy-start | bytes 1572868
  5035.6 4.8 copy-start.33
  5044.2 6.4 copy-start.1
  (42 other events, 83.3 us)
Sparse Core Ops, SparseCore 0:
  11.4 37.8 all-gather.5
  78.1 52.6 reduce-scatter.8
  285.7 225.5 all-gather.7
  513.0 227.5 all-gather.9
  4450.6 34.7 all-gather.11
  4517.0 52.5 reduce-scatter.10
  4575.7 124.4 all-reduce.15
  4703.7 331.8 all-reduce.17
where the time goes:
time: 5070 us; the launch traced here: 5060 us
  blocking collectives  3660 us (72%)
  waiting for transfers between devices  998 us (20%)
  matrix products  225 us (4%)
  local copies, waits for them, and re-layouts  107 us (2%)
    unnamed x1, blocking collectives  3290 us
    psum x1, waiting for transfers between devices, on_device(): lax.psum((query_grad, key_grad, value_grad, out_grad, q_gain_grad, k_gain...  335 us
    all_to_all x2, blocking collectives, to_owner(): lax.all_to_all(block_rows, 'expert', split_axis=0, concat_axis=0, tiled=T...  289 us
    all_gather x2, waiting for transfers between devices, shard_gather(): return lax.all_gather(block_rows, 'fsdp', axis=0, tiled=True)  253 us
    all_to_all x2, waiting for transfers between devices, from_owner(): lax.all_to_all(block_rows, 'expert', split_axis=0, concat_axis=0, tiled=T...  246 us
  transfers between devices with their start and end apart: 10, of which 9 were waited for; matrix products, arithmetic and copies ran while one was open for 3% of the time, Pallas kernels for 0%

commit v1 on v0

--- a/solution.py
+++ b/solution.py
@@ -84,6 +84,189 @@
         "thd,shd->hts", q_heads, k_heads, preferred_element_type=jnp.float32
     ) * HEAD_DIM ** (-0.5)
     return jnp.where(allowed[None], scores, -1e30)
+
+
+def experts_by_slot(
+    second_in, second_rows, cotangent, routes, capacity, w_router, w_gate, w_up, w_down
+):
+    tok_count, model_width = second_rows.shape
+    experts = w_router.shape[1]
+    local_experts = w_gate.shape[0]
+    slot_count = tok_count * TOP * 3 // (2 * experts)
+    pair_count = tok_count * TOP
+    zero_row = jnp.zeros((1, model_width), jnp.bfloat16)
+    logits = jnp.dot(second_rows, w_router, preferred_element_type=jnp.float32)
+    chosen = routes
+    expert_ids = lax.iota(jnp.int32, experts)
+    chosen_hot = (chosen[:, :, None] == expert_ids[None, None, :]).astype(jnp.float32)
+    routed = jnp.sum(chosen_hot * logits[:, None, :], axis=2)
+    gate_wts = jax.nn.softmax(routed, axis=1)
+    pair_hot = chosen_hot.reshape(pair_count, experts).astype(jnp.int32)
+    earlier_hits = jnp.cumsum(pair_hot, axis=0) - pair_hot
+    ranking = jnp.sum(earlier_hits * pair_hot, axis=1)
+    cap_pair = jnp.sum(pair_hot * capacity[None, :], axis=1)
+    is_kept = ranking < cap_pair
+    pair_route = chosen.reshape(pair_count)
+    slot_place = jnp.where(is_kept, pair_route * slot_count + ranking, experts * slot_count)
+    pair_ids = lax.iota(jnp.int32, pair_count)
+    slot_pair = (
+        jnp.full((experts * slot_count,), pair_count, jnp.int32)
+        .at[slot_place]
+        .set(pair_ids, mode="drop")
+    )
+    padded = jnp.concatenate([second_rows, zero_row], axis=0)
+    outgoing = padded[slot_pair // TOP].reshape(experts, slot_count, model_width)
+    arrived = shard_gather(to_owner(outgoing))
+    gate_w, up_w, down_w = (w_gate, w_up, w_down)
+    owner_rows = arrived.reshape(-1, local_experts, slot_count, model_width)
+    sources = owner_rows.shape[0]
+    gate_act = jnp.einsum("sjcd,jdh->sjch", owner_rows, gate_w, preferred_element_type=jnp.float32)
+    up_act = jnp.einsum("sjcd,jdh->sjch", owner_rows, up_w, preferred_element_type=jnp.float32)
+    sig_gate = jax.nn.sigmoid(gate_act)
+    silu_gate = gate_act * sig_gate
+    hidden = (silu_gate * up_act).astype(jnp.bfloat16)
+
+    def down_term(start, length):
+        return jnp.einsum("sjch,jhd->sjcd", hidden, down_w, preferred_element_type=jnp.float32)
+
+    produced = owner_sum(down_term, sources)
+    returned = from_owner(produced.astype(jnp.bfloat16).reshape(-1, slot_count, model_width))
+    slot_rows = jnp.concatenate(
+        [returned.reshape(experts * slot_count, model_width), zero_row], axis=0
+    )
+    pair_rows = slot_rows[slot_place].reshape(tok_count, TOP, model_width).astype(jnp.float32)
+    kept_mask = is_kept.reshape(tok_count, TOP).astype(jnp.float32)
+    gate_kept = gate_wts * kept_mask
+    moe_rows = jnp.sum(gate_kept[:, :, None] * pair_rows, axis=1)
+    final_rows = second_in + moe_rows
+    block_output = final_rows.astype(jnp.bfloat16)
+    grad_out = cotangent.astype(jnp.float32)
+    grad_gate_k = jnp.sum(pair_rows * grad_out[:, None, :], axis=2) * kept_mask
+    grad_routed = gate_wts * (grad_gate_k - jnp.sum(gate_wts * grad_gate_k, axis=1, keepdims=True))
+    grad_logits = jnp.sum(chosen_hot * grad_routed[:, :, None], axis=1)
+    router_grad = jnp.dot(second_rows.astype(jnp.float32).T, grad_logits, precision=precise)
+    grad_second = jnp.dot(grad_logits, w_router.astype(jnp.float32).T, precision=precise)
+    pair_grads = (
+        (gate_kept[:, :, None] * grad_out[:, None, :])
+        .astype(jnp.bfloat16)
+        .reshape(pair_count, model_width)
+    )
+    pair_grads = jnp.concatenate([pair_grads, zero_row], axis=0)
+    slot_grads = pair_grads[slot_pair].reshape(experts, slot_count, model_width)
+    grad_blocks = shard_gather(to_owner(slot_grads)).reshape(
+        -1, local_experts, slot_count, model_width
+    )
+    grad_hidden = jnp.einsum(
+        "sjcd,jhd->sjch", grad_blocks, down_w, preferred_element_type=jnp.float32
+    )
+    grad_down_w = jnp.einsum(
+        "sjch,sjcd->jhd", hidden, grad_blocks, preferred_element_type=jnp.float32
+    )
+    grad_gate_in = (grad_hidden * up_act * sig_gate * (1.0 + gate_act * (1.0 - sig_gate))).astype(
+        jnp.bfloat16
+    )
+    grad_up_in = (grad_hidden * silu_gate).astype(jnp.bfloat16)
+    grad_gate_w = jnp.einsum(
+        "sjcd,sjch->jdh", owner_rows, grad_gate_in, preferred_element_type=jnp.float32
+    )
+    grad_up_w = jnp.einsum(
+        "sjcd,sjch->jdh", owner_rows, grad_up_in, preferred_element_type=jnp.float32
+    )
+
+    def back_term(start, length):
+        from_gate = jnp.einsum(
+            "sjch,jdh->sjcd", grad_gate_in, gate_w, preferred_element_type=jnp.float32
+        )
+        from_up = jnp.einsum("sjch,jdh->sjcd", grad_up_in, up_w, preferred_element_type=jnp.float32)
+        return from_gate + from_up
+
+    grad_slots = from_owner(
+        owner_sum(back_term, sources).astype(jnp.bfloat16).reshape(-1, slot_count, model_width)
+    )
+    back_rows = jnp.concatenate(
+        [grad_slots.reshape(experts * slot_count, model_width), zero_row], axis=0
+    )
+    grad_second = grad_second + jnp.sum(
+        back_rows[slot_place].reshape(tok_count, TOP, model_width).astype(jnp.float32), axis=1
+    )
+    return block_output[None], grad_second, router_grad.T, (grad_gate_w, grad_up_w, grad_down_w)
+
+
+def experts_dense(
+    second_in, second_rows, cotangent, routes, capacity, w_router, w_gate, w_up, w_down
+):
+    tok_count = second_rows.shape[0]
+    experts = w_router.shape[1]
+    local_experts, model_width, hidden_here = w_gate.shape
+    shards = lax.axis_size("fsdp")
+    owners = lax.axis_size("expert")
+    wide = local_experts * hidden_here
+    logits = jnp.dot(second_rows, w_router, preferred_element_type=jnp.float32)
+    expert_ids = lax.iota(jnp.int32, experts)
+    named = jnp.any(routes[:, :, None] == expert_ids[None, None, :], axis=1)
+    before = lax.iota(jnp.int32, tok_count)[None, :] < lax.iota(jnp.int32, tok_count)[:, None]
+    ranking = jnp.dot(
+        before.astype(jnp.bfloat16), named.astype(jnp.bfloat16), preferred_element_type=jnp.float32
+    )
+    kept = named & (ranking < capacity.astype(jnp.float32)[None, :])
+    kept_mask = kept.astype(jnp.float32)
+    top_logit = jnp.max(jnp.where(named, logits, -jnp.inf), axis=1, keepdims=True)
+    powers = jnp.where(named, jnp.exp(jnp.where(named, logits - top_logit, 0.0)), 0.0)
+    gate_wts = powers / jnp.sum(powers, axis=1, keepdims=True)
+    gate_kept = gate_wts * kept_mask
+
+    grad_all = lax.all_gather(cotangent, ("fsdp", "expert"), axis=0, tiled=True)
+    rows_all = lax.all_gather(second_rows, ("fsdp", "expert"), axis=0, tiled=True)
+    kept_all = lax.all_gather(gate_kept, ("fsdp", "expert"), axis=0, tiled=True)
+    first_expert = lax.axis_index("expert") * local_experts
+    gate_here = lax.dynamic_slice_in_dim(kept_all, first_expert, local_experts, axis=1)
+    gate_cols = jnp.repeat(gate_here, hidden_here, axis=1)
+    tokens = rows_all.shape[0]
+
+    gate_w = jnp.transpose(w_gate, (1, 0, 2)).reshape(model_width, wide)
+    up_w = jnp.transpose(w_up, (1, 0, 2)).reshape(model_width, wide)
+    down_w = w_down.reshape(wide, model_width)
+    grad_hid = jnp.einsum("td,hd->th", grad_all, down_w, preferred_element_type=jnp.float32)
+    gate_act = jnp.dot(rows_all, gate_w, preferred_element_type=jnp.float32)
+    up_act = jnp.dot(rows_all, up_w, preferred_element_type=jnp.float32)
+    sig_gate = jax.nn.sigmoid(gate_act)
+    silu_gate = gate_act * sig_gate
+    hidden = silu_gate * up_act
+    gate_terms = jnp.sum((hidden * grad_hid).reshape(tokens, local_experts, hidden_here), axis=2)
+    weighted = (hidden * gate_cols).astype(jnp.bfloat16)
+    grad_hid = grad_hid * gate_cols
+    grad_gate_in = (grad_hid * up_act * sig_gate * (1.0 + gate_act * (1.0 - sig_gate))).astype(
+        jnp.bfloat16
+    )
+    grad_up_in = (grad_hid * silu_gate).astype(jnp.bfloat16)
+    back = (
+        jnp.einsum("th,dh->td", grad_gate_in, gate_w, preferred_element_type=jnp.float32)
+        + jnp.einsum("th,dh->td", grad_up_in, up_w, preferred_element_type=jnp.float32)
+    ).astype(jnp.bfloat16)
+    back_rows = lax.psum_scatter(back, "fsdp", scatter_dimension=0, tiled=True)
+    back_rows = lax.psum_scatter(back_rows, "expert", scatter_dimension=0, tiled=True)
+    terms = lax.psum_scatter(
+        gate_terms.reshape(shards, owners * tok_count, local_experts), "fsdp", scatter_dimension=0, tiled=True
+    ).reshape(owners, tok_count, local_experts)
+    terms = lax.all_to_all(terms, "expert", split_axis=0, concat_axis=0, tiled=True)
+    grad_gate_k = jnp.transpose(terms, (1, 0, 2)).reshape(tok_count, experts) * kept_mask
+    forward = jnp.dot(weighted, down_w, preferred_element_type=jnp.float32).astype(jnp.bfloat16)
+    forward_rows = lax.psum_scatter(forward, "fsdp", scatter_dimension=0, tiled=True)
+    forward_rows = lax.psum_scatter(forward_rows, "expert", scatter_dimension=0, tiled=True)
+    block_output = (second_in + forward_rows.astype(jnp.float32)).astype(jnp.bfloat16)[None]
+    grad_logits = gate_wts * (grad_gate_k - jnp.sum(gate_wts * grad_gate_k, axis=1, keepdims=True))
+    router_grad = jnp.dot(grad_logits.T, second_rows.astype(jnp.float32), precision=precise)
+    grad_second = jnp.dot(grad_logits, w_router.astype(jnp.float32).T, precision=precise)
+    grad_second = grad_second + back_rows.astype(jnp.float32)
+
+    def by_expert(left, right):
+        return jnp.dot(left.T, right, preferred_element_type=jnp.float32)
+
+    parts = [slice(j * hidden_here, (j + 1) * hidden_here) for j in range(local_experts)]
+    grad_gate_w = jnp.stack([by_expert(rows_all, grad_gate_in[:, p]) for p in parts])
+    grad_up_w = jnp.stack([by_expert(rows_all, grad_up_in[:, p]) for p in parts])
+    grad_down_w = by_expert(weighted, grad_all).reshape(local_experts, hidden_here, model_width)
+    return block_output, grad_second, router_grad, (grad_gate_w, grad_up_w, grad_down_w)
 
 
 def on_device(
@@ -107,11 +290,6 @@
 ):
     tok_count = block_input.shape[1]
     model_width = block_input.shape[2]
-    experts = w_router.shape[1]
-    local_experts = w_gate.shape[0]
-    slot_count = tok_count * TOP * 3 // (2 * experts)
-    pair_count = tok_count * TOP
-    zero_row = jnp.zeros((1, model_width), jnp.bfloat16)
     flat_in = block_input[0].astype(jnp.float32)
     scale_one = lax.rsqrt(jnp.mean(flat_in * flat_in, axis=1, keepdims=True) + epsilon)
     normed_one = flat_in * scale_one
@@ -156,107 +334,24 @@
     attn_rows = mixed_heads.reshape(group_len, heads_here * HEAD_DIM).astype(jnp.bfloat16)
 
     def mixed_term(start, length):
-        return jnp.dot(attn_rows, w_output, preferred_element_type=jnp.float32)
-
-    mixed_rows = share_rows(mixed_term, tok_count)
+        return jnp.dot(attn_rows, w_output, preferred_element_type=jnp.float32).astype(jnp.bfloat16)
+
+    mixed_rows = share_rows(mixed_term, tok_count).astype(jnp.float32)
     second_in = flat_in + mixed_rows
     scale_two = lax.rsqrt(jnp.mean(second_in * second_in, axis=1, keepdims=True) + epsilon)
     normed_two = second_in * scale_two
     second_rows = (normed_two * mlp_gain).astype(jnp.bfloat16)
-    logits = jnp.dot(second_rows, w_router, preferred_element_type=jnp.float32)
-    chosen = routes[0]
-    expert_ids = lax.iota(jnp.int32, experts)
-    chosen_hot = (chosen[:, :, None] == expert_ids[None, None, :]).astype(jnp.float32)
-    routed = jnp.sum(chosen_hot * logits[:, None, :], axis=2)
-    gate_wts = jax.nn.softmax(routed, axis=1)
-    pair_hot = chosen_hot.reshape(pair_count, experts).astype(jnp.int32)
-    earlier_hits = jnp.cumsum(pair_hot, axis=0) - pair_hot
-    ranking = jnp.sum(earlier_hits * pair_hot, axis=1)
-    cap_pair = jnp.sum(pair_hot * capacity[None, :], axis=1)
-    is_kept = ranking < cap_pair
-    pair_route = chosen.reshape(pair_count)
-    slot_place = jnp.where(is_kept, pair_route * slot_count + ranking, experts * slot_count)
-    pair_ids = lax.iota(jnp.int32, pair_count)
-    slot_pair = (
-        jnp.full((experts * slot_count,), pair_count, jnp.int32)
-        .at[slot_place]
-        .set(pair_ids, mode="drop")
-    )
-    padded = jnp.concatenate([second_rows, zero_row], axis=0)
-    outgoing = padded[slot_pair // TOP].reshape(experts, slot_count, model_width)
-    arrived = shard_gather(to_owner(outgoing))
-    gate_w, up_w, down_w = (w_gate, w_up, w_down)
-    owner_rows = arrived.reshape(-1, local_experts, slot_count, model_width)
-    sources = owner_rows.shape[0]
-    gate_act = jnp.einsum("sjcd,jdh->sjch", owner_rows, gate_w, preferred_element_type=jnp.float32)
-    up_act = jnp.einsum("sjcd,jdh->sjch", owner_rows, up_w, preferred_element_type=jnp.float32)
-    sig_gate = jax.nn.sigmoid(gate_act)
-    silu_gate = gate_act * sig_gate
-    hidden = (silu_gate * up_act).astype(jnp.bfloat16)
-
-    def down_term(start, length):
-        return jnp.einsum("sjch,jhd->sjcd", hidden, down_w, preferred_element_type=jnp.float32)
-
-    produced = owner_sum(down_term, sources)
-    returned = from_owner(produced.astype(jnp.bfloat16).reshape(-1, slot_count, model_width))
-    slot_rows = jnp.concatenate(
-        [returned.reshape(experts * slot_count, model_width), zero_row], axis=0
-    )
-    pair_rows = slot_rows[slot_place].reshape(tok_count, TOP, model_width).astype(jnp.float32)
-    kept_mask = is_kept.reshape(tok_count, TOP).astype(jnp.float32)
-    gate_kept = gate_wts * kept_mask
-    moe_rows = jnp.sum(gate_kept[:, :, None] * pair_rows, axis=1)
-    final_rows = second_in + moe_rows
-    block_output = final_rows.astype(jnp.bfloat16)[None]
+    experts = w_router.shape[1]
+    if TOP * 2 >= experts:
+        block_output, grad_second, router_grad, expert_grads = experts_dense(
+            second_in, second_rows, cotangent[0], routes[0], capacity, w_router, w_gate, w_up, w_down
+        )
+    else:
+        block_output, grad_second, router_grad, expert_grads = experts_by_slot(
+            second_in, second_rows, cotangent[0], routes[0], capacity, w_router, w_gate, w_up, w_down
+        )
+    grad_gate_w, grad_up_w, grad_down_w = expert_grads
     grad_out = cotangent[0].astype(jnp.float32)
-    grad_gate_k = jnp.sum(pair_rows * grad_out[:, None, :], axis=2) * kept_mask
-    grad_routed = gate_wts * (grad_gate_k - jnp.sum(gate_wts * grad_gate_k, axis=1, keepdims=True))
-    grad_logits = jnp.sum(chosen_hot * grad_routed[:, :, None], axis=1)
-    router_grad = jnp.dot(second_rows.astype(jnp.float32).T, grad_logits, precision=precise)
-    grad_second = jnp.dot(grad_logits, w_router.astype(jnp.float32).T, precision=precise)
-    pair_grads = (
-        (gate_kept[:, :, None] * grad_out[:, None, :])
-        .astype(jnp.bfloat16)
-        .reshape(pair_count, model_width)
-    )
-    pair_grads = jnp.concatenate([pair_grads, zero_row], axis=0)
-    slot_grads = pair_grads[slot_pair].reshape(experts, slot_count, model_width)
-    grad_blocks = shard_gather(to_owner(slot_grads)).reshape(
-        -1, local_experts, slot_count, model_width
-    )
-    grad_hidden = jnp.einsum(
-        "sjcd,jhd->sjch", grad_blocks, down_w, preferred_element_type=jnp.float32
-    )
-    grad_down_w = jnp.einsum(
-        "sjch,sjcd->jhd", hidden, grad_blocks, preferred_element_type=jnp.float32
-    )
-    grad_gate_in = (grad_hidden * up_act * sig_gate * (1.0 + gate_act * (1.0 - sig_gate))).astype(
-        jnp.bfloat16
-    )
-    grad_up_in = (grad_hidden * silu_gate).astype(jnp.bfloat16)
-    grad_gate_w = jnp.einsum(
-        "sjcd,sjch->jdh", owner_rows, grad_gate_in, preferred_element_type=jnp.float32
-    )
-    grad_up_w = jnp.einsum(
-        "sjcd,sjch->jdh", owner_rows, grad_up_in, preferred_element_type=jnp.float32
-    )
-
-    def back_term(start, length):
-        from_gate = jnp.einsum(
-            "sjch,jdh->sjcd", grad_gate_in, gate_w, preferred_element_type=jnp.float32
-        )
-        from_up = jnp.einsum("sjch,jdh->sjcd", grad_up_in, up_w, preferred_element_type=jnp.float32)
-        return from_gate + from_up
-
-    grad_slots = from_owner(
-        owner_sum(back_term, sources).astype(jnp.bfloat16).reshape(-1, slot_count, model_width)
-    )
-    back_rows = jnp.concatenate(
-        [grad_slots.reshape(experts * slot_count, model_width), zero_row], axis=0
-    )
-    grad_second = grad_second + jnp.sum(
-        back_rows[slot_place].reshape(tok_count, TOP, model_width).astype(jnp.float32), axis=1
-    )
     mlp_gain_grad = jnp.sum(grad_second * normed_two, axis=0)
     grad_normed_two = grad_second * mlp_gain
     grad_mid = grad_out + scale_two * (
@@ -323,18 +418,21 @@
         from_v = jnp.einsum(
             "ti,di->td", grad_value_rows, w_value, preferred_element_type=jnp.float32
         )
-        return from_q + from_k + from_v
-
-    grad_first = share_rows(input_term, tok_count)
+        return (from_q + from_k + from_v).astype(jnp.bfloat16)
+
+    grad_first = share_rows(input_term, tok_count).astype(jnp.float32)
     attn_gain_grad = jnp.sum(grad_first * normed_one, axis=0)
     grad_normed_one = grad_first * attn_gain
     grad_x = grad_mid + scale_one * (
         grad_normed_one - normed_one * jnp.mean(grad_normed_one * normed_one, axis=1, keepdims=True)
     )
-    mixer = lax.psum(
-        (query_grad, key_grad, value_grad, out_grad, q_gain_grad, k_gain_grad), "expert"
-    )
-    shared = lax.psum((attn_gain_grad, mlp_gain_grad, router_grad), ("fsdp", "expert"))
+    narrow = tuple(g.astype(jnp.bfloat16) for g in (query_grad, key_grad, value_grad, out_grad))
+    mixer = tuple(g.astype(jnp.float32) for g in lax.psum(narrow, "expert"))
+    mixer = mixer + lax.psum((q_gain_grad, k_gain_grad), "expert")
+    shared = lax.psum(
+        jnp.concatenate([attn_gain_grad[None], mlp_gain_grad[None], router_grad], axis=0),
+        ("fsdp", "expert"),
+    )
     return (
         block_output,
         grad_x[None],
@@ -346,7 +444,7 @@
         mixer[5],
         shared[0],
         shared[1],
-        shared[2],
+        shared[2:].T,
         grad_gate_w,
         grad_up_w,
         grad_down_w,

time: 5070 us -> 1300 us (0.26)
  blocking collectives: 3660 us -> 100 us
  waiting for transfers between devices: 998 us -> 895 us
  local copies, waits for them, and re-layouts: 107 us -> 21.5 us
    unnamed x1, blocking collectives: 3290 us -> 15.3 us
    reduce_scatter x0 -> x4, waiting for transfers between devices: none -> 332 us  [the longest x1 151 us: experts_dense(): back_rows = lax.psum_scatter(back, 'fsdp', scatter_dimension=0, tiled=True)]
    all_to_all x2 -> x0, blocking collectives: 289 us -> none  [to_owner(): lax.all_to_all(block_rows, 'expert', split_axis=0, concat_axis=0, tiled=T...]
    all_to_all x2 -> x1, waiting for transfers between devices: 246 us -> 5.46 us  [experts_dense(): lax.all_to_all(terms, 'expert', split_axis=0, concat_axis=0, tiled=True)]
    psum x2, waiting for transfers between devices: 396 us -> 292 us  [the longest x1 174 us: on_device(): mixer = tuple((g.astype(jnp.float32) for g in lax.psum(narrow, 'expert')))]
    all_gather x2, waiting for transfers between devices: 253 us -> 185 us  [the longest x1 95.5 us: experts_dense(): lax.all_gather(second_rows, ('fsdp', 'expert'), axis=0, tiled=True)]
    dot_general x13 -> x16, matrix products: 186 us -> 154 us  [the longest x5 49.6 us: by_expert(): return jnp.dot(left.T, right, preferred_element_type=jnp.float32)]
  transfers between devices with their start and end apart: 10 -> 13, of which waited for: 9 -> 12; matrix products, arithmetic and copies ran while one was open for 3% -> 12% of each run, Pallas kernels for 0% -> 0%
where the time goes in v1:
time: 1300 us; the launch traced here: 1290 us
  waiting for transfers between devices  895 us (69%)
  matrix products  188 us (14%)
  blocking collectives  100 us (8%)
  other arithmetic  57 us (4%)
  local copies, waits for them, and re-layouts  21.5 us (2%)
  between operations  15.3 us (1%)
  starting transfers between devices  13.8 us (1%)
    psum x1, waiting for transfers between devices, on_device(): mixer = tuple((g.astype(jnp.float32) for g in lax.psum(narrow, 'expert')))  174 us
    reduce_scatter x1, waiting for transfers between devices, experts_dense(): back_rows = lax.psum_scatter(back, 'fsdp', scatter_dimension=0, tiled=True)  151 us
    reduce_scatter x1, waiting for transfers between devices, experts_dense(): lax.psum_scatter(forward, 'fsdp', scatter_dimension=0, tiled=True)  125 us
    psum x1, waiting for transfers between devices, on_device(): lax.psum(jnp.concatenate([attn_gain_grad[None], mlp_gain_grad[None], rout...  118 us
    all_gather x1, waiting for transfers between devices, experts_dense(): lax.all_gather(second_rows, ('fsdp', 'expert'), axis=0, tiled=True)  95.5 us
    all_gather x1, waiting for transfers between devices, experts_dense(): grad_all = lax.all_gather(cotangent, ('fsdp', 'expert'), axis=0, tiled=True)  89.2 us
    reduce_scatter x1, waiting for transfers between devices, experts_dense(): lax.psum_scatter(back_rows, 'expert', scatter_dimension=0, tiled=True)  52 us
    dot_general x5, matrix products, by_expert(): return jnp.dot(left.T, right, preferred_element_type=jnp.float32)  49.6 us
  transfers between devices with their start and end apart: 13, of which 12 were waited for; matrix products, arithmetic and copies ran while one was open for 12% of the time, Pallas kernels for 0%

profile of v1, /device:TPU:0, one launch (start us, length us, event | category | flops | bytes accessed | tf_op | source)
XLA Modules:
  0.0 1290.1 jit_solution(8901709786228698419)
XLA Ops:
  11.2 9.5 all-gather
  23.0 26.2 %all-gather.7.cloned.1.call-done = bf16[512,2048]{1,0:T(8,128)(2,1)} async-done(((bf16[128,2048]{1,0:T(8,128)(2,1)}), bf16[512,2048]{1,0:T(8,128)(2,1)}) %all-gather.7.cloned.1.call-update) | async-done | bytes 2097168 | tf_op jit(solution)/shard_map/all_gather | solution.py:298
  49.2 3.7 multiply_reduce_fusion.6
  55.2 9.0 all-reduce.3
  74.1 2.6 convolution_convert_fusion.5
  76.8 35.3 %reduce-scatter.7.cloned.1.call-done = bf16[128,2048]{1,0:T(8,128)(2,1)} async-done(((bf16[512,2048]{1,0:T(8,128)(2,1)}), bf16[128,2048]{1,0:T(8,128)(2,1)}) %reduce-scatter.7.cloned.1.call-update) | async-done | bytes 524304 | tf_op jit(solution)/shard_map/reduce_scatter | solution.py:52
  115.5 10.0 all-gather.13.cloned.1.call-start
  125.6 4.0 copy.80
  129.6 3.9 copy.81
  134.4 95.5 %all-gather.9.cloned.1.call-done = bf16[4096,2048]{1,0:T(8,128)(2,1)} async-done(((bf16[128,2048]{1,0:T(8,128)(2,1)}), bf16[4096,2048]{1,0:T(8,128)(2,1)}) %all-gather.9.cloned.1.call-update) | async-done | bytes 16777232 | tf_op jit(solution)/shard_map/all_gather | solution.py:219
  230.0 15.2 %fusion.52 = f32[4096,512]{0,1:T(8,128)} fusion(bf16[4096,2048]{1,0:T(8,128)(2,1)} %all-gather.9.cloned.1.call-done, bf16[2048,512]{0,1:T(8,128)(2,1)} %bitcast.174), kind=kOutput, calls=%fused_computation.145 | convolution fusion | flops 8589934592 | bytes 27262976 | tf_op jit(solution)/shard_map/dot_general | solution.py:231
  245.1 11.1 fusion.51
  256.2 89.2 %all-gather.13.cloned.1.call-done = bf16[1,4096,2048]{2,1,0:T(8,128)(2,1)} async-done(((bf16[1,128,2048]{2,1,0:T(8,128)(2,1)}), bf16[1,4096,2048]{2,1,0:T(8,128)(2,1)}) %all-gather.13.cloned.1.call-update) | async-done | bytes 16777232 | tf_op jit(solution)/shard_map/all_gather | solution.py:218
  345.5 20.2 %bitcast_reduce_fusion = (f32[4096,2]{0,1:T(2,128)S(1)}, f32[4096,512]{0,1:T(8,128)}) fusion(f32[4096,512]{0,1:T(8,128)} %fusion.52, f32[4096,512]{0,1:T(8,128)} %fusion.51, bf16[512,2048]{1,0:T(8,128)(2,1)S(1)} %bitcast.169, bf16[1,4096,2048]{2,1,0:T(8,128)(2,1)} %all-gather.13.cloned.1.call-done), kind=kOutput, calls=%fused_computation.9 | convolution fusion | flops 8604606464 | bytes 44072960 | tf_op jit(solution)/shard_map/td,hd->th/dot_general | solution.py:229
  365.7 15.3 %all-reduce = f32[4,1024,2]{1,2,0:T(2,128)S(1)} all-reduce(f32[4,1024,2]{1,2,0:T(2,128)S(1)} %bitcast.190), channel_id=7, replica_groups=mesh['fsdp'=4,'expert'=8] {'fsdp'}, use_global_device_ids=true, to_apply=%region_16.17.clone | all-reduce | flops 8192 | bytes 65536
  382.3 3.3 all-to-all-start
  385.7 5.5 all-to-all-done
  391.3 38.7 %all_gather.21 = f32[4096,16]{0,1:T(8,128)S(1)} all-gather(f32[128,16]{0,1:T(8,128)S(1)} %get-tuple-element.58), channel_id=1, replica_groups=mesh['fsdp'=4,'expert'=8] {'fsdp','expert'}, dimensions={0}, use_global_device_ids=true | all-gather | bytes 270336 | tf_op jit(solution)/shard_map/all_gather | solution.py:220
  430.1 13.7 %multiply_convert_fusion = (bf16[4096,512]{0,1:T(8,128)(2,1)}, bf16[4096,512]{0,1:T(8,128)(2,1)S(1)}, bf16[4096,512]{0,1:T(8,128)(2,1)}) fusion(f32[4096,512]{0,1:T(8,128)} %get-tuple-element.66, f32[4096,2]{0,1:T(2,128)S(1)} %constant_dynamic-slice_fusion, f32[4096,512]{0,1:T(8,128)} %fusion.51, f32[4096,512]{0,1:T(8,128)} %fusion.52), kind=kLoop, calls=%fused_computation.10 | loop fusion | flops 35651584 | bytes 37781504 | tf_op jit(solution)/shard_map/convert_element_type | solution.py:241
  443.8 15.3 %fusion.53 = f32[4096,2048]{1,0:T(8,128)} fusion(bf16[4096,512]{0,1:T(8,128)(2,1)S(1)} %get-tuple-element.33, bf16[2048,512]{0,1:T(8,128)(2,1)S(1)} %bitcast.177), kind=kOutput, calls=%fused_computation.146 | convolution fusion | flops 8589934592 | bytes 39845888 | tf_op jit(solution)/shard_map/th,dh->td/dot_general | solution.py:243
  459.2 22.7 %add_convert_fusion = bf16[4096,2048]{1,0:T(8,128)(2,1)} fusion(f32[4096,2048]{1,0:T(8,128)} %fusion.53, bf16[4096,512]{0,1:T(8,128)(2,1)} %get-tuple-element.32, bf16[2048,512]{0,1:T(8,128)(2,1)} %bitcast.175), kind=kOutput, calls=%fused_computation | convolution fusion | flops 8606711808 | bytes 56623104 | tf_op jit(solution)/shard_map/th,dh->td/dot_general | solution.py:244
  482.0 151.0 %reduce-scatter.13.cloned.1.call-done = bf16[1024,2048]{1,0:T(8,128)(2,1)} async-done(((bf16[4096,2048]{1,0:T(8,128)(2,1)}), bf16[1024,2048]{1,0:T(8,128)(2,1)}) %reduce-scatter.13.cloned.1.call-update) | async-done | bytes 4194320 | tf_op jit(solution)/shard_map/reduce_scatter | solution.py:246
  633.0 52.0 %reduce-scatter.15.cloned.1.call-done = bf16[128,2048]{1,0:T(8,128)(2,1)} async-done(((bf16[1024,2048]{1,0:T(8,128)(2,1)}), bf16[128,2048]{1,0:T(8,128)(2,1)}) %reduce-scatter.15.cloned.1.call-update) | async-done | bytes 524304 | tf_op jit(solution)/shard_map/reduce_scatter | solution.py:247
  690.5 14.8 %convolution_convert_fusion = bf16[4096,2048]{1,0:T(8,128)(2,1)} fusion(bf16[4096,512]{0,1:T(8,128)(2,1)} %get-tuple-element.34, bf16[512,2048]{1,0:T(8,128)(2,1)S(1)} %bitcast.168), kind=kOutput, calls=%fused_computation.5 | convolution fusion | flops 8598323200 | bytes 23068672 | tf_op jit(solution)/shard_map/dot_general | solution.py:253
  705.4 18.8 %all-gather.11.cloned.1.call-done = bf16[512,2048]{1,0:T(8,128)(2,1)} async-done(((bf16[128,2048]{1,0:T(8,128)(2,1)}), bf16[512,2048]{1,0:T(8,128)(2,1)}) %all-gather.11.cloned.1.call-update) | async-done | bytes 2097168 | tf_op jit(solution)/shard_map/all_gather | solution.py:360
  724.3 3.7 convolution_convert_fusion.6
  734.4 9.4 all-reduce.2
  753.2 2.7 add_convert_fusion.1
  756.0 125.4 %reduce-scatter.9.cloned.1.call-done = bf16[1024,2048]{1,0:T(8,128)(2,1)} async-done(((bf16[4096,2048]{1,0:T(8,128)(2,1)}), bf16[1024,2048]{1,0:T(8,128)(2,1)}) %reduce-scatter.9.cloned.1.call-update) | async-done | bytes 4194320 | tf_op jit(solution)/shard_map/reduce_scatter | solution.py:254
  881.8 9.4 convolution_bitcast_fusion
  891.2 8.3 convolution_bitcast_fusion.1
  899.5 2.4 pad_maximum_fusion.1
  903.3 8.3 convolution_bitcast_fusion.2
  911.6 8.4 convolution_bitcast_fusion.3
  922.9 2.6 convolution_convert_fusion.1
  925.5 2.6 convolution_convert_fusion.2
  928.2 2.6 convolution_convert_fusion.3
  930.8 2.6 convolution_convert_fusion.4
  933.6 15.2 %fusion = f32[512,2048]{1,0:T(8,128)} fusion(bf16[4096,512]{0,1:T(8,128)(2,1)} %get-tuple-element.34, bf16[1,4096,2048]{2,1,0:T(8,128)(2,1)} %all-gather.13.cloned.1.call-done), kind=kOutput, calls=%fused_computation.1 | convolution fusion | flops 8589934592 | bytes 25165824 | tf_op jit(solution)/shard_map/dot_general | solution.py:263
  948.7 18.1 %all-reduce.1 = (f32[512]{0:T(512)}, f32[512]{0:T(512)}) all-reduce(f32[512]{0:T(512)S(1)} %get-tuple-element.18, f32[512]{0:T(512)S(1)} %get-tuple-element.16), channel_id=1, replica_groups=mesh['fsdp'=4,'expert'=8] {'expert'}, use_global_device_ids=true, to_apply=%region_33.34 | all-reduce | flops 1024 | bytes 8192 | tf_op jit(solution)/shard_map/psum | solution.py:431
  969.1 3.4 reduce-scatter.11.cloned.1.call-done
  972.5 3.1 fusion.20
  975.6 174.2 %all-reduce.10.cloned.1.call-done = (bf16[2048,512]{1,0:T(8,128)(2,1)}, bf16[2048,512]{1,0:T(8,128)(2,1)}, bf16[2048,512]{1,0:T(8,128)(2,1)}, bf16[512,2048]{1,0:T(8,128)(2,1)}) async-done(((bf16[2048,512]{1,0:T(8,128)(2,1)}, bf16[2048,512]{1,0:T(8,128)(2,1)}, bf16[2048,512]{1,0:T(8,128)(2,1)}, bf16[512,2048]{1,0:T(8,128)(2,1)}), (bf16[2048,512]{1,0:T(8,128)(2,1)}, bf16[2048,512]{1,0:T(8,128)(2,1)}, ...) | async-done | bytes 8388624 | tf_op jit(solution)/shard_map/psum | solution.py:430
  1149.8 4.3 convert_element_type.183
  1154.2 2.6 convert_element_type.185
  1156.8 2.7 convert_element_type.187
  1159.5 2.5 convert_element_type.189
  1162.0 117.9 %all-reduce.8.cloned.1.call-done = f32[18,2048]{1,0:T(8,128)} async-done(((f32[18,2048]{1,0:T(8,128)}), f32[18,2048]{1,0:T(8,128)}) %all-reduce.8.cloned.1.call-update) | async-done | bytes 147472 | tf_op jit(solution)/shard_map/psum | solution.py:432
  (214 shorter events, 55.2 us)
Async XLA Ops:
  7.2 338.3 %copy-start = (bf16[2,256,2048]{2,1,0:T(8,128)(2,1)S(1)}, bf16[2,256,2048]{2,1,0:T(8,128)(2,1)}, u32[]{:S(2)}) copy-start(bf16[2,256,2048]{2,1,0:T(8,128)(2,1)} %param.30) | copy-start | bytes 6291460
  7.2 42.0 %all-gather.7.cloned.1.call-start = ((), (), s32[]{:S(2)}) async-start(), calls=%async_computation.7 | async-start | bytes 2621440 | tf_op jit(solution)/shard_map/all_gather | solution.py:298
  11.2 100.9 %reduce-scatter.7.cloned.1.call-start = ((), (), s32[]{:S(2)}) async-start(), calls=%async_computation.8 | async-start | bytes 2621440 | tf_op jit(solution)/shard_map/reduce_scatter | solution.py:52
  49.2 3.7 copy-start.31
  49.2 3.7 copy-start.58
  52.9 13.9 %copy-start.6 = (f32[512,512]{0,1:T(8,128)}, f32[512,512]{0,1:T(8,128)S(1)}, u32[]{:S(2)}) copy-start(f32[512,512]{0,1:T(8,128)S(1)} %get-tuple-element.62) | copy-start | bytes 3145732
  53.0 11.3 copy-start.49
  55.2 10.7 copy-start.51
  66.9 4.1 copy-start.59
  67.9 4.4 copy-start.2
  73.7 39.7 %copy-start.63 = (bf16[4,128,512]{2,1,0:T(8,128)(2,1)}, bf16[4,128,512]{2,1,0:T(8,128)(2,1)S(1)}, u32[]{:S(2)}) copy-start(bf16[4,128,512]{2,1,0:T(8,128)(2,1)S(1)} %convolution_convert_fusion.9) | copy-start | bytes 1572868
  73.7 38.4 %copy-start.5 = (bf16[1,128,2048]{2,1,0:T(8,128)(2,1)S(1)}, bf16[1,128,2048]{2,1,0:T(8,128)(2,1)}, u32[]{:S(2)}) copy-start(bf16[1,128,2048]{2,1,0:T(8,128)(2,1)} %param.17) | copy-start | bytes 1572868
  74.1 39.3 %copy-start.43 = (f32[2048]{0:T(1024)S(1)}, f32[2048]{0:T(1024)}, u32[]{:S(2)}) copy-start(f32[2048]{0:T(1024)} %param.26) | copy-start | bytes 24580
  76.7 48.8 %copy-start.62 = (s32[16]{0:T(128)S(1)}, s32[16]{0:T(128)}, u32[]{:S(2)}) copy-start(s32[16]{0:T(128)} %param.33) | copy-start | bytes 196
  76.7 153.3 %all-gather.9.cloned.1.call-start = ((), (), s32[]{:S(2)}) async-start(), calls=%async_computation.9 | async-start | bytes 17301504 | tf_op jit(solution)/shard_map/all_gather | solution.py:219
  115.5 230.0 %all-gather.13.cloned.1.call-start = ((), (), s32[]{:S(2)}) async-start(), calls=%async_computation.17 | async-start | bytes 17301504 | tf_op jit(solution)/shard_map/all_gather | solution.py:218
  125.5 8.0 copy-start.65
  125.6 8.6 copy-start.55
  125.6 8.6 copy-start.10
  125.6 8.6 copy-start.44
  230.0 15.2 %copy-start.29 = (bf16[2,2048,256]{1,2,0:T(8,128)(2,1)S(1)}, bf16[2,2048,256]{1,2,0:T(8,128)(2,1)}, u32[]{:S(2)}) copy-start(bf16[2,2048,256]{1,2,0:T(8,128)(2,1)} %copy.80) | copy-start | bytes 6291460
  230.0 15.2 %copy-start.56 = (bf16[4096,2048]{1,0:T(8,128)(2,1)S(1)}, bf16[4096,2048]{1,0:T(8,128)(2,1)}, u32[]{:S(2)}) copy-start(bf16[4096,2048]{1,0:T(8,128)(2,1)} %all-gather.9.cloned.1.call-done) | copy-start | bytes 50331652
  382.3 8.9 all-to-all-start
  385.6 247.3 %reduce-scatter.13.cloned.1.call-start = ((), (), s32[]{:S(2)}) async-start(), calls=%async_computation.12 | async-start | bytes 20971520 | tf_op jit(solution)/shard_map/reduce_scatter | solution.py:246
  430.0 13.8 %copy-start.30 = (bf16[2,2048,256]{1,2,0:T(8,128)(2,1)S(1)}, bf16[2,2048,256]{1,2,0:T(8,128)(2,1)}, u32[]{:S(2)}) copy-start(bf16[2,2048,256]{1,2,0:T(8,128)(2,1)} %copy.80) | copy-start | bytes 6291460
  443.8 15.4 %copy-start.19 = (bf16[4096,512]{0,1:T(8,128)(2,1)}, bf16[4096,512]{0,1:T(8,128)(2,1)S(1)}, u32[]{:S(2)}) copy-start(bf16[4096,512]{0,1:T(8,128)(2,1)S(1)} %get-tuple-element.33) | copy-start | bytes 12582916
  481.9 203.1 %copy-start.9 = (bf16[128,2048]{1,0:T(8,128)(2,1)S(1)}, bf16[128,2048]{1,0:T(8,128)(2,1)}, u32[]{:S(2)}) copy-start(bf16[128,2048]{1,0:T(8,128)(2,1)} %reduce-scatter.7.cloned.1.call-done) | copy-start | bytes 1572868
  481.9 203.1 %reduce-scatter.15.cloned.1.call-start = ((), (), s32[]{:S(2)}) async-start(), calls=%async_computation.13 | async-start | bytes 4718592 | tf_op jit(solution)/shard_map/reduce_scatter | solution.py:247
  632.9 91.3 %all-gather.11.cloned.1.call-start = ((), (), s32[]{:S(2)}) async-start(), calls=%async_computation.14 | async-start | bytes 2621440 | tf_op jit(solution)/shard_map/all_gather | solution.py:360
  690.5 190.9 %reduce-scatter.9.cloned.1.call-start = ((), (), s32[]{:S(2)}) async-start(), calls=%async_computation.10 | async-start | bytes 20971520 | tf_op jit(solution)/shard_map/reduce_scatter | solution.py:254
  705.4 22.6 %copy-start.39 = (bf16[512,512]{0,1:T(8,128)(2,1)S(1)}, bf16[512,512]{0,1:T(8,128)(2,1)}, u32[]{:S(2)}) copy-start(bf16[512,512]{0,1:T(8,128)(2,1)} %copy-done.38) | copy-start | bytes 1572868
  705.4 261.5 %reduce-scatter.17.cloned.1.call-start = ((), (), s32[]{:S(2)}) async-start(), calls=%async_computation.15 | async-start | bytes 2621440 | tf_op jit(solution)/shard_map/reduce_scatter | solution.py:52
  724.3 3.7 copy-start.3
  743.8 3.6 copy-start.32
  755.9 125.5 %copy-start.11 = (bf16[128,2048]{1,0:T(8,128)(2,1)S(1)}, bf16[128,2048]{1,0:T(8,128)(2,1)}, u32[]{:S(2)}) copy-start(bf16[128,2048]{1,0:T(8,128)(2,1)} %multiply_convert_fusion.5) | copy-start | bytes 1572868
  755.9 216.6 %reduce-scatter.11.cloned.1.call-start = ((), (), s32[]{:S(2)}) async-start(), calls=%async_computation.11 | async-start | bytes 4718592 | tf_op jit(solution)/shard_map/reduce_scatter | solution.py:255
  881.4 268.4 %all-reduce.10.cloned.1.call-start = ((), (), s32[]{:S(2)}) async-start(), calls=%async_computation.18 | async-start | bytes 16777216 | tf_op jit(solution)/shard_map/psum | solution.py:430
  881.8 9.4 copy-start.21
  899.5 3.8 copy-start.20
  920.0 2.9 copy-start.64
  933.5 33.4 %copy-start.42 = (f32[2048]{0:T(1024)S(1)}, f32[2048]{0:T(1024)}, u32[]{:S(2)}) copy-start(f32[2048]{0:T(1024)} %param.25) | copy-start | bytes 24580
  933.5 33.4 %copy-start.54 = (f32[128]{0:T(128)S(1)}, f32[128]{0:T(128)}, u32[]{:S(2)}) copy-start(f32[128]{0:T(128)} %copy-done.53) | copy-start | bytes 1540
  933.5 39.0 %copy-start.12 = (bf16[1,128,2048]{2,1,0:T(8,128)(2,1)S(1)}, bf16[1,128,2048]{2,1,0:T(8,128)(2,1)}, u32[]{:S(2)}) copy-start(bf16[1,128,2048]{2,1,0:T(8,128)(2,1)} %param.18) | copy-start | bytes 1572868
  933.5 39.0 %copy-start.18 = (f32[128,2048]{1,0:T(8,128)S(1)}, f32[128,2048]{1,0:T(8,128)}, u32[]{:S(2)}) copy-start(f32[128,2048]{1,0:T(8,128)} %copy-done.17) | copy-start | bytes 3145732
  933.5 346.4 %all-reduce.8.cloned.1.call-start = ((), (), s32[]{:S(2)}) async-start(), calls=%async_computation.16 | async-start | bytes 393216 | tf_op jit(solution)/shard_map/psum | solution.py:432
  1149.8 4.4 copy-start.28
  1156.8 2.7 copy-start.26
  1156.8 126.3 %copy-start.1 = (bf16[2,256,2048]{2,1,0:T(8,128)(2,1)S(1)}, bf16[2,256,2048]{2,1,0:T(8,128)(2,1)}, u32[]{:S(2)}) copy-start(bf16[2,256,2048]{2,1,0:T(8,128)(2,1)} %param.30) | copy-start | bytes 6291460
  (31 other events, 54.0 us)
Sparse Core Ops, SparseCore 0:
  11.3 37.8 all-gather.6
  76.8 35.1 reduce-scatter.6
  115.6 114.3 all-gather.8
  232.8 112.5 all-gather.12
  482.0 150.8 reduce-scatter.12
  635.1 49.9 reduce-scatter.14
  690.6 33.6 all-gather.10
  727.3 153.9 reduce-scatter.8
  884.9 35.1 reduce-scatter.16
  922.3 50.1 reduce-scatter.10
  975.7 174.0 all-reduce.9
  1155.2 124.7 all-reduce.7

commit v2 on v1

--- a/solution.py
+++ b/solution.py
@@ -1,6 +1,10 @@
+import functools
+
 import jax
 import jax.numpy as jnp
 from jax import lax
+from jax.experimental import pallas as pl
+from jax.experimental.pallas import tpu as pltpu
 from jax.sharding import PartitionSpec as P
 
 HEAD_DIM = 128
@@ -10,6 +14,874 @@
 epsilon = 1e-05
 rope_base = 10000.0
 precise = lax.Precision.HIGHEST
+
+
+MESH = pl.DeviceIdType.MESH
+DMA = pltpu.SemaphoreType.DMA
+
+
+class Place:
+    def __init__(self):
+        self.f, self.e = lax.axis_index("fsdp"), lax.axis_index("expert")
+        self.c, self.z = self.e % 2, self.e // 2
+        self.fx = self.f + 1 - 2 * (self.f % 2)
+        self.fy = (self.f + 2) % 4
+        self.fd = 3 - self.f
+        self.pe = self.e + 1 - 2 * self.c
+
+
+def send(src, dst, send_sem, recv_sem, f, e):
+    return pltpu.make_async_remote_copy(
+        src_ref=src,
+        dst_ref=dst,
+        send_sem=send_sem,
+        recv_sem=recv_sem,
+        device_id={"fsdp": f, "expert": e},
+        device_id_type=MESH,
+    )
+
+
+def greet(peers, line=None):
+    barrier = pltpu.get_barrier_semaphore()
+
+    def hello(f, e):
+        pl.semaphore_signal(
+            barrier, inc=1, device_id={"fsdp": f, "expert": e}, device_id_type=MESH
+        )
+
+    for f, e in peers:
+        hello(f, e)
+    if line is not None:
+        at, nz = line
+        for step in range(1, nz):
+            hello(at.f, 2 * ((at.z + step) % nz) + at.c)
+        pl.semaphore_wait(barrier, len(peers) + nz - 1)
+    else:
+        pl.semaphore_wait(barrier, len(peers))
+
+
+class SmallGather:
+    sems = staticmethod(
+        lambda nz: [DMA((nz,)), DMA((nz,)), DMA((4,)), DMA((4,))]
+    )
+
+    def __init__(self, at, nz, own, out, sems):
+        self.at, self.nz, self.own, self.out = at, nz, own, out
+        self.ls, self.lr, self.ss, self.sr = sems
+
+    def line(self, step):
+        at = self.at
+        z = (at.z + step) % self.nz
+        back = (at.z + self.nz - step) % self.nz
+        slot = self.out.at[at.c, at.f]
+        to = send(self.own, slot.at[at.z], self.ls.at[step], self.lr.at[step], at.f, 2 * z + at.c)
+        come = send(self.own, slot.at[back], self.ls.at[step], self.lr.at[step], at.f, 2 * z + at.c)
+        return to, come
+
+    def plane(self, i):
+        at, out = self.at, self.out
+        f, to_f = ((at.f, at.fx), (at.f, at.fy), (at.fx, at.fy))[i]
+        slot = out.at[at.c, f]
+        return send(slot, slot, self.ss.at[i], self.sr.at[i], to_f, at.e)
+
+    def pair(self):
+        at = self.at
+        slot = self.out.at[at.c]
+        return send(slot, slot, self.ss.at[3], self.sr.at[3], at.f, at.pe)
+
+    def stage(self, i):
+        at = self.at
+        if i == 0:
+            for step in range(1, self.nz):
+                self.line(step)[0].start()
+            self.out[at.c, at.f, at.z] = self.own[...]
+        elif i == 1:
+            for step in range(1, self.nz):
+                self.line(step)[1].wait_recv()
+            self.plane(0).start()
+            self.plane(1).start()
+        elif i == 2:
+            self.plane(0).wait_recv()
+            self.plane(2).start()
+        elif i == 3:
+            self.plane(1).wait_recv()
+            self.plane(2).wait_recv()
+            self.pair().start()
+        elif i == 4:
+            self.pair().wait_recv()
+            self.pair().wait_send()
+            for step in range(1, self.nz):
+                self.line(step)[0].wait_send()
+            for k in range(3):
+                self.plane(k).wait_send()
+
+
+class SmallScatter:
+    sems = staticmethod(lambda nz: [DMA((nz,)), DMA((nz,)), DMA((4,)), DMA((4,))])
+    scratch = staticmethod(
+        lambda nz, shape: [
+            pltpu.VMEM((4, nz, *shape), jnp.float32),
+            pltpu.VMEM((4, nz, *shape), jnp.float32),
+            pltpu.VMEM((3, nz, *shape), jnp.float32),
+            pltpu.VMEM((nz, *shape), jnp.float32),
+        ]
+    )
+
+    def __init__(self, at, nz, part, out, scratch, sems):
+        self.at, self.nz, self.part, self.out = at, nz, part, out
+        self.acc, self.pb, self.xy, self.zb = scratch
+        self.ls, self.lr, self.ss, self.sr = sems
+
+    def pair(self):
+        at = self.at
+        return send(
+            self.part.at[1 - at.c], self.pb, self.ss.at[0], self.sr.at[0], at.f, at.pe
+        )
+
+    def plane(self, i):
+        at = self.at
+        f, to_f = ((at.fx, at.fx), (at.fd, at.fx), (at.fy, at.fy))[i]
+        return send(
+            self.acc.at[f], self.xy.at[i], self.ss.at[1 + i], self.sr.at[1 + i], to_f, at.e
+        )
+
+    def line(self, step):
+        at = self.at
+        z = (at.z + step) % self.nz
+        return send(
+            self.acc.at[at.f, z], self.zb.at[step], self.ls.at[step], self.lr.at[step], at.f, 2 * z + at.c
+        )
+
+    def stage(self, i):
+        at, acc, xy = self.at, self.acc, self.xy
+        if i == 0:
+            self.pair().start()
+        elif i == 1:
+            self.pair().wait_recv()
+            acc[...] = self.part[at.c] + self.pb[...]
+            self.plane(0).start()
+            self.plane(1).start()
+        elif i == 2:
+            self.plane(0).wait_recv()
+            self.plane(1).wait_recv()
+            acc[at.fy] = acc[at.fy] + xy[1]
+            self.plane(2).start()
+            acc[at.f] = acc[at.f] + xy[0]
+        elif i == 3:
+            self.plane(2).wait_recv()
+            acc[at.f] = acc[at.f] + xy[2]
+            for step in range(1, self.nz):
+                self.line(step).start()
+        elif i == 4:
+            total = acc[at.f, at.z]
+            for step in range(1, self.nz):
+                self.line(step).wait_recv()
+                total = total + self.zb[step]
+            self.out[...] = total
+            self.pair().wait_send()
+            for k in range(3):
+                self.plane(k).wait_send()
+            for step in range(1, self.nz):
+                self.line(step).wait_send()
+
+
+def take(sequence, count):
+    return [next(sequence) for _ in range(count)]
+
+
+def gather_kernel(nz, own, own_small, out, out_small, own_sem, zr, zs, xr, xs, yr, ys, dr, xf, yf, pr, ps, *small_sems):
+    at = Place()
+    half = own.shape[0] // 2
+    halves = (pl.ds(0, half), pl.ds(half, half))
+    small = SmallGather(at, nz, own_small, out_small, small_sems)
+    greet([(at.fx, at.e), (at.fy, at.e), (at.f, at.pe)], (at, nz))
+    keep = pltpu.make_async_copy(own, out.at[at.f, at.e], own_sem)
+    keep.start()
+    small.stage(0)
+
+    def up(z, slot):
+        return send(slot, slot, zs.at[0, z], zr.at[z], at.f, at.e + 2)
+
+    def down(z, slot):
+        return send(slot, slot, zs.at[1, z], zr.at[z], at.f, at.e - 2)
+
+    def to_x(z, h):
+        ref = out.at[at.f, 2 * z + at.c, halves[h]]
+        return send(ref, ref, xs.at[h, z], xr.at[h, z], at.fx, at.e)
+
+    def to_y(z, h):
+        ref = out.at[at.f, 2 * z + at.c, halves[h]]
+        return send(ref, ref, ys.at[h, z], yr.at[h, z], at.fy, at.e)
+
+    def x_on(z):
+        ref = out.at[at.fx, 2 * z + at.c, halves[0]]
+        return send(ref, ref, yf.at[z], dr.at[0, z], at.fy, at.e)
+
+    def y_on(z):
+        ref = out.at[at.fy, 2 * z + at.c, halves[1]]
+        return send(ref, ref, xf.at[z], dr.at[1, z], at.fx, at.e)
+
+    def to_p(f, z, h):
+        ref = out.at[f, 2 * z + at.c, halves[h]]
+        return send(ref, ref, ps.at[f, z, h], pr.at[f, z, h], at.f, at.pe)
+
+    def order(i):
+        return at.z + (i + 1) // 2 * (1 - 2 * (i % 2))
+
+    def on_line(i, run):
+        z = order(i)
+        pl.when((z >= 0) & (z < nz))(lambda: run(z))
+
+    def line_step(z):
+        slot = out.at[at.f, 2 * z + at.c]
+
+        @pl.when(z != at.z)
+        def _():
+            up(z, slot).wait_recv()
+
+        @pl.when((z <= at.z) & (at.z < nz - 1))
+        def _():
+            up(z, slot).start()
+
+        @pl.when((z >= at.z) & (at.z > 0))
+        def _():
+            down(z, slot).start()
+
+        to_x(z, 0).start()
+        to_y(z, 1).start()
+        to_x(z, 1).start()
+        to_y(z, 0).start()
+        for h in range(2):
+            to_p(at.f, z, h).start()
+
+    def plane_step(z):
+        to_x(z, 0).wait_recv()
+        x_on(z).start()
+        to_y(z, 1).wait_recv()
+        y_on(z).start()
+        to_p(at.fx, z, 0).start()
+        to_p(at.fy, z, 1).start()
+        to_x(z, 1).wait_recv()
+        to_p(at.fx, z, 1).start()
+        to_y(z, 0).wait_recv()
+        to_p(at.fy, z, 0).start()
+
+    def diag_step(z):
+        x_on(z).wait_recv()
+        to_p(at.fd, z, 0).start()
+        y_on(z).wait_recv()
+        to_p(at.fd, z, 1).start()
+
+    keep.wait()
+    steps = 2 * nz - 1
+
+    def body(i, carry):
+        pl.when(i < steps)(lambda: on_line(i, line_step))
+        pl.when((i >= 1) & (i < steps + 1))(lambda: on_line(i - 1, plane_step))
+        pl.when(i >= 2)(lambda: on_line(i - 2, diag_step))
+        for k in range(1, 5):
+            pl.when(i == k)(functools.partial(small.stage, k))
+        return carry
+
+    lax.fori_loop(0, steps + 2, body, 0)
+
+    def finish(z, carry):
+        slot = out.at[at.f, 2 * z + at.c]
+
+        @pl.when((z <= at.z) & (at.z < nz - 1))
+        def _():
+            up(z, slot).wait_send()
+
+        @pl.when((z >= at.z) & (at.z > 0))
+        def _():
+            down(z, slot).wait_send()
+
+        for h in range(2):
+            to_x(z, h).wait_send()
+            to_y(z, h).wait_send()
+        x_on(z).wait_send()
+        y_on(z).wait_send()
+        for f in range(4):
+            for h in range(2):
+                to_p(f, z, h).wait_send()
+                to_p(f, z, h).wait_recv()
+        return carry
+
+    lax.fori_loop(0, nz, finish, 0)
+
+
+def gather_all(rows, small, nz, cid):
+    r, c = rows.shape
+    return pl.pallas_call(
+        functools.partial(gather_kernel, nz),
+        out_shape=(
+            jax.ShapeDtypeStruct((4, 2 * nz, r, c), rows.dtype),
+            jax.ShapeDtypeStruct((2, 4, nz, *small.shape), jnp.float32),
+        ),
+        in_specs=[pl.BlockSpec(memory_space=pltpu.VMEM)] * 2,
+        out_specs=(pl.BlockSpec(memory_space=pl.ANY), pl.BlockSpec(memory_space=pltpu.VMEM)),
+        scratch_shapes=[
+            DMA(()), DMA((nz,)), DMA((2, nz)), DMA((2, nz)), DMA((2, nz)), DMA((2, nz)), DMA((2, nz)),
+            DMA((2, nz)), DMA((nz,)), DMA((nz,)), DMA((4, nz, 2)), DMA((4, nz, 2)),
+            *SmallGather.sems(nz),
+        ],
+        compiler_params=pltpu.CompilerParams(collective_id=cid, has_side_effects=True),
+        cost_estimate=pl.CostEstimate(flops=0, bytes_accessed=240 << 20, transcendentals=0),
+        name="gather_all",
+    )(rows, small)
+
+
+def add_rows(dst, dst_rows, parts):
+    start, count = dst_rows
+
+    def body(i, carry):
+        r = pl.multiple_of(i * 16, 16)
+        total = None
+        for ref, offset in parts:
+            piece = ref[pl.ds(offset + r, 16), :].astype(jnp.float32)
+            total = piece if total is None else total + piece
+        dst[pl.ds(start + r, 16), :] = total.astype(dst.dtype)
+        return carry
+
+    lax.fori_loop(0, count // 16, body, 0)
+
+
+def scatter_kernel(nz, part, part_small, out, out_small, acc, pb, xh, yh, xf, yf, zu, zd, ls, pr, ps, xhs, xhr, yhs, yhr, xs, xr, ys, yr, us, ur, ds_, dr, *small_refs):
+    at = Place()
+    rows = out.shape[0]
+    half = rows // 2
+    lo, hi = pl.ds(0, half), pl.ds(half, half)
+    small = SmallScatter(at, nz, part_small, out_small, small_refs[:4], small_refs[4:])
+    greet([(at.fx, at.e), (at.fy, at.e), (at.f, at.pe)], (at, nz))
+    steps = 2 * nz - 1
+    small.stage(0)
+
+    def order(i):
+        return at.z + (nz - 1 - i // 2) * (2 * (i % 2) - 1)
+
+    def on_line(i, run):
+        z = order(i)
+        pl.when((z >= 0) & (z < nz))(lambda: run(z))
+
+    def load(f, z):
+        return pltpu.make_async_copy(part.at[f, 2 * z + at.c], acc.at[f, z], ls.at[f, z])
+
+    def to_p(f, z):
+        return send(part.at[f, 2 * z + 1 - at.c], pb.at[f, z], ps.at[f, z], pr.at[f, z], at.f, at.pe)
+
+    def start_step(z):
+        for f in (at.fd, at.fx, at.fy, at.f):
+            load(f, z).start()
+            to_p(f, z).start()
+
+    def start(i, carry):
+        on_line(i, start_step)
+        return carry
+
+    lax.fori_loop(0, steps, start, 0)
+
+    def half_x(z):
+        return send(acc.at[at.fd, z, lo], xh.at[z], xhs.at[z], xhr.at[z], at.fx, at.e)
+
+    def half_y(z):
+        return send(acc.at[at.fd, z, hi], yh.at[z], yhs.at[z], yhr.at[z], at.fy, at.e)
+
+    def full_x(z):
+        return send(acc.at[at.fx, z], xf.at[z], xs.at[z], xr.at[z], at.fx, at.e)
+
+    def full_y(z):
+        return send(acc.at[at.fy, z], yf.at[z], ys.at[z], yr.at[z], at.fy, at.e)
+
+    def go_up(z):
+        return send(acc.at[at.f, z], zu.at[z], us.at[z], ur.at[z], at.f, at.e + 2)
+
+    def go_down(z):
+        return send(acc.at[at.f, z], zd.at[z], ds_.at[z], dr.at[z], at.f, at.e - 2)
+
+    def diag_step(z):
+        load(at.fd, z).wait()
+        to_p(at.fd, z).wait_recv()
+        a, b = acc.at[at.fd, z], pb.at[at.fd, z]
+        add_rows(a, (0, half), [(a, 0), (b, 0)])
+        half_x(z).start()
+        add_rows(a, (half, half), [(a, half), (b, half)])
+        half_y(z).start()
+
+    def plane_step(z):
+        load(at.fx, z).wait()
+        to_p(at.fx, z).wait_recv()
+        a, b = acc.at[at.fx, z], pb.at[at.fx, z]
+        half_y(z).wait_recv()
+        add_rows(a, (0, half), [(a, 0), (b, 0)])
+        add_rows(a, (half, half), [(a, half), (b, half), (yh.at[z], 0)])
+        full_x(z).start()
+        load(at.fy, z).wait()
+        to_p(at.fy, z).wait_recv()
+        half_x(z).wait_recv()
+        a, b = acc.at[at.fy, z], pb.at[at.fy, z]
+        add_rows(a, (0, half), [(a, 0), (b, 0), (xh.at[z], 0)])
+        add_rows(a, (half, half), [(a, half), (b, half)])
+        full_y(z).start()
+
+    def line_step(z):
+        load(at.f, z).wait()
+        to_p(at.f, z).wait_recv()
+        full_x(z).wait_recv()
+        full_y(z).wait_recv()
+        a = acc.at[at.f, z]
+        four = [(a, 0), (pb.at[at.f, z], 0), (xf.at[z], 0), (yf.at[z], 0)]
+
+        @pl.when(z > at.z)
+        def _():
+            @pl.when(at.z > 0)
+            def _():
+                go_up(z).wait_recv()
+                add_rows(a, (0, rows), four + [(zu.at[z], 0)])
+
+            pl.when(at.z == 0)(lambda: add_rows(a, (0, rows), four))
+            go_up(z).start()
+
+        @pl.when(z < at.z)
+        def _():
+            @pl.when(at.z < nz - 1)
+            def _():
+                go_down(z).wait_recv()
+                add_rows(a, (0, rows), four + [(zd.at[z], 0)])
+
+            pl.when(at.z == nz - 1)(lambda: add_rows(a, (0, rows), four))
+            go_down(z).start()
+
+        @pl.when(z == at.z)
+        def _():
+            add_rows(out, (0, rows), four)
+
+            @pl.when(at.z > 0)
+            def _():
+                go_up(z).wait_recv()
+                add_rows(out, (0, rows), [(out, 0), (zu.at[z], 0)])
+
+            @pl.when(at.z < nz - 1)
+            def _():
+                go_down(z).wait_recv()
+                add_rows(out, (0, rows), [(out, 0), (zd.at[z], 0)])
+
+    def body(i, carry):
+        pl.when(i < steps)(lambda: on_line(i, diag_step))
+        pl.when((i >= 1) & (i < steps + 1))(lambda: on_line(i - 1, plane_step))
+        pl.when(i >= 2)(lambda: on_line(i - 2, line_step))
+        for k in range(1, 5):
+            pl.when(i == k)(functools.partial(small.stage, k))
+        return carry
+
+    lax.fori_loop(0, steps + 2, body, 0)
+
+    def finish(z, carry):
+        for f in range(4):
+            to_p(f, z).wait_send()
+        half_x(z).wait_send()
+        half_y(z).wait_send()
+        full_x(z).wait_send()
+        full_y(z).wait_send()
+        pl.when(z > at.z)(lambda: go_up(z).wait_send())
+        pl.when(z < at.z)(lambda: go_down(z).wait_send())
+        return carry
+
+    lax.fori_loop(0, nz, finish, 0)
+
+
+def scatter_all(parts, small, nz, cid):
+    _, _, r, c = parts.shape
+
+    def buf(*n):
+        return pltpu.VMEM((*n, c), parts.dtype)
+
+    return pl.pallas_call(
+        functools.partial(scatter_kernel, nz),
+        out_shape=(
+            jax.ShapeDtypeStruct((r, c), jnp.float32),
+            jax.ShapeDtypeStruct(small.shape[-2:], jnp.float32),
+        ),
+        in_specs=[pl.BlockSpec(memory_space=pl.ANY), pl.BlockSpec(memory_space=pltpu.VMEM)],
+        out_specs=(pl.BlockSpec(memory_space=pltpu.VMEM),) * 2,
+        scratch_shapes=[
+            buf(4, nz, r), buf(4, nz, r), buf(nz, r // 2), buf(nz, r // 2),
+            buf(nz, r), buf(nz, r), buf(nz, r), buf(nz, r),
+            DMA((4, nz)), DMA((4, nz)), DMA((4, nz)),
+            *[DMA((nz,))] * 12,
+            *SmallScatter.scratch(nz, small.shape[-2:]),
+            *SmallScatter.sems(nz),
+        ],
+        compiler_params=pltpu.CompilerParams(
+            collective_id=cid, has_side_effects=True, vmem_limit_bytes=50 << 20
+        ),
+        cost_estimate=pl.CostEstimate(flops=0, bytes_accessed=240 << 20, transcendentals=0),
+        name="scatter_all",
+    )(parts, small)
+
+
+def square_gather_kernel(own, ids, out, out_ids, xs, xr, ys, yr, fs, fr, js, jr):
+    at = Place()
+    half = own.shape[0] // 2
+    halves = (pl.ds(0, half), pl.ds(half, half))
+    peers = [(at.fx, at.e), (at.fy, at.e), (at.fd, at.e)]
+    greet(peers)
+
+    def to_x(h):
+        return send(own.at[halves[h]], out.at[at.f, halves[h]], xs.at[h], xr.at[h], at.fx, at.e)
+
+    def to_y(h):
+        return send(own.at[halves[h]], out.at[at.f, halves[h]], ys.at[h], yr.at[h], at.fy, at.e)
+
+    x_ref, y_ref = out.at[at.fx, halves[0]], out.at[at.fy, halves[1]]
+    x_on = send(x_ref, x_ref, fs.at[0], fr.at[0], at.fy, at.e)
+    y_on = send(y_ref, y_ref, fs.at[1], fr.at[1], at.fx, at.e)
+    notes = [
+        send(ids, out_ids.at[at.f], js.at[k], jr.at[k], f, e) for k, (f, e) in enumerate(peers)
+    ]
+    to_x(0).start()
+    to_y(1).start()
+    for note in notes:
+        note.start()
+    to_x(1).start()
+    to_y(0).start()
+    out[at.f] = own[...]
+    out_ids[at.f] = ids[...]
+    to_x(0).wait_recv()
+    x_on.start()
+    to_y(1).wait_recv()
+    y_on.start()
+    to_x(1).wait()
+    to_y(0).wait()
+    for note in notes:
+        note.wait()
+    to_x(0).wait_send()
+    to_y(1).wait_send()
+    x_on.wait()
+    y_on.wait()
+
+
+def square_gather(rows, ids, cid):
+    r, c = rows.shape
+    vmem = pl.BlockSpec(memory_space=pltpu.VMEM)
+    return pl.pallas_call(
+        square_gather_kernel,
+        out_shape=(
+            jax.ShapeDtypeStruct((4, r, c), rows.dtype),
+            jax.ShapeDtypeStruct((4, *ids.shape), ids.dtype),
+        ),
+        in_specs=[vmem] * 2,
+        out_specs=(vmem,) * 2,
+        scratch_shapes=[DMA((2,))] * 6 + [DMA((3,))] * 2,
+        compiler_params=pltpu.CompilerParams(collective_id=cid, has_side_effects=True),
+        cost_estimate=pl.CostEstimate(flops=0, bytes_accessed=60 << 20, transcendentals=0),
+        name="square_gather",
+    )(rows, ids)
+
+
+def square_scatter_kernel(part, out, xh, yh, xf, yf, ss, rs):
+    at = Place()
+    rows = out.shape[0]
+    half = rows // 2
+    lo, hi = pl.ds(0, half), pl.ds(half, half)
+    greet([(at.fx, at.e), (at.fy, at.e)])
+
+    def to_x(k, src, dst):
+        return send(src, dst, ss.at[k], rs.at[k], at.fx, at.e)
+
+    def to_y(k, src, dst):
+        return send(src, dst, ss.at[k], rs.at[k], at.fy, at.e)
+
+    copies = [
+        to_x(0, part.at[at.fd, lo], xh),
+        to_y(1, part.at[at.fd, hi], yh),
+        to_x(2, part.at[at.fx, lo], xf.at[lo]),
+        to_y(3, part.at[at.fy, hi], yf.at[hi]),
+        to_x(4, yh, xf.at[hi]),
+        to_y(5, xh, yf.at[lo]),
+    ]
+    for copy in copies[:4]:
+        copy.start()
+    copies[1].wait_recv()
+    add_rows(yh, (0, half), [(yh, 0), (part.at[at.fx], half)])
+    copies[4].start()
+    copies[0].wait_recv()
+    add_rows(xh, (0, half), [(xh, 0), (part.at[at.fy], 0)])
+    copies[5].start()
+    copies[2].wait_recv()
+    copies[5].wait_recv()
+    copies[3].wait_recv()
+    copies[4].wait_recv()
+    add_rows(out, (0, rows), [(part.at[at.f], 0), (xf, 0), (yf, 0)])
+    for copy in copies:
+        copy.wait_send()
+
+
+def square_scatter(parts, cid):
+    _, r, c = parts.shape
+    vmem = pl.BlockSpec(memory_space=pltpu.VMEM)
+
+    def buf(n):
+        return pltpu.VMEM((n, c), parts.dtype)
+
+    return pl.pallas_call(
+        square_scatter_kernel,
+        out_shape=jax.ShapeDtypeStruct((r, c), jnp.float32),
+        in_specs=[vmem],
+        out_specs=vmem,
+        scratch_shapes=[buf(r // 2), buf(r // 2), buf(r), buf(r), DMA((6,)), DMA((6,))],
+        compiler_params=pltpu.CompilerParams(collective_id=cid, has_side_effects=True),
+        cost_estimate=pl.CostEstimate(flops=0, bytes_accessed=60 << 20, transcendentals=0),
+        name="square_scatter",
+    )(parts)
+
+
+def square_sum_kernel(own, out, got, ss, rs):
+    at = Place()
+    peers = [(at.fx, at.e), (at.fy, at.e), (at.fd, at.e)]
+    greet(peers)
+    copies = [send(own, got.at[k], ss.at[k], rs.at[k], f, e) for k, (f, e) in enumerate(peers)]
+    for copy in copies:
+        copy.start()
+    for copy in copies:
+        copy.wait()
+    out[...] = (own[...] + got[0]) + (got[1] + got[2])
+
+
+def square_sum(values, cid):
+    flat = values.reshape(8, -1)
+    vmem = pl.BlockSpec(memory_space=pltpu.VMEM)
+    return pl.pallas_call(
+        square_sum_kernel,
+        out_shape=jax.ShapeDtypeStruct(flat.shape, jnp.float32),
+        in_specs=[vmem],
+        out_specs=vmem,
+        scratch_shapes=[pltpu.VMEM((3, *flat.shape), jnp.float32), DMA((3,)), DMA((3,))],
+        compiler_params=pltpu.CompilerParams(collective_id=cid, has_side_effects=True),
+        cost_estimate=pl.CostEstimate(flops=0, bytes_accessed=10 << 20, transcendentals=0),
+        name="square_sum",
+    )(flat).reshape(values.shape)
+
+
+def line_sum_kernel(nz, counts, *refs):
+    at = Place()
+    refs = iter(refs)
+    n = len(counts)
+    parts, part_small, outs, out_small = take(refs, n), next(refs), take(refs, n), next(refs)
+    bufs = [take(refs, 5) for _ in range(n)]
+    sems = [take(refs, 12) for _ in range(n)]
+    own_small = next(refs)
+    scatter_small = SmallScatter(at, nz, part_small, own_small, take(refs, 4), take(refs, 4))
+    gather_small = SmallGather(at, nz, own_small, out_small, take(refs, 4))
+    greet([(at.fx, at.e), (at.fy, at.e), (at.f, at.pe)], (at, nz))
+    scatter_small.stage(0)
+    total = sum(counts)
+    last = nz - 1
+
+    class Piece:
+        def __init__(self, k, p):
+            self.p, self.part, self.out = p, parts[k], outs[k]
+            self.acc, self.pb, self.zu, self.zd, self.mine = bufs[k]
+            self.sems = sems[k]
+            self.r = self.acc.shape[2]
+
+        def load(self):
+            p = self.p
+            return pltpu.make_async_copy(self.part.at[p, at.c], self.acc.at[p], self.sems[0].at[p])
+
+        def to_p(self):
+            p, (_, s, r, *_rest) = self.p, self.sems
+            return send(self.part.at[p, 1 - at.c], self.pb.at[p], s.at[p], r.at[p], at.f, at.pe)
+
+        def go_up(self, z):
+            p, s, r = self.p, self.sems[3], self.sems[4]
+            return send(self.acc.at[p, z], self.zu.at[p, z], s.at[p, z], r.at[p, z], at.f, at.e + 2)
+
+        def go_down(self, z):
+            p, s, r = self.p, self.sems[5], self.sems[6]
+            return send(self.acc.at[p, z], self.zd.at[p, z], s.at[p, z], r.at[p, z], at.f, at.e - 2)
+
+        def res(self, z, way):
+            p, s, r = self.p, self.sems[7], self.sems[8]
+            ref = self.out.at[p, at.c, z]
+            return send(ref, ref, s.at[way, p, z], r.at[p, z], at.f, at.e + 2 - 4 * way)
+
+        def res_p(self, z):
+            p, s, r = self.p, self.sems[9], self.sems[10]
+            ref = self.out.at[p, at.c, z]
+            return send(ref, ref, s.at[p, z], r.at[p, z], at.f, at.pe)
+
+        def keep(self):
+            p = self.p
+            return pltpu.make_async_copy(self.mine.at[p], self.out.at[p, at.c, at.z], self.sems[11].at[p])
+
+    def piece(q, run, when=True):
+        low = 0
+        for k, count in enumerate(counts):
+            @pl.when((q >= low) & (q < low + count) & when)
+            def _(k=k, low=low):
+                run(Piece(k, q - low))
+
+            low += count
+
+    def start(q, carry):
+        def run(it):
+            it.load().start()
+            it.to_p().start()
+
+        piece(q, run)
+        return carry
+
+    lax.fori_loop(0, total, start, 0)
+
+    def halve(it):
+        it.load().wait()
+        it.to_p().wait_recv()
+        p = it.p
+
+        def body(z, carry):
+            a = it.acc.at[p, z]
+            add_rows(a, (0, it.r), [(a, 0), (it.pb.at[p, z], 0)])
+            return carry
+
+        lax.fori_loop(0, nz, body, 0)
+
+    def rise(it):
+        p = it.p
+
+        def body(i, carry):
+            z = last - i
+
+            @pl.when(z > at.z)
+            def _():
+                a = it.acc.at[p, z]
+
+                @pl.when(at.z > 0)
+                def _():
+                    it.go_up(z).wait_recv()
+                    add_rows(a, (0, it.r), [(a, 0), (it.zu.at[p, z], 0)])
+
+                it.go_up(z).start()
+
+            return carry
+
+        lax.fori_loop(0, last, body, 0)
+
+    def sink(it):
+        p = it.p
+
+        def body(z, carry):
+            @pl.when(z < at.z)
+            def _():
+                a = it.acc.at[p, z]
+
+                @pl.when(at.z < last)
+                def _():
+                    it.go_down(z).wait_recv()
+                    add_rows(a, (0, it.r), [(a, 0), (it.zd.at[p, z], 0)])
+
+                it.go_down(z).start()
+
+            return carry
+
+        lax.fori_loop(0, last, body, 0)
+
+    def settle(it):
+        p, z = it.p, at.z
+        pl.when(z > 0)(lambda: it.go_up(z).wait_recv())
+        pl.when(z < last)(lambda: it.go_down(z).wait_recv())
+        a, dst = (it.acc.at[p, z], 0), it.mine.at[p]
+        up, down = (it.zu.at[p, z], 0), (it.zd.at[p, z], 0)
+        pl.when((z > 0) & (z < last))(lambda: add_rows(dst, (0, it.r), [a, up, down]))
+        pl.when(z == 0)(lambda: add_rows(dst, (0, it.r), [a, down]))
+        pl.when(z == last)(lambda: add_rows(dst, (0, it.r), [a, up]))
+        it.keep().start()
+
+    def tell(it):
+        z = at.z
+        it.keep().wait()
+        pl.when(z < last)(lambda: it.res(z, 0).start())
+        pl.when(z > 0)(lambda: it.res(z, 1).start())
+        it.res_p(z).start()
+
+    def pass_up(it, z):
+        it.res(z, 0).wait_recv()
+        pl.when(at.z < last)(lambda: it.res(z, 0).start())
+        it.res_p(z).start()
+
+    def pass_down(it, z):
+        it.res(z, 0).wait_recv()
+        pl.when(at.z > 0)(lambda: it.res(z, 1).start())
+        it.res_p(z).start()
+
+    def body(i, carry):
+        piece(i, halve)
+        piece(i - at.z, rise, at.z < last)
+        piece(i - (last - at.z), sink, at.z > 0)
+        piece(i - nz, settle)
+        piece(i - nz, tell)
+        for d in range(1, nz):
+            piece(i - nz - d, functools.partial(pass_up, z=at.z - d), at.z >= d)
+            piece(i - nz - d, functools.partial(pass_down, z=at.z + d), at.z + d <= last)
+        for s in range(1, 5):
+            pl.when(i == s)(functools.partial(scatter_small.stage, s))
+        for s in range(5):
+            pl.when(i == 5 + s)(functools.partial(gather_small.stage, s))
+        return carry
+
+    lax.fori_loop(0, total + 2 * nz - 1, body, 0)
+
+    def finish(q, carry):
+        def run(it):
+            it.to_p().wait_send()
+
+            def one(z, carry):
+                pl.when(z > at.z)(lambda: it.go_up(z).wait_send())
+                pl.when(z < at.z)(lambda: it.go_down(z).wait_send())
+                pl.when((z <= at.z) & (at.z < last))(lambda: it.res(z, 0).wait_send())
+                pl.when((z >= at.z) & (at.z > 0))(lambda: it.res(z, 1).wait_send())
+                it.res_p(z).wait_send()
+                it.res_p(z).wait_recv()
+                return carry
+
+            lax.fori_loop(0, nz, one, 0)
+
+        piece(q, run)
+        return carry
+
+    lax.fori_loop(0, total, finish, 0)
+
+
+def line_sum(parts, small, nz, cid):
+    counts = tuple(p.shape[0] for p in parts)
+    scratch, sems = [], []
+    for p in parts:
+        n, _, _, r, c = p.shape
+
+        def buf(*lead):
+            return pltpu.VMEM((*lead, r, c), p.dtype)
+
+        scratch += [buf(n, nz), buf(n, nz), buf(n, nz), buf(n, nz), buf(n)]
+        each, line = DMA((n,)), DMA((n, nz))
+        sems += [each, each, each, line, line, line, line, DMA((2, n, nz)), line, line, line, each]
+    hbm, vmem = pl.BlockSpec(memory_space=pl.ANY), pl.BlockSpec(memory_space=pltpu.VMEM)
+    return pl.pallas_call(
+        functools.partial(line_sum_kernel, nz, counts),
+        out_shape=(
+            *(jax.ShapeDtypeStruct(p.shape, p.dtype) for p in parts),
+            jax.ShapeDtypeStruct(small.shape, jnp.float32),
+        ),
+        in_specs=[hbm] * len(parts) + [vmem],
+        out_specs=(*[hbm] * len(parts), vmem),
+        scratch_shapes=[
+            *scratch, *sems, pltpu.VMEM(small.shape[-2:], jnp.float32),
+            *SmallScatter.scratch(nz, small.shape[-2:]), *SmallScatter.sems(nz), *SmallGather.sems(nz),
+        ],
+        compiler_params=pltpu.CompilerParams(
+            collective_id=cid, has_side_effects=True, vmem_limit_bytes=50 << 20
+        ),
+        cost_estimate=pl.CostEstimate(flops=0, bytes_accessed=300 << 20, transcendentals=0),
+        name="line_sum",
+    )(*parts, small)
 
 
 def rope_tables(seg_ids, head_dim):
@@ -44,11 +916,16 @@
     return grads_in * cosine[:, None, :] + rotate_back(grads_in * sine_table[:, None, :])
 
 
-def across_heads(pair_sums):
+def across_heads(kernel, pair_sums):
+    if kernel:
+        return square_sum(jnp.stack(pair_sums), kernel)
     return lax.psum((pair_sums[0], pair_sums[1]), "fsdp")
 
 
-def share_rows(term_fn, own_rows):
+def share_rows(kernel, term_fn, own_rows):
+    if kernel:
+        parts = term_fn(jnp.int32(0), own_rows * lax.axis_size("fsdp"))
+        return square_scatter(parts.reshape(-1, own_rows, parts.shape[1]), kernel)
     return lax.psum_scatter(
         term_fn(jnp.int32(0), own_rows * lax.axis_size("fsdp")),
         "fsdp",
@@ -216,10 +1093,12 @@
     gate_kept = gate_wts * kept_mask
 
     grad_all = lax.all_gather(cotangent, ("fsdp", "expert"), axis=0, tiled=True)
-    rows_all = lax.all_gather(second_rows, ("fsdp", "expert"), axis=0, tiled=True)
-    kept_all = lax.all_gather(gate_kept, ("fsdp", "expert"), axis=0, tiled=True)
+    nz = owners // 2
+    rows_all, kept_all = gather_all(second_rows, gate_kept.T, nz, 7)
+    rows_all = rows_all.reshape(-1, model_width)
     first_expert = lax.axis_index("expert") * local_experts
-    gate_here = lax.dynamic_slice_in_dim(kept_all, first_expert, local_experts, axis=1)
+    gate_here = lax.dynamic_slice_in_dim(kept_all, first_expert, local_experts, axis=3)
+    gate_here = jnp.transpose(gate_here, (1, 2, 0, 4, 3)).reshape(-1, local_experts)
     gate_cols = jnp.repeat(gate_here, hidden_here, axis=1)
     tokens = rows_all.shape[0]
 
@@ -243,13 +1122,15 @@
         jnp.einsum("th,dh->td", grad_gate_in, gate_w, preferred_element_type=jnp.float32)
         + jnp.einsum("th,dh->td", grad_up_in, up_w, preferred_element_type=jnp.float32)
     ).astype(jnp.bfloat16)
-    back_rows = lax.psum_scatter(back, "fsdp", scatter_dimension=0, tiled=True)
-    back_rows = lax.psum_scatter(back_rows, "expert", scatter_dimension=0, tiled=True)
-    terms = lax.psum_scatter(
-        gate_terms.reshape(shards, owners * tok_count, local_experts), "fsdp", scatter_dimension=0, tiled=True
-    ).reshape(owners, tok_count, local_experts)
-    terms = lax.all_to_all(terms, "expert", split_axis=0, concat_axis=0, tiled=True)
-    grad_gate_k = jnp.transpose(terms, (1, 0, 2)).reshape(tok_count, experts) * kept_mask
+    terms = jnp.transpose(
+        gate_terms.reshape(shards, nz, 2, tok_count, local_experts), (2, 0, 1, 4, 3)
+    )
+    terms = lax.dynamic_update_slice_in_dim(
+        jnp.zeros((2, shards, nz, experts, tok_count), jnp.float32), terms, first_expert, axis=3
+    )
+    back = back.reshape(shards, owners, tok_count, model_width)
+    back_rows, terms = scatter_all(back, terms, nz, 8)
+    grad_gate_k = terms.T * kept_mask
     forward = jnp.dot(weighted, down_w, preferred_element_type=jnp.float32).astype(jnp.bfloat16)
     forward_rows = lax.psum_scatter(forward, "fsdp", scatter_dimension=0, tiled=True)
     forward_rows = lax.psum_scatter(forward_rows, "expert", scatter_dimension=0, tiled=True)
@@ -257,7 +1138,7 @@
     grad_logits = gate_wts * (grad_gate_k - jnp.sum(gate_wts * grad_gate_k, axis=1, keepdims=True))
     router_grad = jnp.dot(grad_logits.T, second_rows.astype(jnp.float32), precision=precise)
     grad_second = jnp.dot(grad_logits, w_router.astype(jnp.float32).T, precision=precise)
-    grad_second = grad_second + back_rows.astype(jnp.float32)
+    grad_second = grad_second + back_rows
 
     def by_expert(left, right):
         return jnp.dot(left.T, right, preferred_element_type=jnp.float32)
@@ -267,6 +1148,22 @@
     grad_up_w = jnp.stack([by_expert(rows_all, grad_up_in[:, p]) for p in parts])
     grad_down_w = by_expert(weighted, grad_all).reshape(local_experts, hidden_here, model_width)
     return block_output, grad_second, router_grad, (grad_gate_w, grad_up_w, grad_down_w)
+
+
+def sum_grads(narrow, gains, head_gains, nz):
+    shards, width = lax.axis_size("fsdp"), gains.shape[1]
+    mine = lax.iota(jnp.int32, shards) == lax.axis_index("fsdp")
+    heads_flat = jnp.pad(head_gains.reshape(-1), (0, width - head_gains.size))
+    rows = jnp.concatenate([gains, jnp.where(mine[:, None], heads_flat[None], 0.0)], axis=0)
+    share = -(-rows.size // (2 * shards * nz * 1024)) * 8
+    small = jnp.pad(rows.reshape(-1), (0, 2 * shards * nz * share * 128 - rows.size))
+    small = small.reshape(2, shards, nz, share, 128)
+    parts = [g.reshape(-1, 2, nz, 16, g.shape[1]) for g in narrow]
+    *sums, small = line_sum(parts, small, nz, 9)
+    small = small.reshape(-1)[: rows.size].reshape(rows.shape)
+    own = lax.dynamic_slice_in_dim(small, gains.shape[0] + lax.axis_index("fsdp"), 1, axis=0)
+    head_gains = own[0, : head_gains.size].reshape(head_gains.shape)
+    return [s.reshape(g.shape) for s, g in zip(sums, narrow)], small[: gains.shape[0]], head_gains
 
 
 def on_device(
@@ -290,14 +1187,22 @@
 ):
     tok_count = block_input.shape[1]
     model_width = block_input.shape[2]
+    experts = w_router.shape[1]
+    nz = lax.axis_size("expert") // 2
+    dense = 2 * TOP >= experts and lax.axis_size("fsdp") == 4
     flat_in = block_input[0].astype(jnp.float32)
     scale_one = lax.rsqrt(jnp.mean(flat_in * flat_in, axis=1, keepdims=True) + epsilon)
     normed_one = flat_in * scale_one
     first_rows = (normed_one * attn_gain).astype(jnp.bfloat16)
-    group_rows, group_segs = (
-        lax.all_gather(first_rows, "fsdp", axis=0, tiled=True),
-        lax.all_gather(segments[0], "fsdp", axis=0, tiled=True),
-    )
+    if dense:
+        group_rows, group_segs = square_gather(first_rows, jnp.tile(segments, (8, 1)), 1)
+        group_rows = group_rows.reshape(-1, model_width)
+        group_segs = group_segs[:, 0].reshape(-1)
+    else:
+        group_rows, group_segs = (
+            lax.all_gather(first_rows, "fsdp", axis=0, tiled=True),
+            lax.all_gather(segments[0], "fsdp", axis=0, tiled=True),
+        )
     group_len = group_rows.shape[0]
     heads_here = w_query.shape[1] // HEAD_DIM
     query_rows = jnp.dot(group_rows, w_query, preferred_element_type=jnp.float32)
@@ -306,6 +1211,7 @@
         jnp.bfloat16
     )
     square_sums = across_heads(
+        dense and 2,
         (jnp.sum(query_rows * query_rows, axis=1), jnp.sum(key_rows * key_rows, axis=1))
     )
     q_scale = lax.rsqrt(square_sums[0][:, None] / model_width + epsilon)
@@ -336,13 +1242,12 @@
     def mixed_term(start, length):
         return jnp.dot(attn_rows, w_output, preferred_element_type=jnp.float32).astype(jnp.bfloat16)
 
-    mixed_rows = share_rows(mixed_term, tok_count).astype(jnp.float32)
+    mixed_rows = share_rows(dense and 4, mixed_term, tok_count).astype(jnp.float32)
     second_in = flat_in + mixed_rows
     scale_two = lax.rsqrt(jnp.mean(second_in * second_in, axis=1, keepdims=True) + epsilon)
     normed_two = second_in * scale_two
     second_rows = (normed_two * mlp_gain).astype(jnp.bfloat16)
-    experts = w_router.shape[1]
-    if TOP * 2 >= experts:
+    if dense:
         block_output, grad_second, router_grad, expert_grads = experts_dense(
             second_in, second_rows, cotangent[0], routes[0], capacity, w_router, w_gate, w_up, w_down
         )
@@ -357,7 +1262,11 @@
     grad_mid = grad_out + scale_two * (
         grad_normed_two - normed_two * jnp.mean(grad_normed_two * normed_two, axis=1, keepdims=True)
     )
-    group_grad = lax.all_gather(grad_mid.astype(jnp.bfloat16), "fsdp", axis=0, tiled=True)
+    if dense:
+        group_grad, _ = square_gather(grad_mid.astype(jnp.bfloat16), jnp.tile(segments, (8, 1)), 6)
+        group_grad = group_grad.reshape(-1, model_width)
+    else:
+        group_grad = lax.all_gather(grad_mid.astype(jnp.bfloat16), "fsdp", axis=0, tiled=True)
     out_grad = jnp.einsum("ti,td->id", attn_rows, group_grad, preferred_element_type=jnp.float32)
     grad_attn = (
         jnp.einsum("td,id->ti", group_grad, w_output, preferred_element_type=jnp.float32)
@@ -390,6 +1299,7 @@
     inner_q = grad_q_normed * q_gain
     inner_k = grad_k_normed * k_gain
     inner_sums = across_heads(
+        dense and 3,
         (jnp.sum(inner_q * query_rows, axis=1), jnp.sum(inner_k * key_rows, axis=1))
     )
     grad_query_rows = (
@@ -400,15 +1310,10 @@
         k_scale * (inner_k - key_rows * k_scale * k_scale * (inner_sums[1][:, None] / model_width))
     ).astype(jnp.bfloat16)
     grad_value_rows = grad_values.reshape(group_len, -1).astype(jnp.bfloat16)
-    query_grad = jnp.einsum(
-        "td,ti->di", group_rows, grad_query_rows, preferred_element_type=jnp.float32
-    )
-    key_grad = jnp.einsum(
-        "td,ti->di", group_rows, grad_key_rows, preferred_element_type=jnp.float32
-    )
-    value_grad = jnp.einsum(
-        "td,ti->di", group_rows, grad_value_rows, preferred_element_type=jnp.float32
-    )
+    head_grads = jnp.concatenate([grad_query_rows, grad_key_rows, grad_value_rows], axis=1)
+    mixer_grad = jnp.einsum(
+        "td,ti->di", group_rows, head_grads, preferred_element_type=jnp.float32
+    ).astype(jnp.bfloat16)
 
     def input_term(start, length):
         from_q = jnp.einsum(
@@ -420,19 +1325,23 @@
         )
         return (from_q + from_k + from_v).astype(jnp.bfloat16)
 
-    grad_first = share_rows(input_term, tok_count).astype(jnp.float32)
+    grad_first = share_rows(dense and 5, input_term, tok_count).astype(jnp.float32)
     attn_gain_grad = jnp.sum(grad_first * normed_one, axis=0)
     grad_normed_one = grad_first * attn_gain
     grad_x = grad_mid + scale_one * (
         grad_normed_one - normed_one * jnp.mean(grad_normed_one * normed_one, axis=1, keepdims=True)
     )
-    narrow = tuple(g.astype(jnp.bfloat16) for g in (query_grad, key_grad, value_grad, out_grad))
-    mixer = tuple(g.astype(jnp.float32) for g in lax.psum(narrow, "expert"))
-    mixer = mixer + lax.psum((q_gain_grad, k_gain_grad), "expert")
-    shared = lax.psum(
-        jnp.concatenate([attn_gain_grad[None], mlp_gain_grad[None], router_grad], axis=0),
-        ("fsdp", "expert"),
-    )
+    narrow = (mixer_grad, out_grad.astype(jnp.bfloat16))
+    gains = jnp.concatenate([attn_gain_grad[None], mlp_gain_grad[None], router_grad], axis=0)
+    head_gains = jnp.stack([q_gain_grad, k_gain_grad])
+    if dense:
+        narrow, gains, head_gains = sum_grads(narrow, gains, head_gains, nz)
+    else:
+        narrow = lax.psum(narrow, "expert")
+        head_gains = lax.psum(head_gains, "expert")
+        gains = lax.psum(gains, ("fsdp", "expert"))
+    wide = tuple(jnp.split(narrow[0], 3, axis=1)) + (narrow[1],)
+    mixer = tuple(g.astype(jnp.float32) for g in wide) + (head_gains[0], head_gains[1])
     return (
         block_output,
         grad_x[None],
@@ -442,9 +1351,9 @@
         mixer[3],
         mixer[4],
         mixer[5],
-        shared[0],
-        shared[1],
-        shared[2:].T,
+        gains[0],
+        gains[1],
+        gains[2:].T,
         grad_gate_w,
         grad_up_w,
         grad_down_w,

time: 1300 us -> 784 us (0.60)
  waiting for transfers between devices: 895 us -> 1.55 us
  Pallas kernels: 0 us -> 492 us
  blocking collectives: 100 us -> 0 us
  starting transfers between devices: 13.8 us -> 0.12 us
    pallas_call x0 -> x9, Pallas kernels: none -> 492 us  [the longest x1 141 us: scatter_all(): pl.pallas_call(functools.partial(scatter_kernel, nz), out_shape=(jax.Shap...]
    psum x2 -> x0, waiting for transfers between devices: 292 us -> none  [the longest x1 174 us: on_device(): mixer = tuple((g.astype(jnp.float32) for g in lax.psum(narrow, 'expert')))]
    reduce_scatter x4 -> x0, waiting for transfers between devices: 238 us -> none  [the longest x1 151 us: experts_dense(): back_rows = lax.psum_scatter(back, 'fsdp', scatter_dimension=0, tiled=True)]
    all_gather x3 -> x0, waiting for transfers between devices: 141 us -> none  [the longest x1 95.5 us: experts_dense(): lax.all_gather(second_rows, ('fsdp', 'expert'), axis=0, tiled=True)]
    reduce_scatter x1, waiting for transfers between devices: 125 us -> 0.01 us  [experts_dense(): lax.psum_scatter(forward, 'fsdp', scatter_dimension=0, tiled=True)]
    all_gather x1, waiting for transfers between devices: 89.2 us -> 0.01 us  [experts_dense(): grad_all = lax.all_gather(cotangent, ('fsdp', 'expert'), axis=0, tiled=True)]
    all_gather x2 -> x0, blocking collectives: 48.2 us -> none  [the longest x1 38.7 us: experts_dense(): kept_all = lax.all_gather(gate_kept, ('fsdp', 'expert'), axis=0, tiled=True)]
    psum x3 -> x0, blocking collectives: 36.5 us -> none  [the longest x2 18.4 us: across_heads(): return lax.psum((pair_sums[0], pair_sums[1]), 'fsdp')]
  transfers between devices with their start and end apart: 13 -> 3, of which waited for: 12 -> 1; matrix products, arithmetic and copies ran while one was open for 12% -> 28% of each run, Pallas kernels for 0% -> 63%
where the time goes in v2:
time: 784 us; the launch traced here: 779 us
  Pallas kernels  492 us (63%)
  matrix products  200 us (26%)
  other arithmetic  46.4 us (6%)
  local copies, waits for them, and re-layouts  24.3 us (3%)
  between operations  15.2 us (2%)
    pallas_call x1, Pallas kernels, scatter_all(): pl.pallas_call(functools.partial(scatter_kernel, nz), out_shape=(jax.Shap...  141 us
    pallas_call x1, Pallas kernels, line_sum(): pl.pallas_call(functools.partial(line_sum_kernel, nz, counts), out_shape=...  125 us
    pallas_call x1, Pallas kernels, gather_all(): pl.pallas_call(functools.partial(gather_kernel, nz), out_shape=(jax.Shape...  88.2 us
    pallas_call x2, Pallas kernels, square_gather(): pl.pallas_call(square_gather_kernel, out_shape=(jax.ShapeDtypeStruct((4,...  65.2 us
    pallas_call x2, Pallas kernels, square_scatter(): pl.pallas_call(square_scatter_kernel, out_shape=jax.ShapeDtypeStruct((r,...  60.6 us
    dot_general x5, matrix products, by_expert(): return jnp.dot(left.T, right, preferred_element_type=jnp.float32)  51.7 us
    dot_general x1, matrix products, experts_dense(): jnp.einsum('td,hd->th', grad_all, down_w, preferred_element_type=jnp.floa...  25 us
    dot_general x1, matrix products, experts_dense(): jnp.einsum('th,dh->td', grad_up_in, up_w, preferred_element_type=jnp.floa...  23.7 us
  transfers between devices with their start and end apart: 3, of which 1 were waited for; matrix products, arithmetic and copies ran while one was open for 28% of the time, Pallas kernels for 63%

profile of v2, /device:TPU:0, one launch (start us, length us, event | category | flops | bytes accessed | tf_op | source)
XLA Modules:
  0.0 779.4 jit_solution(7818861447130374600)
XLA Ops:
  9.9 2.0 fusion.21.own
  13.2 28.3 %square_gather.2 = (bf16[4,128,2048]{2,1,0:T(8,128)(2,1)}, s32[4,8,128]{2,1,0:T(8,128)}) custom-call(bf16[128,2048]{1,0:T(8,128)(2,1)} %fusion.21.own, s32[8,128]{1,0:T(8,128)} %tile.5.ids), custom_call_target="tpu_custom_call" | custom-call | bytes 62914560 | tf_op jit(solution)/shard_map/square_gather/pallas_call | solution.py:566
  42.4 4.6 multiply_reduce_fusion.7
  47.0 1.3 multiply_reduce_fusion.6
  49.0 6.2 square_sum.2
  55.2 4.1 copy.56
  59.3 3.9 copy.57
  63.4 1.7 broadcast_multiply_fusion.3
  65.4 1.4 multiply_multiply_fusion.2
  69.8 2.1 copy-done.70
  73.3 1.4 convolution_convert_fusion.7
  75.1 2.6 convolution_convert_fusion.3
  77.7 39.7 %square_scatter.2 = f32[128,2048]{1,0:T(8,128)} custom-call(bf16[4,128,2048]{2,1,0:T(8,128)(2,1)} %bitcast.234), custom_call_target="tpu_custom_call" | custom-call | bytes 62914560 | tf_op jit(solution)/shard_map/square_scatter/pallas_call | solution.py:626
  117.4 1.6 multiply_reduce_fusion.5
  121.7 88.2 %gather_all.1 = (bf16[4,8,128,2048]{3,2,1,0:T(8,128)(2,1)}, f32[2,4,4,16,128]{4,3,2,1,0:T(8,128)}) custom-call(bf16[128,2048]{1,0:T(8,128)(2,1)} %copy-done.13, f32[16,128]{1,0:T(8,128)} %get-tuple-element.86.own_small), custom_call_target="tpu_custom_call" | custom-call | bytes 251658240 | tf_op jit(solution)/shard_map/gather_all/pallas_call | solution.py:315
  210.9 15.5 %fusion.57 = f32[4096,512]{0,1:T(8,128)} fusion(bf16[4096,2048]{1,0:T(8,128)(2,1)} %bitcast.263, bf16[2048,512]{0,1:T(8,128)(2,1)} %bitcast.235), kind=kOutput, calls=%fused_computation.161 | convolution fusion | flops 8589934592 | bytes 27262976 | tf_op jit(solution)/shard_map/dot_general | solution.py:1110
  226.3 11.1 %fusion.56 = f32[4096,512]{0,1:T(8,128)} fusion(bf16[4096,2048]{1,0:T(8,128)(2,1)S(1)} %bitcast.268, bf16[2048,512]{0,1:T(8,128)(2,1)S(1)} %bitcast.238), kind=kOutput, calls=%fused_computation.160 | convolution fusion | flops 8589934592 | bytes 27262976 | tf_op jit(solution)/shard_map/dot_general | solution.py:1109
  237.4 25.0 %multiply_convert_fusion = (bf16[4096,512]{0,1:T(8,128)(2,1)}, bf16[4096,512]{0,1:T(8,128)(2,1)}, bf16[4096,512]{0,1:T(8,128)(2,1)}, f32[4096,512]{0,1:T(8,128)}) fusion(f32[4096,2]{0,1:T(2,128)S(1)} %reshape.367, f32[4096,512]{0,1:T(8,128)} %fusion.56, f32[4096,512]{0,1:T(8,128)} %fusion.57, bf16[512,2048]{1,0:T(8,128)(2,1)S(1)} %bitcast.220, ...), kind=kOutput, calls=%fused_computation.10 | convolution fusion | flops 8625586176 | bytes 56655872 | tf_op jit(solution)/shard_map/td,hd->th/dot_general | solution.py:1108
  262.4 14.7 %convolution_convert_fusion = bf16[4096,2048]{1,0:T(8,128)(2,1)} fusion(bf16[4096,512]{0,1:T(8,128)(2,1)} %get-tuple-element.46, bf16[512,2048]{1,0:T(8,128)(2,1)S(1)} %bitcast.219), kind=kOutput, calls=%fused_computation.5 | convolution fusion | flops 8598323200 | bytes 23068672 | tf_op jit(solution)/shard_map/dot_general | solution.py:1134
  277.1 9.6 %bitcast_reduce_fusion = f32[4096,2]{0,1:T(2,128)S(1)} fusion(f32[4096,512]{0,1:T(8,128)} %get-tuple-element.88, f32[4096,512]{0,1:T(8,128)} %fusion.57, f32[4096,512]{0,1:T(8,128)} %fusion.56), kind=kLoop, calls=%fused_computation.9 | loop fusion | flops 14671872 | bytes 25198592 | tf_op jit(solution)/shard_map/reduce_sum | solution.py:1114
  286.9 18.9 %fusion.58 = f32[4096,2048]{1,0:T(8,128)} fusion(bf16[4096,512]{0,1:T(8,128)(2,1)} %get-tuple-element.45, bf16[2048,512]{0,1:T(8,128)(2,1)} %bitcast.237), kind=kOutput, calls=%fused_computation.162 | convolution fusion | flops 8589934592 | bytes 39845888 | tf_op jit(solution)/shard_map/th,dh->td/dot_general | solution.py:1122
  305.8 23.7 %add_convert_fusion = bf16[4096,2048]{1,0:T(8,128)(2,1)} fusion(f32[4096,2048]{1,0:T(8,128)} %fusion.58, bf16[4096,512]{0,1:T(8,128)(2,1)} %get-tuple-element.44, bf16[2048,512]{0,1:T(8,128)(2,1)} %bitcast.236), kind=kOutput, calls=%fused_computation | convolution fusion | flops 8606711808 | bytes 56623104 | tf_op jit(solution)/shard_map/th,dh->td/dot_general | solution.py:1123
  329.5 141.5 %scatter_all.1 = (f32[128,2048]{1,0:T(8,128)S(1)}, f32[16,128]{1,0:T(8,128)S(1)}) custom-call(bf16[4,8,128,2048]{3,2,1,0:T(8,128)(2,1)} %bitcast.224, f32[2,4,4,16,128]{4,3,2,1,0:T(8,128)S(1)} %bitcast_dynamic-update-slice_fusion.part_small), custom_call_target="tpu_custom_call" | custom-call | bytes 251658240 | tf_op jit(solution)/shard_map/scatter_all/pallas_call | solution.py:498
  474.2 37.0 %square_gather.3 = (bf16[4,128,2048]{2,1,0:T(8,128)(2,1)}, s32[4,8,128]{2,1,0:T(8,128)}) custom-call(bf16[128,2048]{1,0:T(8,128)(2,1)} %fusion.51.own, s32[8,128]{1,0:T(8,128)} %tile.5.ids), custom_call_target="tpu_custom_call" | custom-call | bytes 62914560 | tf_op jit(solution)/shard_map/square_gather/pallas_call | solution.py:566
  511.2 3.7 convolution_convert_fusion.4
  514.9 1.6 multiply_reduce_fusion
  522.3 5.9 square_sum.3
  529.1 1.8 multiply_convert_fusion.4
  530.9 1.5 multiply_convert_fusion.3
  532.4 1.3 fusion.59
  534.2 1.3 fusion.60
  536.5 1.4 convolution_convert_fusion.6
  538.6 3.1 add_convert_fusion.1
  541.8 20.8 %square_scatter.3 = f32[128,2048]{1,0:T(8,128)} custom-call(bf16[4,128,2048]{2,1,0:T(8,128)(2,1)} %bitcast.229), custom_call_target="tpu_custom_call" | custom-call | bytes 62914560 | tf_op jit(solution)/shard_map/square_scatter/pallas_call | solution.py:626
  562.6 1.6 fusion.27
  564.8 4.5 convolution_convert_fusion.2
  569.3 6.4 convolution_convert_fusion.1
  575.7 125.0 %line_sum.1 = (bf16[16,2,4,16,1536]{4,3,2,1,0:T(8,128)(2,1)}, bf16[4,2,4,16,2048]{4,3,2,1,0:T(8,128)(2,1)S(1)}, f32[2,4,4,16,128]{4,3,2,1,0:T(8,128)S(1)}) custom-call(bf16[16,2,4,16,1536]{4,3,2,1,0:T(8,128)(2,1)} %bitcast.230, bf16[4,2,4,16,2048]{4,3,2,1,0:T(8,128)(2,1)} %bitcast.239, f32[2,4,4,16,128]{4,3,2,1,0:T(8,128)S(1)} %bitcast.221), custom_call_target="tpu_custom_call" | custom-call | bytes 314572800 | tf_op jit(solution)/shard_map/line_sum/pallas_call | solution.py:867
  702.1 9.7 %convolution_bitcast_fusion = f32[1,2048,256]{2,1,0:T(8,128)} fusion(bf16[4096,2048]{1,0:T(8,128)(2,1)} %bitcast.264, bf16[4096,512]{0,1:T(8,128)(2,1)S(1)} %copy-done.22), kind=kOutput, calls=%fused_computation.27 | convolution fusion | flops 4294967296 | bytes 20971520 | tf_op jit(solution)/shard_map/dot_general | solution.py:1144
  711.9 9.9 %convolution_bitcast_fusion.1 = f32[1,2048,256]{2,1,0:T(8,128)} fusion(bf16[4096,2048]{1,0:T(8,128)(2,1)} %bitcast.265, bf16[4096,512]{0,1:T(8,128)(2,1)S(1)} %copy-done.22), kind=kOutput, calls=%fused_computation.28 | convolution fusion | flops 4294967296 | bytes 20971520 | tf_op jit(solution)/shard_map/dot_general | solution.py:1144
  721.7 1.4 fusion.55
  723.2 9.4 %convolution_bitcast_fusion.2 = f32[1,2048,256]{2,1,0:T(8,128)S(1)} fusion(bf16[4096,2048]{1,0:T(8,128)(2,1)} %bitcast.266, bf16[4096,512]{0,1:T(8,128)(2,1)} %get-tuple-element.45), kind=kOutput, calls=%fused_computation.29 | convolution fusion | flops 4294967296 | bytes 20971520 | tf_op jit(solution)/shard_map/dot_general | solution.py:1144
  732.6 8.5 %convolution_bitcast_fusion.3 = f32[1,2048,256]{2,1,0:T(8,128)S(1)} fusion(bf16[4096,2048]{1,0:T(8,128)(2,1)} %bitcast.267, bf16[4096,512]{0,1:T(8,128)(2,1)S(1)} %copy-done.21), kind=kOutput, calls=%fused_computation.30 | convolution fusion | flops 4294967296 | bytes 20971520 | tf_op jit(solution)/shard_map/dot_general | solution.py:1144
  741.1 4.1 pad_maximum_fusion
  745.9 2.7 bitcast_convert_fusion
  748.5 5.5 slice_convert_fusion
  754.0 14.2 %fusion = f32[512,2048]{1,0:T(8,128)} fusion(bf16[4096,512]{0,1:T(8,128)(2,1)S(1)} %copy-done.20, bf16[1,4096,2048]{2,1,0:T(8,128)(2,1)} %all-gather.3.cloned.1.call-done), kind=kOutput, calls=%fused_computation.1 | convolution fusion | flops 8589934592 | bytes 25165824 | tf_op jit(solution)/shard_map/dot_general | solution.py:1144
  769.1 3.6 fusion.26
  (220 shorter events, 29.5 us)
Async XLA Ops:
  7.2 230.2 %copy-start = (bf16[2,256,2048]{2,1,0:T(8,128)(2,1)S(1)}, bf16[2,256,2048]{2,1,0:T(8,128)(2,1)}, u32[]{:S(2)}) copy-start(bf16[2,256,2048]{2,1,0:T(8,128)(2,1)} %param.30) | copy-start | bytes 6291460
  7.2 230.2 %all-gather.3.cloned.1.call-start = ((), (), s32[]{:S(2)}) async-start(), calls=%async_computation.4 | async-start | bytes 17301504 | tf_op jit(solution)/shard_map/all_gather | solution.py:1095
  7.9 713.8 %reduce-scatter.3.cloned.1.call-start = ((), (), s32[]{:S(2)}) async-start(), calls=%async_computation.2 | async-start | bytes 20971520 | tf_op jit(solution)/shard_map/reduce_scatter | solution.py:1135
  9.9 32.5 %copy-start.64 = (f32[128]{0:T(128)}, f32[128]{0:T(128)S(1)}, u32[]{:S(2)}) copy-start(f32[128]{0:T(128)S(1)} %add_rsqrt_fusion.1) | copy-start | bytes 1540
  42.3 4.7 copy-start.29
  42.4 4.7 copy-start.69
  48.3 18.6 %copy-start.8 = (f32[512,512]{0,1:T(8,128)}, f32[512,512]{0,1:T(8,128)S(1)}, u32[]{:S(2)}) copy-start(f32[512,512]{0,1:T(8,128)S(1)} %get-tuple-element.79) | copy-start | bytes 3145732
  55.2 9.9 %copy-start.57 = (f32[8,128]{1,0:T(8,128)S(1)}, f32[8,128]{1,0:T(8,128)}, u32[]{:S(2)}) copy-start(f32[8,128]{1,0:T(8,128)} %square_sum.2) | copy-start | bytes 12292
  55.2 10.2 %copy-start.53 = (f32[512]{0:T(512)S(1)}, f32[512]{0:T(512)}, u32[]{:S(2)}) copy-start(f32[512]{0:T(512)} %param.23) | copy-start | bytes 6148
  59.3 7.5 copy-start.55
  67.9 4.1 copy-start.70
  68.8 4.4 copy-start.2
  73.3 4.4 copy-start.35
  74.7 42.7 %copy-start.72 = (bf16[4,128,512]{2,1,0:T(8,128)(2,1)}, bf16[4,128,512]{2,1,0:T(8,128)(2,1)S(1)}, u32[]{:S(2)}) copy-start(bf16[4,128,512]{2,1,0:T(8,128)(2,1)S(1)} %convolution_convert_fusion.7) | copy-start | bytes 1572868
  75.0 42.4 %copy-start.66 = (s32[1,128,8]{1,2,0:T(8,128)S(1)}, s32[1,128,8]{1,2,0:T(8,128)}, u32[]{:S(2)}) copy-start(s32[1,128,8]{1,2,0:T(8,128)} %param.32) | copy-start | bytes 12292
  77.7 42.0 %copy-start.42 = (f32[2048]{0:T(1024)S(1)}, f32[2048]{0:T(1024)}, u32[]{:S(2)}) copy-start(f32[2048]{0:T(1024)} %param.26) | copy-start | bytes 24580
  77.7 42.9 %copy-start.41 = (bf16[2048,16]{0,1:T(8,128)(2,1)S(1)}, bf16[2048,16]{0,1:T(8,128)(2,1)}, u32[]{:S(2)}) copy-start(bf16[2048,16]{0,1:T(8,128)(2,1)} %param.27) | copy-start | bytes 196612
  117.4 3.4 copy-start.44
  210.8 15.5 %copy-start.27 = (bf16[2,2048,256]{1,2,0:T(8,128)(2,1)S(1)}, bf16[2,2048,256]{1,2,0:T(8,128)(2,1)}, u32[]{:S(2)}) copy-start(bf16[2,2048,256]{1,2,0:T(8,128)(2,1)} %copy.56) | copy-start | bytes 6291460
  210.9 15.5 %copy-start.67 = (bf16[4,8,128,2048]{3,2,1,0:T(8,128)(2,1)S(1)}, bf16[4,8,128,2048]{3,2,1,0:T(8,128)(2,1)}, u32[]{:S(2)}) copy-start(bf16[4,8,128,2048]{3,2,1,0:T(8,128)(2,1)} %get-tuple-element.26) | copy-start | bytes 50331652
  277.1 492.0 %reduce-scatter.5.cloned.1.call-start = ((), (), s32[]{:S(2)}) async-start(), calls=%async_computation.3 | async-start | bytes 4718592 | tf_op jit(solution)/shard_map/reduce_scatter | solution.py:1136
  329.5 141.5 %copy-start.45 = (pred[128,16]{0,1:T(8,128)(4,1)S(1)}, pred[128,16]{0,1:T(8,128)(4,1)}, u32[]{:S(2)}) copy-start(pred[128,16]{0,1:T(8,128)(4,1)} %copy-done.44) | copy-start | bytes 6148
  329.5 141.5 %copy-start.52 = (pred[128,16]{0,1:T(8,128)(4,1)S(1)}, pred[128,16]{0,1:T(8,128)(4,1)}, u32[]{:S(2)}) copy-start(pred[128,16]{0,1:T(8,128)(4,1)} %get-tuple-element.87) | copy-start | bytes 6148
  329.5 141.5 %copy-start.59 = (f32[128]{0:T(128)S(1)}, f32[128]{0:T(128)}, u32[]{:S(2)}) copy-start(f32[128]{0:T(128)} %copy-done.58) | copy-start | bytes 1540
  329.5 141.5 %copy-start.63 = (f32[128]{0:T(128)S(1)}, f32[128]{0:T(128)}, u32[]{:S(2)}) copy-start(f32[128]{0:T(128)} %copy-done.62) | copy-start | bytes 1540
  329.5 141.6 %copy-start.61 = (f32[128]{0:T(128)S(1)}, f32[128]{0:T(128)}, u32[]{:S(2)}) copy-start(f32[128]{0:T(128)} %copy-done.60) | copy-start | bytes 1540
  329.5 143.5 %copy-start.15 = (bf16[1,128,2048]{2,1,0:T(8,128)(2,1)S(1)}, bf16[1,128,2048]{2,1,0:T(8,128)(2,1)}, u32[]{:S(2)}) copy-start(bf16[1,128,2048]{2,1,0:T(8,128)(2,1)} %param.18) | copy-start | bytes 1572868
  474.2 40.7 %copy-start.36 = (bf16[512,512]{0,1:T(8,128)(2,1)S(1)}, bf16[512,512]{0,1:T(8,128)(2,1)}, u32[]{:S(2)}) copy-start(bf16[512,512]{0,1:T(8,128)(2,1)} %copy-done.35) | copy-start | bytes 1572868
  474.2 40.7 %copy-start.47 = (f32[4,512]{1,0:T(4,128)S(1)}, f32[4,512]{1,0:T(4,128)}, u32[]{:S(2)}) copy-start(f32[4,512]{1,0:T(4,128)} %copy-done.46) | copy-start | bytes 24580
  511.2 3.7 copy-start.3
  520.1 10.8 %copy-start.10 = (f32[512,512]{0,1:T(8,128)S(1)}, f32[512,512]{0,1:T(8,128)}, u32[]{:S(2)}) copy-start(f32[512,512]{0,1:T(8,128)} %copy-done.8) | copy-start | bytes 3145732
  528.2 4.1 copy-start.28
  534.2 2.3 copy-start.38
  538.6 24.0 %copy-start.5 = (bf16[1,128,2048]{2,1,0:T(8,128)(2,1)S(1)}, bf16[1,128,2048]{2,1,0:T(8,128)(2,1)}, u32[]{:S(2)}) copy-start(bf16[1,128,2048]{2,1,0:T(8,128)(2,1)} %param.17) | copy-start | bytes 1572868
  538.6 24.0 %copy-start.43 = (f32[2048]{0:T(1024)S(1)}, f32[2048]{0:T(1024)}, u32[]{:S(2)}) copy-start(f32[2048]{0:T(1024)} %param.25) | copy-start | bytes 24580
  538.6 24.0 %copy-start.65 = (f32[128]{0:T(128)S(1)}, f32[128]{0:T(128)}, u32[]{:S(2)}) copy-start(f32[128]{0:T(128)} %copy-done.64) | copy-start | bytes 1540
  541.8 22.5 %copy-start.14 = (bf16[128,2048]{1,0:T(8,128)(2,1)S(1)}, bf16[128,2048]{1,0:T(8,128)(2,1)}, u32[]{:S(2)}) copy-start(bf16[128,2048]{1,0:T(8,128)(2,1)} %copy-done.13) | copy-start | bytes 1572868
  564.8 4.5 copy-start.24
  564.8 4.5 copy-start.40
  564.8 4.5 copy-start.71
  575.7 126.4 %copy-start.22 = (bf16[4096,512]{0,1:T(8,128)(2,1)S(1)}, bf16[4096,512]{0,1:T(8,128)(2,1)}, u32[]{:S(2)}) copy-start(bf16[4096,512]{0,1:T(8,128)(2,1)} %get-tuple-element.44) | copy-start | bytes 12582916
  723.1 9.4 %copy-start.21 = (bf16[4096,512]{0,1:T(8,128)(2,1)S(1)}, bf16[4096,512]{0,1:T(8,128)(2,1)}, u32[]{:S(2)}) copy-start(bf16[4096,512]{0,1:T(8,128)(2,1)} %get-tuple-element.45) | copy-start | bytes 12582916
  723.1 25.4 %slice-start = ((s8[6291456]{0:T(1024)(128)(4,1)}), s8[4194304]{0:T(1024)(128)(4,1)S(1)}, s32[]{:S(2)}) async-start(s8[6291456]{0:T(1024)(128)(4,1)} %bitcast.231), calls=%async_computation.5 | async-start | bytes 8388608
  732.5 8.6 %copy-start.31 = (f32[1,2048,256]{2,1,0:T(8,128)S(1)}, f32[1,2048,256]{2,1,0:T(8,128)}, u32[]{:S(2)}) copy-start(f32[1,2048,256]{2,1,0:T(8,128)} %convolution_bitcast_fusion) | copy-start | bytes 6291460
  732.5 8.6 %copy-start.32 = (f32[1,2048,256]{2,1,0:T(8,128)S(1)}, f32[1,2048,256]{2,1,0:T(8,128)}, u32[]{:S(2)}) copy-start(f32[1,2048,256]{2,1,0:T(8,128)} %convolution_bitcast_fusion.1) | copy-start | bytes 6291460
  732.6 16.0 %slice-start.1 = ((s8[6291456]{0:T(1024)(128)(4,1)}), s8[2097152]{0:T(1024)(128)(4,1)S(1)}, s32[]{:S(2)}) async-start(s8[6291456]{0:T(1024)(128)(4,1)} %bitcast.231), calls=%async_computation.6 | async-start | bytes 4194304
  748.5 5.5 copy-start.20
  754.0 18.7 %copy-start.1 = (bf16[2,256,2048]{2,1,0:T(8,128)(2,1)S(1)}, bf16[2,256,2048]{2,1,0:T(8,128)(2,1)}, u32[]{:S(2)}) copy-start(bf16[2,256,2048]{2,1,0:T(8,128)(2,1)} %param.30) | copy-start | bytes 6291460
  (30 other events, 45.5 us)
Sparse Core Ops, SparseCore 0:
  11.0 146.1 all-gather.2
  277.2 230.8 reduce-scatter.2
  721.9 47.1 reduce-scatter.4

commit v3 on v2

--- a/solution.py
+++ b/solution.py
@@ -189,21 +189,43 @@
     return [next(sequence) for _ in range(count)]
 
 
-def gather_kernel(nz, own, own_small, out, out_small, own_sem, zr, zs, xr, xs, yr, ys, dr, xf, yf, pr, ps, *small_sems):
+NT = (((1,), (1,)), ((), ()))
+TN = (((0,), (0,)), ((), ()))
+
+
+def above(a, b):
+    return (a - b + 63) // 64
+
+
+def near_first(at, nz, s):
+    right = above(2 * at.z, nz - 1)
+    alternate = at.z - right * (2 * at.z - (nz - 1))
+    turn = at.z + (s + 1) // 2 * (1 - 2 * (s % 2))
+    rest = s + right * (nz - 1 - 2 * s)
+    return turn + above(s, 2 * alternate) * (rest - turn)
+
+
+def gather_act_kernel(nz, own, own_small, w_gate, w_up, w_down, grads, out, acts, terms, gates, xb, cb, ab, load_x, load_c, store, own_sem, zr, zs, xr, xs, yr, ys, dr, xf, yf, pr, ps, *small_sems):
     at = Place()
-    half = own.shape[0] // 2
+    rows, width = own.shape
+    experts = own_small.shape[0]
+    local, _, hidden = w_gate.shape
+    half = rows // 2
     halves = (pl.ds(0, half), pl.ds(half, half))
-    small = SmallGather(at, nz, own_small, out_small, small_sems)
+    small = SmallGather(at, nz, own_small, gates, small_sems)
     greet([(at.fx, at.e), (at.fy, at.e), (at.f, at.pe)], (at, nz))
     keep = pltpu.make_async_copy(own, out.at[at.f, at.e], own_sem)
     keep.start()
     small.stage(0)
-
-    def up(z, slot):
-        return send(slot, slot, zs.at[0, z], zr.at[z], at.f, at.e + 2)
-
-    def down(z, slot):
-        return send(slot, slot, zs.at[1, z], zr.at[z], at.f, at.e - 2)
+    places = (at.f, at.fx, at.fy, at.fd)
+
+    def up(z):
+        ref = out.at[at.f, 2 * z + at.c]
+        return send(ref, ref, zs.at[0, z], zr.at[z], at.f, at.e + 2)
+
+    def down(z):
+        ref = out.at[at.f, 2 * z + at.c]
+        return send(ref, ref, zs.at[1, z], zr.at[z], at.f, at.e - 2)
 
     def to_x(z, h):
         ref = out.at[at.f, 2 * z + at.c, halves[h]]
@@ -225,28 +247,10 @@
         ref = out.at[f, 2 * z + at.c, halves[h]]
         return send(ref, ref, ps.at[f, z, h], pr.at[f, z, h], at.f, at.pe)
 
-    def order(i):
-        return at.z + (i + 1) // 2 * (1 - 2 * (i % 2))
-
-    def on_line(i, run):
-        z = order(i)
-        pl.when((z >= 0) & (z < nz))(lambda: run(z))
-
     def line_step(z):
-        slot = out.at[at.f, 2 * z + at.c]
-
-        @pl.when(z != at.z)
-        def _():
-            up(z, slot).wait_recv()
-
-        @pl.when((z <= at.z) & (at.z < nz - 1))
-        def _():
-            up(z, slot).start()
-
-        @pl.when((z >= at.z) & (at.z > 0))
-        def _():
-            down(z, slot).start()
-
+        pl.when(z != at.z)(lambda: up(z).wait_recv())
+        pl.when((z <= at.z) & (at.z < nz - 1))(lambda: up(z).start())
+        pl.when((z >= at.z) & (at.z > 0))(lambda: down(z).start())
         to_x(z, 0).start()
         to_y(z, 1).start()
         to_x(z, 1).start()
@@ -272,30 +276,103 @@
         y_on(z).wait_recv()
         to_p(at.fd, z, 1).start()
 
+    def loads(q, z):
+        pair = pl.ds(2 * z, 2)
+        return (
+            pltpu.make_async_copy(out.at[places[q], pair], xb.at[q], load_x.at[q]),
+            pltpu.make_async_copy(grads.at[places[q], pair], cb.at[q], load_c.at[q]),
+        )
+
+    def stores(q, z):
+        pair = pl.ds(2 * z, 2)
+        return [
+            pltpu.make_async_copy(ab.at[q, k], acts.at[k, places[q], pair], store.at[q, k])
+            for k in range(3)
+        ]
+
+    def fetch(q, z):
+        for h in range(2):
+            to_p(places[q], z, h).wait_recv()
+        for copy in loads(q, z):
+            copy.start()
+
+    first = at.e * local
+    expert_row = lax.broadcasted_iota(jnp.int32, (experts, hidden), 0)
+
+    def work(q, z):
+        for copy in loads(q, z):
+            copy.wait()
+        f = places[q]
+        sums = [None, None]
+        x = xb[q].reshape(2 * rows, width)
+        c = cb[q].reshape(2 * rows, width)
+        for j in range(local):
+            pick = (expert_row == first + j).astype(jnp.float32)
+            cols = pl.ds(j * hidden, hidden)
+            g = jnp.dot(x, w_gate[j], preferred_element_type=jnp.float32)
+            u = jnp.dot(x, w_up[j], preferred_element_type=jnp.float32)
+            dh = lax.dot_general(c, w_down[j], NT, preferred_element_type=jnp.float32)
+            sig = 1.0 / (1.0 + jnp.exp(-g))
+            silu = g * sig
+            h = silu * u
+            prod = h * dh
+            for t in range(2):
+                part = slice(t * rows, (t + 1) * rows)
+                gate = lax.dot_general(
+                    gates[t, f, z], pick, TN, precision=precise, preferred_element_type=jnp.float32
+                )
+                mine = lax.dot_general(
+                    pick, prod[part], NT, precision=precise, preferred_element_type=jnp.float32
+                )
+                sums[t] = mine if sums[t] is None else sums[t] + mine
+                d = dh[part] * gate
+                ab[q, 0, t, :, cols] = (
+                    d * u[part] * sig[part] * (1.0 + g[part] * (1.0 - sig[part]))
+                ).astype(jnp.bfloat16)
+                ab[q, 1, t, :, cols] = (d * silu[part]).astype(jnp.bfloat16)
+                ab[q, 2, t, :, cols] = (h[part] * gate).astype(jnp.bfloat16)
+        for t in range(2):
+            terms[t, f, z] = sums[t]
+        for copy in stores(q, z):
+            copy.start()
+
     keep.wait()
-    steps = 2 * nz - 1
-
-    def body(i, carry):
-        pl.when(i < steps)(lambda: on_line(i, line_step))
-        pl.when((i >= 1) & (i < steps + 1))(lambda: on_line(i - 1, plane_step))
-        pl.when(i >= 2)(lambda: on_line(i - 2, diag_step))
+
+    def body(s, carry):
+        def at_step(lag, run):
+            pl.when((s >= lag) & (s < nz + lag))(lambda: run(near_first(at, nz, s - lag)))
+
+        def free(q, lag):
+            def run(z):
+                for copy in stores(q, z):
+                    copy.wait()
+
+            at_step(lag + 1, run)
+
+        at_step(0, line_step)
         for k in range(1, 5):
-            pl.when(i == k)(functools.partial(small.stage, k))
+            pl.when(s == 0)(functools.partial(small.stage, k))
+        at_step(1, lambda z: fetch(0, z))
+        free(3, 4)
+        at_step(4, lambda z: work(3, z))
+        at_step(1, plane_step)
+        at_step(2, lambda z: fetch(1, z))
+        free(0, 1)
+        at_step(1, lambda z: work(0, z))
+        at_step(2, diag_step)
+        at_step(2, lambda z: fetch(2, z))
+        free(1, 2)
+        at_step(2, lambda z: work(1, z))
+        at_step(3, lambda z: fetch(3, z))
+        free(2, 2)
+        at_step(2, lambda z: work(2, z))
         return carry
 
-    lax.fori_loop(0, steps + 2, body, 0)
+    lax.fori_loop(0, nz + 5, body, 0)
 
     def finish(z, carry):
-        slot = out.at[at.f, 2 * z + at.c]
-
-        @pl.when((z <= at.z) & (at.z < nz - 1))
-        def _():
-            up(z, slot).wait_send()
-
-        @pl.when((z >= at.z) & (at.z > 0))
-        def _():
-            down(z, slot).wait_send()
-
+        pl.when((z <= at.z) & (at.z < nz - 1))(lambda: up(z).wait_send())
+        pl.when((z >= at.z) & (at.z > 0))(lambda: down(z).wait_send())
         for h in range(2):
             to_x(z, h).wait_send()
             to_y(z, h).wait_send()
@@ -304,31 +381,42 @@
         for f in range(4):
             for h in range(2):
                 to_p(f, z, h).wait_send()
-                to_p(f, z, h).wait_recv()
         return carry
 
     lax.fori_loop(0, nz, finish, 0)
 
 
-def gather_all(rows, small, nz, cid):
+def gather_act(rows, small, w_gate, w_up, w_down, grads, nz, cid):
     r, c = rows.shape
+    local, _, hidden = w_gate.shape
+    wide = local * hidden
+    hbm, vmem = pl.BlockSpec(memory_space=pl.ANY), pl.BlockSpec(memory_space=pltpu.VMEM)
+    bf16 = jnp.bfloat16
     return pl.pallas_call(
-        functools.partial(gather_kernel, nz),
+        functools.partial(gather_act_kernel, nz),
         out_shape=(
-            jax.ShapeDtypeStruct((4, 2 * nz, r, c), rows.dtype),
+            jax.ShapeDtypeStruct((4, 2 * nz, r, c), bf16),
+            jax.ShapeDtypeStruct((3, 4, 2 * nz, r, wide), bf16),
             jax.ShapeDtypeStruct((2, 4, nz, *small.shape), jnp.float32),
         ),
-        in_specs=[pl.BlockSpec(memory_space=pltpu.VMEM)] * 2,
-        out_specs=(pl.BlockSpec(memory_space=pl.ANY), pl.BlockSpec(memory_space=pltpu.VMEM)),
+        in_specs=[vmem] * 5 + [hbm],
+        out_specs=(hbm, hbm, vmem),
         scratch_shapes=[
+            pltpu.VMEM((2, 4, nz, *small.shape), jnp.float32),
+            pltpu.VMEM((4, 2, r, c), bf16),
+            pltpu.VMEM((4, 2, r, c), bf16),
+            pltpu.VMEM((4, 3, 2, r, wide), bf16),
+            DMA((4,)), DMA((4,)), DMA((4, 3)),
             DMA(()), DMA((nz,)), DMA((2, nz)), DMA((2, nz)), DMA((2, nz)), DMA((2, nz)), DMA((2, nz)),
             DMA((2, nz)), DMA((nz,)), DMA((nz,)), DMA((4, nz, 2)), DMA((4, nz, 2)),
             *SmallGather.sems(nz),
         ],
-        compiler_params=pltpu.CompilerParams(collective_id=cid, has_side_effects=True),
+        compiler_params=pltpu.CompilerParams(
+            collective_id=cid, has_side_effects=True, vmem_limit_bytes=50 << 20
+        ),
         cost_estimate=pl.CostEstimate(flops=0, bytes_accessed=240 << 20, transcendentals=0),
-        name="gather_all",
-    )(rows, small)
+        name="gather_act",
+    )(rows, small, w_gate, w_up, w_down, grads)
 
 
 def add_rows(dst, dst_rows, parts):
@@ -346,22 +434,14 @@
     lax.fori_loop(0, count // 16, body, 0)
 
 
-def scatter_kernel(nz, part, part_small, out, out_small, acc, pb, xh, yh, xf, yf, zu, zd, ls, pr, ps, xhs, xhr, yhs, yhr, xs, xr, ys, yr, us, ur, ds_, dr, *small_refs):
-    at = Place()
+def scatter_plan(at, nz, part, out, refs):
+    acc, pb, xh, yh, xf, yf, zu, zd, ls, pr, ps, xhs, xhr, yhs, yhr, xs, xr, ys, yr, us, ur, ds_, dr = refs
     rows = out.shape[0]
     half = rows // 2
     lo, hi = pl.ds(0, half), pl.ds(half, half)
-    small = SmallScatter(at, nz, part_small, out_small, small_refs[:4], small_refs[4:])
-    greet([(at.fx, at.e), (at.fy, at.e), (at.f, at.pe)], (at, nz))
-    steps = 2 * nz - 1
-    small.stage(0)
-
-    def order(i):
-        return at.z + (nz - 1 - i // 2) * (2 * (i % 2) - 1)
-
-    def on_line(i, run):
-        z = order(i)
-        pl.when((z >= 0) & (z < nz))(lambda: run(z))
+
+    def place(s):
+        return near_first(at, nz, nz - 1 - s)
 
     def load(f, z):
         return pltpu.make_async_copy(part.at[f, 2 * z + at.c], acc.at[f, z], ls.at[f, z])
@@ -369,17 +449,12 @@
     def to_p(f, z):
         return send(part.at[f, 2 * z + 1 - at.c], pb.at[f, z], ps.at[f, z], pr.at[f, z], at.f, at.pe)
 
-    def start_step(z):
+    def start_step(s):
+        z = place(s)
         for f in (at.fd, at.fx, at.fy, at.f):
             load(f, z).start()
             to_p(f, z).start()
 
-    def start(i, carry):
-        on_line(i, start_step)
-        return carry
-
-    lax.fori_loop(0, steps, start, 0)
-
     def half_x(z):
         return send(acc.at[at.fd, z, lo], xh.at[z], xhs.at[z], xhr.at[z], at.fx, at.e)
 
@@ -398,7 +473,8 @@
     def go_down(z):
         return send(acc.at[at.f, z], zd.at[z], ds_.at[z], dr.at[z], at.f, at.e - 2)
 
-    def diag_step(z):
+    def diag_step(s):
+        z = place(s)
         load(at.fd, z).wait()
         to_p(at.fd, z).wait_recv()
         a, b = acc.at[at.fd, z], pb.at[at.fd, z]
@@ -407,7 +483,8 @@
         add_rows(a, (half, half), [(a, half), (b, half)])
         half_y(z).start()
 
-    def plane_step(z):
+    def plane_step(s):
+        z = place(s)
         load(at.fx, z).wait()
         to_p(at.fx, z).wait_recv()
         a, b = acc.at[at.fx, z], pb.at[at.fx, z]
@@ -423,7 +500,8 @@
         add_rows(a, (half, half), [(a, half), (b, half)])
         full_y(z).start()
 
-    def line_step(z):
+    def line_step(s):
+        z = place(s)
         load(at.f, z).wait()
         to_p(at.f, z).wait_recv()
         full_x(z).wait_recv()
@@ -465,36 +543,63 @@
                 go_down(z).wait_recv()
                 add_rows(out, (0, rows), [(out, 0), (zd.at[z], 0)])
 
-    def body(i, carry):
-        pl.when(i < steps)(lambda: on_line(i, diag_step))
-        pl.when((i >= 1) & (i < steps + 1))(lambda: on_line(i - 1, plane_step))
-        pl.when(i >= 2)(lambda: on_line(i - 2, line_step))
+    def finish():
+        def body(z, carry):
+            for f in range(4):
+                to_p(f, z).wait_send()
+            half_x(z).wait_send()
+            half_y(z).wait_send()
+            full_x(z).wait_send()
+            full_y(z).wait_send()
+            pl.when(z > at.z)(lambda: go_up(z).wait_send())
+            pl.when(z < at.z)(lambda: go_down(z).wait_send())
+            return carry
+
+        lax.fori_loop(0, nz, body, 0)
+
+    return start_step, diag_step, plane_step, line_step, finish
+
+
+def scatter_scratch(parts, nz):
+    _, _, r, c = parts.shape
+
+    def buf(*n):
+        return pltpu.VMEM((*n, c), parts.dtype)
+
+    return [
+        buf(4, nz, r), buf(4, nz, r), buf(nz, r // 2), buf(nz, r // 2),
+        buf(nz, r), buf(nz, r), buf(nz, r), buf(nz, r),
+        DMA((4, nz)), DMA((4, nz)), DMA((4, nz)),
+        *[DMA((nz,))] * 12,
+    ]
+
+
+def scatter_kernel(nz, part, part_small, out, out_small, *refs):
+    at = Place()
+    refs = iter(refs)
+    start, diag, plane, line, finish = scatter_plan(at, nz, part, out, take(refs, 23))
+    small = SmallScatter(at, nz, part_small, out_small, take(refs, 4), take(refs, 4))
+    greet([(at.fx, at.e), (at.fy, at.e), (at.f, at.pe)], (at, nz))
+    small.stage(0)
+    for s in range(nz):
+        start(s)
+
+    def body(s, carry):
+        pl.when(s < nz)(lambda: diag(s))
+        pl.when((s >= 1) & (s < nz + 1))(lambda: plane(s - 1))
+        pl.when(s >= 2)(lambda: line(s - 2))
         for k in range(1, 5):
-            pl.when(i == k)(functools.partial(small.stage, k))
+            pl.when(s == k)(functools.partial(small.stage, k))
         return carry
 
-    lax.fori_loop(0, steps + 2, body, 0)
-
-    def finish(z, carry):
-        for f in range(4):
-            to_p(f, z).wait_send()
-        half_x(z).wait_send()
-        half_y(z).wait_send()
-        full_x(z).wait_send()
-        full_y(z).wait_send()
-        pl.when(z > at.z)(lambda: go_up(z).wait_send())
-        pl.when(z < at.z)(lambda: go_down(z).wait_send())
-        return carry
-
-    lax.fori_loop(0, nz, finish, 0)
+    lax.fori_loop(0, nz + 2, body, 0)
+    for k in range(nz + 2, 5):
+        small.stage(k)
+    finish()
 
 
 def scatter_all(parts, small, nz, cid):
     _, _, r, c = parts.shape
-
-    def buf(*n):
-        return pltpu.VMEM((*n, c), parts.dtype)
-
     return pl.pallas_call(
         functools.partial(scatter_kernel, nz),
         out_shape=(
@@ -504,10 +609,7 @@
         in_specs=[pl.BlockSpec(memory_space=pl.ANY), pl.BlockSpec(memory_space=pltpu.VMEM)],
         out_specs=(pl.BlockSpec(memory_space=pltpu.VMEM),) * 2,
         scratch_shapes=[
-            buf(4, nz, r), buf(4, nz, r), buf(nz, r // 2), buf(nz, r // 2),
-            buf(nz, r), buf(nz, r), buf(nz, r), buf(nz, r),
-            DMA((4, nz)), DMA((4, nz)), DMA((4, nz)),
-            *[DMA((nz,))] * 12,
+            *scatter_scratch(parts, nz),
             *SmallScatter.scratch(nz, small.shape[-2:]),
             *SmallScatter.sems(nz),
         ],
@@ -662,11 +764,109 @@
     )(flat).reshape(values.shape)
 
 
+class product_plan:
+    def __init__(self, inputs, outs, refs):
+        self.rows, self.acts, self.grads = inputs
+        self.outs = outs
+        self.wide_acc, self.down_acc, self.xw, self.aw, self.load_sem, self.store_sem = refs
+        self.units = self.rows.shape[0]
+        self.local = self.outs[0].shape[0]
+        self.per_pass = self.units // 2
+        self.steps = self.per_pass * (self.local + 1)
+
+    def loads(self, i, k, p):
+        u = (i - p * self.per_pass) * 2 + k
+        hidden = self.outs[0].shape[2]
+        sem = self.load_sem.at[k]
+        if p == self.local:
+            return [
+                pltpu.make_async_copy(self.grads.at[u], self.xw.at[k], sem.at[0]),
+                pltpu.make_async_copy(self.acts.at[2, u], self.aw.at[k], sem.at[1]),
+            ]
+        cols = pl.ds(p * hidden, hidden)
+        return [
+            pltpu.make_async_copy(self.rows.at[u], self.xw.at[k], sem.at[0]),
+            pltpu.make_async_copy(self.acts.at[0, u, :, cols], self.aw.at[k, :, pl.ds(0, hidden)], sem.at[1]),
+            pltpu.make_async_copy(
+                self.acts.at[1, u, :, cols], self.aw.at[k, :, pl.ds(hidden, hidden)], sem.at[2]
+            ),
+        ]
+
+    def on_pass(self, i, run):
+        for p in range(self.local + 1):
+            pl.when((i >= p * self.per_pass) & (i < (p + 1) * self.per_pass))(functools.partial(run, p))
+
+    def start(self):
+        for k in range(2):
+            for copy in self.loads(0, k, 0):
+                copy.start()
+
+        for acc in (*[self.wide_acc.at[p] for p in range(self.local)], self.down_acc):
+            def body(r, carry, acc=acc):
+                acc[pl.ds(r * 8, 8), :] = jnp.zeros((8, acc.shape[1]), jnp.float32)
+                return carry
+
+            lax.fori_loop(0, acc.shape[0] // 8, body, 0)
+
+    def step(self, i):
+        tile = 512
+
+        def run(p):
+            for k in range(2):
+                for copy in self.loads(i, k, p):
+                    copy.wait()
+                a = self.aw[k]
+                for t in range(self.xw.shape[2] // tile):
+                    cols = pl.ds(t * tile, tile)
+                    x = self.xw[k, :, cols]
+                    if p == self.local:
+                        self.down_acc[:, cols] += lax.dot_general(
+                            a, x, TN, preferred_element_type=jnp.float32
+                        )
+                    else:
+                        self.wide_acc[p, cols, :] += lax.dot_general(
+                            x, a, TN, preferred_element_type=jnp.float32
+                        )
+
+                def more(q, k=k):
+                    for copy in self.loads(i + 1, k, q):
+                        copy.start()
+
+                self.on_pass(i + 1, more)
+
+            @pl.when(i == (p + 1) * self.per_pass - 1)
+            def _():
+                for copy in self.stores(p):
+                    copy.start()
+
+        self.on_pass(i, run)
+
+    def stores(self, p):
+        hidden = self.outs[0].shape[2]
+        if p == self.local:
+            return [pltpu.make_async_copy(self.down_acc, self.outs[2], self.store_sem.at[p, 0])]
+        acc = self.wide_acc.at[p]
+        return [
+            pltpu.make_async_copy(
+                acc.at[:, pl.ds(k * hidden, hidden)], self.outs[k].at[p], self.store_sem.at[p, k]
+            )
+            for k in range(2)
+        ]
+
+    def finish(self):
+        for p in range(self.local + 1):
+            for copy in self.stores(p):
+                copy.wait()
+
+
 def line_sum_kernel(nz, counts, *refs):
     at = Place()
     refs = iter(refs)
     n = len(counts)
-    parts, part_small, outs, out_small = take(refs, n), next(refs), take(refs, n), next(refs)
+    parts, part_small, rows_part, inputs = take(refs, n), next(refs), next(refs), take(refs, 3)
+    outs, out_small, rows_out, grads = take(refs, n), next(refs), next(refs), take(refs, 3)
+    begin, diag, plane, line, close = scatter_plan(at, nz, rows_part, rows_out, take(refs, 23))
+    product = product_plan(inputs, grads, take(refs, 6))
     bufs = [take(refs, 5) for _ in range(n)]
     sems = [take(refs, 12) for _ in range(n)]
     own_small = next(refs)
@@ -723,15 +923,14 @@
 
             low += count
 
-    def start(q, carry):
-        def run(it):
-            it.load().start()
-            it.to_p().start()
-
-        piece(q, run)
-        return carry
-
-    lax.fori_loop(0, total, start, 0)
+    def start(it):
+        it.load().start()
+        it.to_p().start()
+
+    piece(0, start)
+    begin(0)
+    piece(1, start)
+    product.start()
 
     def halve(it):
         it.load().wait()
@@ -814,6 +1013,12 @@
         it.res_p(z).start()
 
     def body(i, carry):
+        piece(i + 2, start)
+        s, turn = i // 5, i % 5
+        pl.when((turn == 0) & (s + 1 < nz))(lambda: begin(s + 1))
+        pl.when((turn == 0) & (s < nz))(lambda: diag(s))
+        pl.when((turn == 2) & (s < nz))(lambda: plane(s))
+        pl.when((turn == 3) & (s >= 1) & (s < nz + 1))(lambda: line(s - 1))
         piece(i, halve)
         piece(i - at.z, rise, at.z < last)
         piece(i - (last - at.z), sink, at.z > 0)
@@ -826,9 +1031,12 @@
             pl.when(i == s)(functools.partial(scatter_small.stage, s))
         for s in range(5):
             pl.when(i == 5 + s)(functools.partial(gather_small.stage, s))
+        product.step(i)
         return carry
 
-    lax.fori_loop(0, total + 2 * nz - 1, body, 0)
+    steps = max(total + 2 * nz - 1, 5 * nz + 4, product.steps)
+    lax.fori_loop(0, steps, body, 0)
+    product.finish()
 
     def finish(q, carry):
         def run(it):
@@ -849,10 +1057,13 @@
         return carry
 
     lax.fori_loop(0, total, finish, 0)
-
-
-def line_sum(parts, small, nz, cid):
+    close()
+
+
+def line_sum(parts, small, rows, inputs, local, nz, cid):
     counts = tuple(p.shape[0] for p in parts)
+    units, unit, width = inputs[0].shape
+    wide = inputs[1].shape[3]
     scratch, sems = [], []
     for p in parts:
         n, _, _, r, c = p.shape
@@ -869,19 +1080,29 @@
         out_shape=(
             *(jax.ShapeDtypeStruct(p.shape, p.dtype) for p in parts),
             jax.ShapeDtypeStruct(small.shape, jnp.float32),
+            jax.ShapeDtypeStruct(rows.shape[2:], jnp.float32),
+            jax.ShapeDtypeStruct((local, width, wide // local), jnp.float32),
+            jax.ShapeDtypeStruct((local, width, wide // local), jnp.float32),
+            jax.ShapeDtypeStruct((wide, width), jnp.float32),
         ),
-        in_specs=[hbm] * len(parts) + [vmem],
-        out_specs=(*[hbm] * len(parts), vmem),
+        in_specs=[hbm] * len(parts) + [vmem, hbm] + [hbm] * 3,
+        out_specs=(*[hbm] * len(parts), vmem, vmem, *[hbm] * 3),
         scratch_shapes=[
+            *scatter_scratch(rows, nz),
+            pltpu.VMEM((local, width, 2 * wide // local), jnp.float32),
+            pltpu.VMEM((wide, width), jnp.float32),
+            pltpu.VMEM((2, unit, width), rows.dtype),
+            pltpu.VMEM((2, unit, wide), rows.dtype),
+            DMA((2, 3)), DMA((local + 1, 2)),
             *scratch, *sems, pltpu.VMEM(small.shape[-2:], jnp.float32),
             *SmallScatter.scratch(nz, small.shape[-2:]), *SmallScatter.sems(nz), *SmallGather.sems(nz),
         ],
         compiler_params=pltpu.CompilerParams(
-            collective_id=cid, has_side_effects=True, vmem_limit_bytes=50 << 20
+            collective_id=cid, has_side_effects=True, vmem_limit_bytes=63 << 20
         ),
         cost_estimate=pl.CostEstimate(flops=0, bytes_accessed=300 << 20, transcendentals=0),
         name="line_sum",
-    )(*parts, small)
+    )(*parts, small, rows, *inputs)
 
 
 def rope_tables(seg_ids, head_dim):
@@ -1094,76 +1315,54 @@
 
     grad_all = lax.all_gather(cotangent, ("fsdp", "expert"), axis=0, tiled=True)
     nz = owners // 2
-    rows_all, kept_all = gather_all(second_rows, gate_kept.T, nz, 7)
+    grad_all = grad_all.reshape(shards, owners, tok_count, model_width)
+    rows_all, acts, terms = gather_act(
+        second_rows, gate_kept.T, w_gate, w_up, w_down, grad_all, nz, 7
+    )
     rows_all = rows_all.reshape(-1, model_width)
-    first_expert = lax.axis_index("expert") * local_experts
-    gate_here = lax.dynamic_slice_in_dim(kept_all, first_expert, local_experts, axis=3)
-    gate_here = jnp.transpose(gate_here, (1, 2, 0, 4, 3)).reshape(-1, local_experts)
-    gate_cols = jnp.repeat(gate_here, hidden_here, axis=1)
-    tokens = rows_all.shape[0]
-
+    grad_all = grad_all.reshape(-1, model_width)
+    grad_gate_in, grad_up_in, weighted = acts.reshape(3, -1, wide)
     gate_w = jnp.transpose(w_gate, (1, 0, 2)).reshape(model_width, wide)
     up_w = jnp.transpose(w_up, (1, 0, 2)).reshape(model_width, wide)
     down_w = w_down.reshape(wide, model_width)
-    grad_hid = jnp.einsum("td,hd->th", grad_all, down_w, preferred_element_type=jnp.float32)
-    gate_act = jnp.dot(rows_all, gate_w, preferred_element_type=jnp.float32)
-    up_act = jnp.dot(rows_all, up_w, preferred_element_type=jnp.float32)
-    sig_gate = jax.nn.sigmoid(gate_act)
-    silu_gate = gate_act * sig_gate
-    hidden = silu_gate * up_act
-    gate_terms = jnp.sum((hidden * grad_hid).reshape(tokens, local_experts, hidden_here), axis=2)
-    weighted = (hidden * gate_cols).astype(jnp.bfloat16)
-    grad_hid = grad_hid * gate_cols
-    grad_gate_in = (grad_hid * up_act * sig_gate * (1.0 + gate_act * (1.0 - sig_gate))).astype(
-        jnp.bfloat16
-    )
-    grad_up_in = (grad_hid * silu_gate).astype(jnp.bfloat16)
     back = (
         jnp.einsum("th,dh->td", grad_gate_in, gate_w, preferred_element_type=jnp.float32)
         + jnp.einsum("th,dh->td", grad_up_in, up_w, preferred_element_type=jnp.float32)
     ).astype(jnp.bfloat16)
-    terms = jnp.transpose(
-        gate_terms.reshape(shards, nz, 2, tok_count, local_experts), (2, 0, 1, 4, 3)
-    )
-    terms = lax.dynamic_update_slice_in_dim(
-        jnp.zeros((2, shards, nz, experts, tok_count), jnp.float32), terms, first_expert, axis=3
-    )
     back = back.reshape(shards, owners, tok_count, model_width)
     back_rows, terms = scatter_all(back, terms, nz, 8)
     grad_gate_k = terms.T * kept_mask
     forward = jnp.dot(weighted, down_w, preferred_element_type=jnp.float32).astype(jnp.bfloat16)
-    forward_rows = lax.psum_scatter(forward, "fsdp", scatter_dimension=0, tiled=True)
-    forward_rows = lax.psum_scatter(forward_rows, "expert", scatter_dimension=0, tiled=True)
-    block_output = (second_in + forward_rows.astype(jnp.float32)).astype(jnp.bfloat16)[None]
+    forward = forward.reshape(shards, owners, tok_count, model_width)
     grad_logits = gate_wts * (grad_gate_k - jnp.sum(gate_wts * grad_gate_k, axis=1, keepdims=True))
     router_grad = jnp.dot(grad_logits.T, second_rows.astype(jnp.float32), precision=precise)
     grad_second = jnp.dot(grad_logits, w_router.astype(jnp.float32).T, precision=precise)
     grad_second = grad_second + back_rows
 
-    def by_expert(left, right):
-        return jnp.dot(left.T, right, preferred_element_type=jnp.float32)
-
-    parts = [slice(j * hidden_here, (j + 1) * hidden_here) for j in range(local_experts)]
-    grad_gate_w = jnp.stack([by_expert(rows_all, grad_gate_in[:, p]) for p in parts])
-    grad_up_w = jnp.stack([by_expert(rows_all, grad_up_in[:, p]) for p in parts])
-    grad_down_w = by_expert(weighted, grad_all).reshape(local_experts, hidden_here, model_width)
-    return block_output, grad_second, router_grad, (grad_gate_w, grad_up_w, grad_down_w)
-
-
-def sum_grads(narrow, gains, head_gains, nz):
+    units = shards * nz
+    inputs = (
+        rows_all.reshape(units, -1, model_width),
+        acts.reshape(3, units, -1, wide),
+        grad_all.reshape(units, -1, model_width),
+    )
+    return forward, grad_second, router_grad, inputs
+
+
+def sum_grads(narrow, gains, head_gains, rows, inputs, local, nz):
     shards, width = lax.axis_size("fsdp"), gains.shape[1]
     mine = lax.iota(jnp.int32, shards) == lax.axis_index("fsdp")
     heads_flat = jnp.pad(head_gains.reshape(-1), (0, width - head_gains.size))
-    rows = jnp.concatenate([gains, jnp.where(mine[:, None], heads_flat[None], 0.0)], axis=0)
-    share = -(-rows.size // (2 * shards * nz * 1024)) * 8
-    small = jnp.pad(rows.reshape(-1), (0, 2 * shards * nz * share * 128 - rows.size))
+    table = jnp.concatenate([gains, jnp.where(mine[:, None], heads_flat[None], 0.0)], axis=0)
+    share = -(-table.size // (2 * shards * nz * 1024)) * 8
+    small = jnp.pad(table.reshape(-1), (0, 2 * shards * nz * share * 128 - table.size))
     small = small.reshape(2, shards, nz, share, 128)
     parts = [g.reshape(-1, 2, nz, 16, g.shape[1]) for g in narrow]
-    *sums, small = line_sum(parts, small, nz, 9)
-    small = small.reshape(-1)[: rows.size].reshape(rows.shape)
+    *sums, small, rows, gate, up, down = line_sum(parts, small, rows, inputs, local, nz, 9)
+    expert_grads = (gate, up, down.reshape(local, -1, width))
+    small = small.reshape(-1)[: table.size].reshape(table.shape)
     own = lax.dynamic_slice_in_dim(small, gains.shape[0] + lax.axis_index("fsdp"), 1, axis=0)
     head_gains = own[0, : head_gains.size].reshape(head_gains.shape)
-    return [s.reshape(g.shape) for s, g in zip(sums, narrow)], small[: gains.shape[0]], head_gains
+    return [s.reshape(g.shape) for s, g in zip(sums, narrow)], small[: gains.shape[0]], head_gains, rows, expert_grads
 
 
 def on_device(
@@ -1255,7 +1454,6 @@
         block_output, grad_second, router_grad, expert_grads = experts_by_slot(
             second_in, second_rows, cotangent[0], routes[0], capacity, w_router, w_gate, w_up, w_down
         )
-    grad_gate_w, grad_up_w, grad_down_w = expert_grads
     grad_out = cotangent[0].astype(jnp.float32)
     mlp_gain_grad = jnp.sum(grad_second * normed_two, axis=0)
     grad_normed_two = grad_second * mlp_gain
@@ -1335,7 +1533,10 @@
     gains = jnp.concatenate([attn_gain_grad[None], mlp_gain_grad[None], router_grad], axis=0)
     head_gains = jnp.stack([q_gain_grad, k_gain_grad])
     if dense:
-        narrow, gains, head_gains = sum_grads(narrow, gains, head_gains, nz)
+        narrow, gains, head_gains, forward, expert_grads = sum_grads(
+            narrow, gains, head_gains, block_output, expert_grads, w_gate.shape[0], nz
+        )
+        block_output = (second_in + forward).astype(jnp.bfloat16)[None]
     else:
         narrow = lax.psum(narrow, "expert")
         head_gains = lax.psum(head_gains, "expert")
@@ -1354,9 +1555,7 @@
         gains[0],
         gains[1],
         gains[2:].T,
-        grad_gate_w,
-        grad_up_w,
-        grad_down_w,
+        *expert_grads,
     )
 
 

time: 784 us -> 701 us (0.89)
  matrix products: 200 us -> 88.1 us
  waiting for transfers between devices: 1.55 us -> 34.7 us
  other arithmetic: 46.4 us -> 29.9 us
  local copies, waits for them, and re-layouts: 24.3 us -> 37.2 us
    dot_general x8 -> x0, matrix products: 103 us -> none  [the longest x5 51.7 us: by_expert(): return jnp.dot(left.T, right, preferred_element_type=jnp.float32)]
    pallas_call x1, Pallas kernels: 125 us -> 190 us  [line_sum(): pl.pallas_call(functools.partial(line_sum_kernel, nz, counts), out_shape=...]
    pallas_call x1, Pallas kernels: 141 us -> 77.9 us  [scatter_all(): pl.pallas_call(functools.partial(scatter_kernel, nz), out_shape=(jax.Shap...]
    all_gather x1, waiting for transfers between devices: 0.01 us -> 34 us  [experts_dense(): grad_all = lax.all_gather(cotangent, ('fsdp', 'expert'), axis=0, tiled=True)]
    pallas_call x1, Pallas kernels: 88.2 us -> 111 us  [gather_act(): pl.pallas_call(functools.partial(gather_act_kernel, nz), out_shape=(jax.S...]
    pallas_call x2, Pallas kernels: 65.2 us -> 50.8 us  [square_gather(): pl.pallas_call(square_gather_kernel, out_shape=(jax.ShapeDtypeStruct((4,...]
    pallas_call x2, Pallas kernels: 60.6 us -> 50 us  [square_scatter(): pl.pallas_call(square_scatter_kernel, out_shape=jax.ShapeDtypeStruct((r,...]
    reduce_sum x2 -> x1, other arithmetic: 11.2 us -> 1.6 us  [on_device(): jnp.mean(grad_normed_one * normed_one, axis=1, keepdims=True)]
  transfers between devices with their start and end apart: 3 -> 1, of which waited for: 1 -> 1; matrix products, arithmetic and copies ran while one was open for 28% -> 4% of each run, Pallas kernels for 63% -> 9%
where the time goes in v3:
time: 701 us; the launch traced here: 697 us
  Pallas kernels  492 us (70%)
  matrix products  88.1 us (13%)
  local copies, waits for them, and re-layouts  37.2 us (5%)
  waiting for transfers between devices  34.7 us (5%)
  other arithmetic  29.9 us (4%)
  between operations  15.1 us (2%)
    pallas_call x1, Pallas kernels, line_sum(): pl.pallas_call(functools.partial(line_sum_kernel, nz, counts), out_shape=...  190 us
    pallas_call x1, Pallas kernels, gather_act(): pl.pallas_call(functools.partial(gather_act_kernel, nz), out_shape=(jax.S...  111 us
    pallas_call x1, Pallas kernels, scatter_all(): pl.pallas_call(functools.partial(scatter_kernel, nz), out_shape=(jax.Shap...  77.9 us
    pallas_call x2, Pallas kernels, square_gather(): pl.pallas_call(square_gather_kernel, out_shape=(jax.ShapeDtypeStruct((4,...  50.8 us
    pallas_call x2, Pallas kernels, square_scatter(): pl.pallas_call(square_scatter_kernel, out_shape=jax.ShapeDtypeStruct((r,...  50 us
    all_gather x1, waiting for transfers between devices, experts_dense(): grad_all = lax.all_gather(cotangent, ('fsdp', 'expert'), axis=0, tiled=True)  34 us
    unnamed x113, local copies, waits for them, and re-layouts  22.5 us
    dot_general x1, matrix products, experts_dense(): jnp.einsum('th,dh->td', grad_up_in, up_w, preferred_element_type=jnp.floa...  20.1 us
  transfers between devices with their start and end apart: 1, of which 1 were waited for; matrix products, arithmetic and copies ran while one was open for 4% of the time, Pallas kernels for 9%

profile of v3, /device:TPU:0, one launch (start us, length us, event | category | flops | bytes accessed | tf_op | source)
XLA Modules:
  0.0 697.0 jit_solution(903204874588754856)
XLA Ops:
  7.9 1.2 fusion.18
  9.2 2.0 fusion.11.own
  11.2 1.2 tile.5.ids
  12.5 28.3 %square_gather.2 = (bf16[4,128,2048]{2,1,0:T(8,128)(2,1)}, s32[4,8,128]{2,1,0:T(8,128)}) custom-call(bf16[128,2048]{1,0:T(8,128)(2,1)} %fusion.11.own, s32[8,128]{1,0:T(8,128)} %tile.5.ids), custom_call_target="tpu_custom_call" | custom-call | bytes 62914560 | tf_op jit(solution)/shard_map/square_gather/pallas_call | solution.py:668
  40.8 3.7 multiply_reduce_fusion.7
  44.5 1.3 multiply_reduce_fusion.6
  46.4 6.2 square_sum.2
  53.7 2.0 broadcast_multiply_fusion.3
  59.8 1.5 copy-done.47
  61.4 1.3 convolution_convert_fusion.5
  62.7 1.4 convolution_convert_fusion.7
  64.5 2.6 convolution_convert_fusion.3
  67.1 29.5 %square_scatter.2 = f32[128,2048]{1,0:T(8,128)} custom-call(bf16[4,128,2048]{2,1,0:T(8,128)(2,1)} %bitcast.200), custom_call_target="tpu_custom_call" | custom-call | bytes 62914560 | tf_op jit(solution)/shard_map/square_scatter/pallas_call | solution.py:728
  96.7 2.4 copy.54
  99.1 4.0 copy.55
  104.0 34.0 %all-gather.3.cloned.1.call-done = bf16[1,4096,2048]{2,1,0:T(8,128)(2,1)} async-done(((bf16[1,128,2048]{2,1,0:T(8,128)(2,1)}), bf16[1,4096,2048]{2,1,0:T(8,128)(2,1)}) %all-gather.3.cloned.1.call-update) | async-done | bytes 16777232 | tf_op jit(solution)/shard_map/all_gather | solution.py:1316
  138.0 1.6 copy-done.3
  139.6 110.9 %gather_act.1 = (bf16[4,8,128,2048]{3,2,1,0:T(8,128)(2,1)}, bf16[3,4,8,128,512]{4,3,2,1,0:T(8,128)(2,1)}, f32[2,4,4,16,128]{4,3,2,1,0:T(8,128)S(1)}) custom-call(bf16[128,2048]{1,0:T(8,128)(2,1)S(1)} %multiply_convert_fusion.3.own, f32[16,128]{1,0:T(8,128)S(1)} %get-tuple-element.96.own_small, bf16[2,2048,256]{2,1,0:T(8,128)(2,1)S(1)} %copy-done.3, ...), custom_call_target="tpu_custom_call" | custom-call | bytes 251658240 | tf_op jit(solution)/shard_map/gather_act/pallas_call | solution.py:395
  250.6 7.9 %fusion.42 = (bf16[1,4,8,128,512]{4,3,2,1,0:T(8,128)(2,1)}, bf16[1,4,8,128,512]{4,3,2,1,0:T(8,128)(2,1)}, bf16[1,4,8,128,512]{4,3,2,1,0:T(8,128)(2,1)S(1)}) fusion(bf16[3,4,8,128,512]{4,3,2,1,0:T(8,128)(2,1)} %get-tuple-element.31), kind=kLoop, calls=%fused_computation.131 | loop fusion | bytes 25165824 | tf_op jit(solution)/shard_map/unstack | solution.py:1324
  258.5 14.7 %fusion.47 = f32[4096,2048]{1,0:T(8,128)} fusion(bf16[4096,512]{1,0:T(8,128)(2,1)S(1)} %bitcast.198, bf16[2048,512]{0,1:T(8,128)(2,1)S(1)} %bitcast.202), kind=kOutput, calls=%fused_computation.136 | convolution fusion | flops 8589934592 | bytes 39845888 | tf_op jit(solution)/shard_map/th,dh->td/dot_general | solution.py:1329
  273.2 20.1 %add_convert_fusion = bf16[4096,2048]{1,0:T(8,128)(2,1)} fusion(f32[4096,2048]{1,0:T(8,128)} %fusion.47, bf16[4096,512]{1,0:T(8,128)(2,1)} %bitcast.197, bf16[2048,512]{0,1:T(8,128)(2,1)S(1)} %bitcast.201), kind=kOutput, calls=%fused_computation | convolution fusion | flops 8606711808 | bytes 56623104 | tf_op jit(solution)/shard_map/th,dh->td/dot_general | solution.py:1330
  293.3 77.9 %scatter_all.1 = (f32[128,2048]{1,0:T(8,128)S(1)}, f32[16,128]{1,0:T(8,128)S(1)}) custom-call(bf16[4,8,128,2048]{3,2,1,0:T(8,128)(2,1)} %bitcast.187, f32[2,4,4,16,128]{4,3,2,1,0:T(8,128)S(1)} %get-tuple-element.32.part_small), custom_call_target="tpu_custom_call" | custom-call | bytes 251658240 | tf_op jit(solution)/shard_map/scatter_all/pallas_call | solution.py:603
  374.2 1.1 fusion.41.own
  375.4 22.6 %square_gather.3 = (bf16[4,128,2048]{2,1,0:T(8,128)(2,1)}, s32[4,8,128]{2,1,0:T(8,128)}) custom-call(bf16[128,2048]{1,0:T(8,128)(2,1)} %fusion.41.own, s32[8,128]{1,0:T(8,128)} %tile.5.ids), custom_call_target="tpu_custom_call" | custom-call | bytes 62914560 | tf_op jit(solution)/shard_map/square_gather/pallas_call | solution.py:668
  397.9 3.7 convolution_convert_fusion.4
  401.6 1.6 multiply_reduce_fusion
  403.3 2.2 convolution_convert_fusion.6
  405.4 2.6 convolution_convert_fusion.2
  408.0 1.3 multiply_convert_fusion
  413.7 5.9 square_sum.3
  420.4 1.6 multiply_convert_fusion.1
  422.0 3.1 fusion.49
  425.3 1.7 fusion.48
  427.1 6.4 convolution_convert_fusion.1
  433.5 2.6 add_convert_fusion.1
  436.1 20.5 %square_scatter.3 = f32[128,2048]{1,0:T(8,128)} custom-call(bf16[4,128,2048]{2,1,0:T(8,128)(2,1)} %bitcast.192), custom_call_target="tpu_custom_call" | custom-call | bytes 62914560 | tf_op jit(solution)/shard_map/square_scatter/pallas_call | solution.py:728
  456.6 1.6 fusion.13
  459.1 14.6 %convolution_convert_fusion = bf16[4096,2048]{1,0:T(8,128)(2,1)} fusion(bf16[4096,512]{1,0:T(8,128)(2,1)} %bitcast.196, bf16[512,2048]{1,0:T(8,128)(2,1)S(1)} %bitcast.203), kind=kOutput, calls=%fused_computation.1 | convolution fusion | flops 8598323200 | bytes 23068672 | tf_op jit(solution)/shard_map/dot_general | solution.py:1335
  473.7 190.2 %line_sum.1 = (bf16[16,2,4,16,1536]{4,3,2,1,0:T(8,128)(2,1)}, bf16[4,2,4,16,2048]{4,3,2,1,0:T(8,128)(2,1)}, f32[2,4,4,16,128]{4,3,2,1,0:T(8,128)}, f32[128,2048]...) custom-call(bf16[16,2,4,16,1536]{4,3,2,1,0:T(8,128)(2,1)} %bitcast.193, ...), custom_call_target="tpu_custom_call" | custom-call | bytes 314572800 | tf_op jit(solution)/shard_map/line_sum/pallas_call | solution.py:1078
  665.6 8.3 %slice_convert_fusion = (f32[2048,512]{1,0:T(8,128)}, f32[2048,512]{1,0:T(8,128)}, f32[2048,512]{1,0:T(8,128)}) fusion(bf16[2048,1536]{1,0:T(8,128)(2,1)} %bitcast.194), kind=kLoop, calls=%fused_computation.14 | loop fusion | flops 3145728 | bytes 18874368 | tf_op jit(solution)/shard_map/convert_element_type | solution.py:1545
  674.0 2.8 bitcast_convert_fusion
  676.8 1.5 fusion.45
  678.3 1.7 fusion.17
  680.6 2.1 copy.76
  682.7 1.6 copy-done.23
  684.3 2.1 copy.77
  686.4 1.6 copy-done.22
  688.0 2.0 copy.78
  (157 shorter events, 19.3 us)
Async XLA Ops:
  7.2 96.4 %copy-start = (bf16[2048,16]{0,1:T(8,128)(2,1)S(1)}, bf16[2048,16]{0,1:T(8,128)(2,1)}, u32[]{:S(2)}) copy-start(bf16[2048,16]{0,1:T(8,128)(2,1)} %param.27) | copy-start | bytes 196612
  7.2 130.8 %all-gather.3.cloned.1.call-start = ((), (), s32[]{:S(2)}) async-start(), calls=%async_computation | async-start | bytes 17301504 | tf_op jit(solution)/shard_map/all_gather | solution.py:1316
  40.7 3.7 copy-start.30
  40.7 3.7 copy-start.46
  44.5 12.2 %copy-start.12 = (f32[512,512]{0,1:T(8,128)}, f32[512,512]{0,1:T(8,128)S(1)}, u32[]{:S(2)}) copy-start(f32[512,512]{0,1:T(8,128)S(1)} %get-tuple-element.91) | copy-start | bytes 3145732
  44.5 12.2 %copy-start.43 = (f32[512]{0:T(512)S(1)}, f32[512]{0:T(512)}, u32[]{:S(2)}) copy-start(f32[512]{0:T(512)} %param.23) | copy-start | bytes 6148
  45.8 11.4 %copy-start.15 = (f32[512,512]{0,1:T(8,128)}, f32[512,512]{0,1:T(8,128)S(1)}, u32[]{:S(2)}) copy-start(f32[512,512]{0,1:T(8,128)S(1)} %get-tuple-element.89) | copy-start | bytes 3145732
  45.8 11.1 %copy-start.42 = (f32[512]{0:T(512)S(1)}, f32[512]{0:T(512)}, u32[]{:S(2)}) copy-start(f32[512]{0:T(512)} %param.24) | copy-start | bytes 6148
  57.9 1.9 copy-start.19
  57.9 2.0 copy-start.25
  57.9 3.5 copy-start.47
  58.9 3.8 copy-start.4
  62.7 4.4 copy-start.36
  62.7 1.8 copy-start.45
  64.1 3.0 copy-start.51
  64.5 32.1 %copy-start.50 = (s32[16]{0:T(128)S(1)}, s32[16]{0:T(128)}, u32[]{:S(2)}) copy-start(s32[16]{0:T(128)} %param.33) | copy-start | bytes 196
  64.5 32.1 %copy-start.2 = (bf16[2,2048,256]{2,1,0:T(8,128)(2,1)S(1)}, bf16[2,2048,256]{2,1,0:T(8,128)(2,1)}, u32[]{:S(2)}) copy-start(bf16[2,2048,256]{2,1,0:T(8,128)(2,1)} %w_gate.1) | copy-start | bytes 6291460
  96.6 6.4 copy-start.44
  96.7 6.5 copy-start.8
  99.1 4.1 copy-start.21
  99.1 4.3 copy-start.40
  103.4 269.9 %copy-start.6 = (f32[128,2048]{1,0:T(8,128)}, f32[128,2048]{1,0:T(8,128)S(1)}, u32[]{:S(2)}) copy-start(f32[128,2048]{1,0:T(8,128)S(1)} %get-tuple-element.53) | copy-start | bytes 3145732
  250.5 7.9 %copy-start.29 = (bf16[2,2048,256]{1,2,0:T(8,128)(2,1)S(1)}, bf16[2,2048,256]{1,2,0:T(8,128)(2,1)}, u32[]{:S(2)}) copy-start(bf16[2,2048,256]{1,2,0:T(8,128)(2,1)} %copy.54) | copy-start | bytes 6291460
  258.5 14.7 %copy-start.28 = (bf16[2,2048,256]{1,2,0:T(8,128)(2,1)S(1)}, bf16[2,2048,256]{1,2,0:T(8,128)(2,1)}, u32[]{:S(2)}) copy-start(bf16[2,2048,256]{1,2,0:T(8,128)(2,1)} %copy.55) | copy-start | bytes 6291460
  371.2 3.0 copy-start.17
  375.4 26.2 %copy-start.37 = (bf16[512,512]{0,1:T(8,128)(2,1)S(1)}, bf16[512,512]{0,1:T(8,128)(2,1)}, u32[]{:S(2)}) copy-start(bf16[512,512]{0,1:T(8,128)(2,1)} %copy-done.36) | copy-start | bytes 1572868
  397.9 3.7 copy-start.5
  403.3 2.2 copy-start.49
  403.3 2.2 copy-start.52
  408.0 2.1 copy-start.33
  421.9 3.1 copy-start.14
  422.0 3.3 copy-start.31
  425.3 1.8 copy-start.38
  425.3 1.8 copy-start.48
  427.1 6.4 copy-start.26
  433.5 23.2 %copy-start.41 = (f32[2048]{0:T(1024)S(1)}, f32[2048]{0:T(1024)}, u32[]{:S(2)}) copy-start(f32[2048]{0:T(1024)} %param.25) | copy-start | bytes 24580
  436.1 22.2 %copy-start.39 = (f32[16,2048]{1,0:T(8,128)S(1)}, f32[16,2048]{1,0:T(8,128)}, u32[]{:S(2)}) copy-start(f32[16,2048]{1,0:T(8,128)} %fusion.38) | copy-start | bytes 393220
  436.1 23.0 %copy-start.32 = (bf16[2,256,2048]{2,1,0:T(8,128)(2,1)S(1)}, bf16[2,256,2048]{2,1,0:T(8,128)(2,1)}, u32[]{:S(2)}) copy-start(bf16[2,256,2048]{2,1,0:T(8,128)(2,1)} %w_down.1) | copy-start | bytes 6291460
  665.6 8.3 %copy-start.27 = (bf16[4,2,4,16,2048]{4,3,2,1,0:T(8,128)(2,1)S(1)}, bf16[4,2,4,16,2048]{4,3,2,1,0:T(8,128)(2,1)}, u32[]{:S(2)}) copy-start(bf16[4,2,4,16,2048]{4,3,2,1,0:T(8,128)(2,1)} %get-tuple-element.39) | copy-start | bytes 6291460
  673.9 4.3 copy-start.7
  673.9 4.3 copy-start.9
  673.9 4.3 copy-start.11
  673.9 4.3 copy-start.18
  673.9 4.3 copy-start.34
  676.8 3.8 copy-start.24
  680.6 3.7 copy-start.23
  684.3 3.7 copy-start.22
  684.3 5.7 copy-start.1
  (6 other events, 7.6 us)
Sparse Core Ops, SparseCore 0:
  11.0 126.9 all-gather.2

commit v4 on v3

--- a/solution.py
+++ b/solution.py
@@ -205,10 +205,9 @@
     return turn + above(s, 2 * alternate) * (rest - turn)
 
 
-def gather_act_kernel(nz, own, own_small, w_gate, w_up, w_down, grads, out, acts, terms, gates, xb, cb, ab, load_x, load_c, store, own_sem, zr, zs, xr, xs, yr, ys, dr, xf, yf, pr, ps, *small_sems):
+def gather_act_kernel(nz, own, own_small, w_gate, w_up, out, acts, gates, xb, ab, load_x, store, own_sem, zr, zs, xr, xs, yr, ys, dr, xf, yf, pr, ps, *small_sems):
     at = Place()
     rows, width = own.shape
-    experts = own_small.shape[0]
     local, _, hidden = w_gate.shape
     half = rows // 2
     halves = (pl.ds(0, half), pl.ds(half, half))
@@ -276,63 +275,29 @@
         y_on(z).wait_recv()
         to_p(at.fd, z, 1).start()
 
-    def loads(q, z):
-        pair = pl.ds(2 * z, 2)
-        return (
-            pltpu.make_async_copy(out.at[places[q], pair], xb.at[q], load_x.at[q]),
-            pltpu.make_async_copy(grads.at[places[q], pair], cb.at[q], load_c.at[q]),
-        )
+    def load(q, z):
+        return pltpu.make_async_copy(out.at[places[q], pl.ds(2 * z, 2)], xb.at[q], load_x.at[q])
 
     def stores(q, z):
-        pair = pl.ds(2 * z, 2)
         return [
-            pltpu.make_async_copy(ab.at[q, k], acts.at[k, places[q], pair], store.at[q, k])
-            for k in range(3)
+            pltpu.make_async_copy(
+                ab.at[q, k], acts.at[k, places[q], pl.ds(2 * z, 2)], store.at[q, k]
+            )
+            for k in range(2)
         ]
 
     def fetch(q, z):
         for h in range(2):
             to_p(places[q], z, h).wait_recv()
-        for copy in loads(q, z):
-            copy.start()
-
-    first = at.e * local
-    expert_row = lax.broadcasted_iota(jnp.int32, (experts, hidden), 0)
+        load(q, z).start()
 
     def work(q, z):
-        for copy in loads(q, z):
-            copy.wait()
-        f = places[q]
-        sums = [None, None]
+        load(q, z).wait()
         x = xb[q].reshape(2 * rows, width)
-        c = cb[q].reshape(2 * rows, width)
         for j in range(local):
-            pick = (expert_row == first + j).astype(jnp.float32)
-            cols = pl.ds(j * hidden, hidden)
-            g = jnp.dot(x, w_gate[j], preferred_element_type=jnp.float32)
-            u = jnp.dot(x, w_up[j], preferred_element_type=jnp.float32)
-            dh = lax.dot_general(c, w_down[j], NT, preferred_element_type=jnp.float32)
-            sig = 1.0 / (1.0 + jnp.exp(-g))
-            silu = g * sig
-            h = silu * u
-            prod = h * dh
-            for t in range(2):
-                part = slice(t * rows, (t + 1) * rows)
-                gate = lax.dot_general(
-                    gates[t, f, z], pick, TN, precision=precise, preferred_element_type=jnp.float32
-                )
-                mine = lax.dot_general(
-                    pick, prod[part], NT, precision=precise, preferred_element_type=jnp.float32
-                )
-                sums[t] = mine if sums[t] is None else sums[t] + mine
-                d = dh[part] * gate
-                ab[q, 0, t, :, cols] = (
-                    d * u[part] * sig[part] * (1.0 + g[part] * (1.0 - sig[part]))
-                ).astype(jnp.bfloat16)
-                ab[q, 1, t, :, cols] = (d * silu[part]).astype(jnp.bfloat16)
-                ab[q, 2, t, :, cols] = (h[part] * gate).astype(jnp.bfloat16)
-        for t in range(2):
-            terms[t, f, z] = sums[t]
+            for k, w in enumerate((w_gate, w_up)):
+                g = jnp.dot(x, w[j], preferred_element_type=jnp.float32)
+                ab[q, k, :, :, pl.ds(j * hidden, hidden)] = g.reshape(2, rows, hidden)
         for copy in stores(q, z):
             copy.start()
 
@@ -386,7 +351,7 @@
     lax.fori_loop(0, nz, finish, 0)
 
 
-def gather_act(rows, small, w_gate, w_up, w_down, grads, nz, cid):
+def gather_act(rows, small, w_gate, w_up, nz, cid):
     r, c = rows.shape
     local, _, hidden = w_gate.shape
     wide = local * hidden
@@ -396,17 +361,15 @@
         functools.partial(gather_act_kernel, nz),
         out_shape=(
             jax.ShapeDtypeStruct((4, 2 * nz, r, c), bf16),
-            jax.ShapeDtypeStruct((3, 4, 2 * nz, r, wide), bf16),
+            jax.ShapeDtypeStruct((2, 4, 2 * nz, r, wide), jnp.float32),
             jax.ShapeDtypeStruct((2, 4, nz, *small.shape), jnp.float32),
         ),
-        in_specs=[vmem] * 5 + [hbm],
+        in_specs=[vmem] * 4,
         out_specs=(hbm, hbm, vmem),
         scratch_shapes=[
-            pltpu.VMEM((2, 4, nz, *small.shape), jnp.float32),
             pltpu.VMEM((4, 2, r, c), bf16),
-            pltpu.VMEM((4, 2, r, c), bf16),
-            pltpu.VMEM((4, 3, 2, r, wide), bf16),
-            DMA((4,)), DMA((4,)), DMA((4, 3)),
+            pltpu.VMEM((4, 2, 2, r, wide), jnp.float32),
+            DMA((4,)), DMA((4, 2)),
             DMA(()), DMA((nz,)), DMA((2, nz)), DMA((2, nz)), DMA((2, nz)), DMA((2, nz)), DMA((2, nz)),
             DMA((2, nz)), DMA((nz,)), DMA((nz,)), DMA((4, nz, 2)), DMA((4, nz, 2)),
             *SmallGather.sems(nz),
@@ -416,7 +379,7 @@
         ),
         cost_estimate=pl.CostEstimate(flops=0, bytes_accessed=240 << 20, transcendentals=0),
         name="gather_act",
-    )(rows, small, w_gate, w_up, w_down, grads)
+    )(rows, small, w_gate, w_up)
 
 
 def add_rows(dst, dst_rows, parts):
@@ -434,7 +397,7 @@
     lax.fori_loop(0, count // 16, body, 0)
 
 
-def scatter_plan(at, nz, part, out, refs):
+def scatter_plan(at, nz, part, out, refs, staged=None):
     acc, pb, xh, yh, xf, yf, zu, zd, ls, pr, ps, xhs, xhr, yhs, yhr, xs, xr, ys, yr, us, ur, ds_, dr = refs
     rows = out.shape[0]
     half = rows // 2
@@ -446,14 +409,23 @@
     def load(f, z):
         return pltpu.make_async_copy(part.at[f, 2 * z + at.c], acc.at[f, z], ls.at[f, z])
 
-    def to_p(f, z):
-        return send(part.at[f, 2 * z + 1 - at.c], pb.at[f, z], ps.at[f, z], pr.at[f, z], at.f, at.pe)
+    fs = (at.fd, at.fx, at.fy, at.f)
+
+    def to_p(q, z):
+        f = fs[q]
+        src = staged.at[q] if staged is not None else part.at[f, 2 * z + 1 - at.c]
+        return send(src, pb.at[f, z], ps.at[f, z], pr.at[f, z], at.f, at.pe)
+
+    def ready(q, z):
+        if staged is None:
+            load(fs[q], z).wait()
+        to_p(q, z).wait_recv()
 
     def start_step(s):
         z = place(s)
-        for f in (at.fd, at.fx, at.fy, at.f):
-            load(f, z).start()
-            to_p(f, z).start()
+        for q in range(4):
+            load(fs[q], z).start()
+            to_p(q, z).start()
 
     def half_x(z):
         return send(acc.at[at.fd, z, lo], xh.at[z], xhs.at[z], xhr.at[z], at.fx, at.e)
@@ -475,8 +447,7 @@
 
     def diag_step(s):
         z = place(s)
-        load(at.fd, z).wait()
-        to_p(at.fd, z).wait_recv()
+        ready(0, z)
         a, b = acc.at[at.fd, z], pb.at[at.fd, z]
         add_rows(a, (0, half), [(a, 0), (b, 0)])
         half_x(z).start()
@@ -485,15 +456,13 @@
 
     def plane_step(s):
         z = place(s)
-        load(at.fx, z).wait()
-        to_p(at.fx, z).wait_recv()
+        ready(1, z)
         a, b = acc.at[at.fx, z], pb.at[at.fx, z]
         half_y(z).wait_recv()
         add_rows(a, (0, half), [(a, 0), (b, 0)])
         add_rows(a, (half, half), [(a, half), (b, half), (yh.at[z], 0)])
         full_x(z).start()
-        load(at.fy, z).wait()
-        to_p(at.fy, z).wait_recv()
+        ready(2, z)
         half_x(z).wait_recv()
         a, b = acc.at[at.fy, z], pb.at[at.fy, z]
         add_rows(a, (0, half), [(a, 0), (b, 0), (xh.at[z], 0)])
@@ -502,8 +471,7 @@
 
     def line_step(s):
         z = place(s)
-        load(at.f, z).wait()
-        to_p(at.f, z).wait_recv()
+        ready(3, z)
         full_x(z).wait_recv()
         full_y(z).wait_recv()
         a = acc.at[at.f, z]
@@ -545,8 +513,9 @@
 
     def finish():
         def body(z, carry):
-            for f in range(4):
-                to_p(f, z).wait_send()
+            for q in range(4):
+                if staged is None:
+                    to_p(q, z).wait_send()
             half_x(z).wait_send()
             half_y(z).wait_send()
             full_x(z).wait_send()
@@ -556,8 +525,11 @@
             return carry
 
         lax.fori_loop(0, nz, body, 0)
-
-    return start_step, diag_step, plane_step, line_step, finish
+        for q in range(4):
+            if staged is not None:
+                to_p(q, place(nz - 1)).wait_send()
+
+    return start_step, diag_step, plane_step, line_step, finish, place, to_p
 
 
 def scatter_scratch(parts, nz):
@@ -574,51 +546,215 @@
     ]
 
 
-def scatter_kernel(nz, part, part_small, out, out_small, *refs):
+def scatter_act_kernel(nz, pre, grads, gates, w_gate, w_up, w_down, out, out_small, acts, forward, *refs):
     at = Place()
     refs = iter(refs)
-    start, diag, plane, line, finish = scatter_plan(at, nz, part, out, take(refs, 23))
-    small = SmallScatter(at, nz, part_small, out_small, take(refs, 4), take(refs, 4))
+    moved = take(refs, 23)
+    acc = moved[0]
+    pb_, cb, ab, sb, fb, terms, load_sem, store_sem, forward_sem = take(refs, 9)
+    _, diag, plane, line, close, place, to_p = scatter_plan(at, nz, None, out, moved, sb)
+    small = SmallScatter(at, nz, terms, out_small, take(refs, 4), take(refs, 4))
     greet([(at.fx, at.e), (at.fy, at.e), (at.f, at.pe)], (at, nz))
-    small.stage(0)
-    for s in range(nz):
-        start(s)
+    rows, width = out.shape
+    local, _, hidden = w_gate.shape
+    experts = gates.shape[3]
+    fs = (at.fd, at.fx, at.fy, at.f)
+    cores = (at.c, 1 - at.c)
+    first = at.e * local
+    expert_row = lax.broadcasted_iota(jnp.int32, (experts, hidden), 0)
+    tile = 512
+
+    def loads(q, s):
+        z, f = place(s), fs[q]
+        copies = []
+        for h, core in enumerate(cores):
+            slot = 2 * z + core
+            for k in range(2):
+                copies.append(
+                    pltpu.make_async_copy(pre.at[k, f, slot], pb_.at[q, k, h], load_sem.at[q, h, k])
+                )
+            copies.append(pltpu.make_async_copy(grads.at[f, slot], cb.at[q, h], load_sem.at[q, h, 2]))
+        return copies
+
+    def stores(q, s):
+        z, f = place(s), fs[q]
+        return [
+            pltpu.make_async_copy(
+                ab.at[q, k, h], acts.at[k, f, 2 * z + core], store_sem.at[q, h, k]
+            )
+            for h, core in enumerate(cores)
+            for k in range(3)
+        ]
+
+    def sends(q, s):
+        z, f = place(s), fs[q]
+        return [
+            pltpu.make_async_copy(fb.at[q, h], forward.at[f, 2 * z + core], forward_sem.at[q, h])
+            for h, core in enumerate(cores)
+        ]
+
+    def act(q, s):
+        z, f = place(s), fs[q]
+        for copy in loads(q, s):
+            copy.wait()
+
+        @pl.when(s > 0)
+        def _():
+            for copy in stores(q, s - 1):
+                copy.wait()
+
+        c = cb[q].reshape(2 * rows, width)
+        sums = [None, None]
+        for j in range(local):
+            pick = (expert_row == first + j).astype(jnp.float32)
+            cols = pl.ds(j * hidden, hidden)
+            dh = lax.dot_general(c, w_down[j], NT, preferred_element_type=jnp.float32)
+            for h, core in enumerate(cores):
+                g, u = pb_[q, 0, h, :, cols], pb_[q, 1, h, :, cols]
+                d = dh[h * rows : (h + 1) * rows]
+                sig = 1.0 / (1.0 + jnp.exp(-g))
+                silu = g * sig
+                hid = silu * u
+                gate = lax.dot_general(
+                    gates[core, f, z], pick, TN, precision=precise, preferred_element_type=jnp.float32
+                )
+                mine = lax.dot_general(
+                    pick, hid * d, NT, precision=precise, preferred_element_type=jnp.float32
+                )
+                sums[h] = mine if sums[h] is None else sums[h] + mine
+                d = d * gate
+                ab[q, 0, h, :, cols] = (d * u * sig * (1.0 + g * (1.0 - sig))).astype(jnp.bfloat16)
+                ab[q, 1, h, :, cols] = (d * silu).astype(jnp.bfloat16)
+                ab[q, 2, h, :, cols] = (hid * gate).astype(jnp.bfloat16)
+        for h, core in enumerate(cores):
+            terms[core, f, z] = sums[h]
+        for copy in stores(q, s):
+            copy.start()
+
+        @pl.when(s + 1 < nz)
+        def _():
+            for copy in loads(q, s + 1):
+                copy.start()
+
+    def back(q, s):
+        z, f = place(s), fs[q]
+        pl.when(s > 0)(lambda: to_p(q, place(s - 1)).wait_send())
+        pieces = [
+            (ab[q, k].reshape(2 * rows, local * hidden)[:, j * hidden : (j + 1) * hidden], w.at[j])
+            for j in range(local)
+            for k, w in enumerate((w_gate, w_up))
+        ]
+
+        def body(t, carry):
+            cols = pl.ds(pl.multiple_of(t * tile, tile), tile)
+            total = None
+            for a, w in pieces:
+                term = lax.dot_general(a, w[cols, :], NT, preferred_element_type=jnp.float32)
+                total = term if total is None else total + term
+            total = total.astype(jnp.bfloat16)
+            acc[f, z, :, cols] = total[:rows]
+            sb[q, :, cols] = total[rows:]
+            return carry
+
+        lax.fori_loop(0, width // tile, body, 0)
+        to_p(q, z).start()
+
+    def ahead(q, s):
+        @pl.when(s > 0)
+        def _():
+            for copy in sends(q, s - 1):
+                copy.wait()
+
+        a = ab[q, 2].reshape(2 * rows, local * hidden)
+
+        def body(t, carry):
+            cols = pl.ds(pl.multiple_of(t * tile, tile), tile)
+            total = None
+            for j in range(local):
+                term = jnp.dot(
+                    a[:, j * hidden : (j + 1) * hidden],
+                    w_down[j, :, cols],
+                    preferred_element_type=jnp.float32,
+                )
+                total = term if total is None else total + term
+            total = total.astype(jnp.bfloat16)
+            fb[q, 0, :, cols] = total[:rows]
+            fb[q, 1, :, cols] = total[rows:]
+            return carry
+
+        lax.fori_loop(0, width // tile, body, 0)
+        for copy in sends(q, s):
+            copy.start()
+
+    for q in range(4):
+        for copy in loads(q, 0):
+            copy.start()
 
     def body(s, carry):
-        pl.when(s < nz)(lambda: diag(s))
-        pl.when((s >= 1) & (s < nz + 1))(lambda: plane(s - 1))
-        pl.when(s >= 2)(lambda: line(s - 2))
-        for k in range(1, 5):
-            pl.when(s == k)(functools.partial(small.stage, k))
+        @pl.when(s < nz)
+        def _():
+            last = s == nz - 1
+            for q in (0, 1):
+                act(q, s)
+                back(q, s)
+            diag(s)
+            act(2, s)
+            back(2, s)
+            act(3, s)
+            pl.when(last)(lambda: small.stage(0))
+            back(3, s)
+            for q in range(4):
+                ahead(q, s)
+            pl.when(last)(lambda: small.stage(1))
+            plane(s)
+            pl.when(last)(lambda: small.stage(2))
+
+        pl.when(s == nz)(lambda: small.stage(3))
+        pl.when(s >= 1)(lambda: line(s - 1))
         return carry
 
-    lax.fori_loop(0, nz + 2, body, 0)
-    for k in range(nz + 2, 5):
-        small.stage(k)
-    finish()
-
-
-def scatter_all(parts, small, nz, cid):
-    _, _, r, c = parts.shape
+    lax.fori_loop(0, nz + 1, body, 0)
+    small.stage(4)
+    for q in range(4):
+        for copy in stores(q, nz - 1) + sends(q, nz - 1):
+            copy.wait()
+    close()
+
+
+def scatter_act(pre, grads, gates, w_gate, w_up, w_down, nz, cid):
+    _, _, _, r, wide = pre.shape
+    c = grads.shape[3]
+    small = gates.shape[3:]
+    hbm, vmem = pl.BlockSpec(memory_space=pl.ANY), pl.BlockSpec(memory_space=pltpu.VMEM)
+    bf16 = jnp.bfloat16
     return pl.pallas_call(
-        functools.partial(scatter_kernel, nz),
+        functools.partial(scatter_act_kernel, nz),
         out_shape=(
             jax.ShapeDtypeStruct((r, c), jnp.float32),
-            jax.ShapeDtypeStruct(small.shape[-2:], jnp.float32),
+            jax.ShapeDtypeStruct(small, jnp.float32),
+            jax.ShapeDtypeStruct((3, 4, 2 * nz, r, wide), bf16),
+            jax.ShapeDtypeStruct((4, 2 * nz, r, c), bf16),
         ),
-        in_specs=[pl.BlockSpec(memory_space=pl.ANY), pl.BlockSpec(memory_space=pltpu.VMEM)],
-        out_specs=(pl.BlockSpec(memory_space=pltpu.VMEM),) * 2,
+        in_specs=[hbm, hbm, vmem, vmem, vmem, vmem],
+        out_specs=(vmem, vmem, hbm, hbm),
         scratch_shapes=[
-            *scatter_scratch(parts, nz),
-            *SmallScatter.scratch(nz, small.shape[-2:]),
+            *scatter_scratch(grads, nz),
+            pltpu.VMEM((4, 2, 2, r, wide), jnp.float32),
+            pltpu.VMEM((4, 2, r, c), bf16),
+            pltpu.VMEM((4, 3, 2, r, wide), bf16),
+            pltpu.VMEM((4, r, c), bf16),
+            pltpu.VMEM((4, 2, r, c), bf16),
+            pltpu.VMEM((2, 4, nz, *small), jnp.float32),
+            DMA((4, 2, 3)), DMA((4, 2, 3)), DMA((4, 2)),
+            *SmallScatter.scratch(nz, small),
             *SmallScatter.sems(nz),
         ],
         compiler_params=pltpu.CompilerParams(
-            collective_id=cid, has_side_effects=True, vmem_limit_bytes=50 << 20
+            collective_id=cid, has_side_effects=True, vmem_limit_bytes=62 << 20
         ),
-        cost_estimate=pl.CostEstimate(flops=0, bytes_accessed=240 << 20, transcendentals=0),
-        name="scatter_all",
-    )(parts, small)
+        cost_estimate=pl.CostEstimate(flops=0, bytes_accessed=300 << 20, transcendentals=0),
+        name="scatter_act",
+    )(pre, grads, gates, w_gate, w_up, w_down)
 
 
 def square_gather_kernel(own, ids, out, out_ids, xs, xr, ys, yr, fs, fr, js, jr):
@@ -865,7 +1001,7 @@
     n = len(counts)
     parts, part_small, rows_part, inputs = take(refs, n), next(refs), next(refs), take(refs, 3)
     outs, out_small, rows_out, grads = take(refs, n), next(refs), next(refs), take(refs, 3)
-    begin, diag, plane, line, close = scatter_plan(at, nz, rows_part, rows_out, take(refs, 23))
+    begin, diag, plane, line, close, _, _ = scatter_plan(at, nz, rows_part, rows_out, take(refs, 23))
     product = product_plan(inputs, grads, take(refs, 6))
     bufs = [take(refs, 5) for _ in range(n)]
     sems = [take(refs, 12) for _ in range(n)]
@@ -876,6 +1012,7 @@
     scatter_small.stage(0)
     total = sum(counts)
     last = nz - 1
+    lag, per = 2, 5
 
     class Piece:
         def __init__(self, k, p):
@@ -1014,19 +1151,19 @@
 
     def body(i, carry):
         piece(i + 2, start)
-        s, turn = i // 5, i % 5
+        s, turn = i // per, i % per
         pl.when((turn == 0) & (s + 1 < nz))(lambda: begin(s + 1))
         pl.when((turn == 0) & (s < nz))(lambda: diag(s))
         pl.when((turn == 2) & (s < nz))(lambda: plane(s))
         pl.when((turn == 3) & (s >= 1) & (s < nz + 1))(lambda: line(s - 1))
         piece(i, halve)
-        piece(i - at.z, rise, at.z < last)
-        piece(i - (last - at.z), sink, at.z > 0)
-        piece(i - nz, settle)
-        piece(i - nz, tell)
+        piece(i - lag * at.z, rise, at.z < last)
+        piece(i - lag * (last - at.z), sink, at.z > 0)
+        piece(i - lag * nz, settle)
+        piece(i - lag * nz, tell)
         for d in range(1, nz):
-            piece(i - nz - d, functools.partial(pass_up, z=at.z - d), at.z >= d)
-            piece(i - nz - d, functools.partial(pass_down, z=at.z + d), at.z + d <= last)
+            piece(i - lag * (nz + d), functools.partial(pass_up, z=at.z - d), at.z >= d)
+            piece(i - lag * (nz + d), functools.partial(pass_down, z=at.z + d), at.z + d <= last)
         for s in range(1, 5):
             pl.when(i == s)(functools.partial(scatter_small.stage, s))
         for s in range(5):
@@ -1034,7 +1171,7 @@
         product.step(i)
         return carry
 
-    steps = max(total + 2 * nz - 1, 5 * nz + 4, product.steps)
+    steps = max(total + lag * (2 * nz - 1), per * (nz + 1), product.steps)
     lax.fori_loop(0, steps, body, 0)
     product.finish()
 
@@ -1316,24 +1453,11 @@
     grad_all = lax.all_gather(cotangent, ("fsdp", "expert"), axis=0, tiled=True)
     nz = owners // 2
     grad_all = grad_all.reshape(shards, owners, tok_count, model_width)
-    rows_all, acts, terms = gather_act(
-        second_rows, gate_kept.T, w_gate, w_up, w_down, grad_all, nz, 7
-    )
-    rows_all = rows_all.reshape(-1, model_width)
-    grad_all = grad_all.reshape(-1, model_width)
-    grad_gate_in, grad_up_in, weighted = acts.reshape(3, -1, wide)
-    gate_w = jnp.transpose(w_gate, (1, 0, 2)).reshape(model_width, wide)
-    up_w = jnp.transpose(w_up, (1, 0, 2)).reshape(model_width, wide)
-    down_w = w_down.reshape(wide, model_width)
-    back = (
-        jnp.einsum("th,dh->td", grad_gate_in, gate_w, preferred_element_type=jnp.float32)
-        + jnp.einsum("th,dh->td", grad_up_in, up_w, preferred_element_type=jnp.float32)
-    ).astype(jnp.bfloat16)
-    back = back.reshape(shards, owners, tok_count, model_width)
-    back_rows, terms = scatter_all(back, terms, nz, 8)
+    rows_all, pre, gates = gather_act(second_rows, gate_kept.T, w_gate, w_up, nz, 7)
+    back_rows, terms, acts, forward = scatter_act(
+        pre, grad_all, gates, w_gate, w_up, w_down, nz, 8
+    )
     grad_gate_k = terms.T * kept_mask
-    forward = jnp.dot(weighted, down_w, preferred_element_type=jnp.float32).astype(jnp.bfloat16)
-    forward = forward.reshape(shards, owners, tok_count, model_width)
     grad_logits = gate_wts * (grad_gate_k - jnp.sum(gate_wts * grad_gate_k, axis=1, keepdims=True))
     router_grad = jnp.dot(grad_logits.T, second_rows.astype(jnp.float32), precision=precise)
     grad_second = jnp.dot(grad_logits, w_router.astype(jnp.float32).T, precision=precise)

time: 701 us -> 649 us (0.926)
  matrix products: 88.1 us -> 39.6 us
  waiting for transfers between devices: 34.7 us -> 0.68 us
  Pallas kernels: 492 us -> 526 us
  local copies, waits for them, and re-layouts: 37.2 us -> 23.9 us
    dot_general x3 -> x0, matrix products: 49.4 us -> none  [the longest x1 20.1 us: experts_dense(): jnp.einsum('th,dh->td', grad_up_in, up_w, preferred_element_type=jnp.floa...]
    pallas_call x1, Pallas kernels: 77.9 us -> 125 us  [scatter_act(): pl.pallas_call(functools.partial(scatter_act_kernel, nz), out_shape=(jax....]
    all_gather x1, waiting for transfers between devices: 34 us -> 0.01 us  [experts_dense(): grad_all = lax.all_gather(cotangent, ('fsdp', 'expert'), axis=0, tiled=True)]
    another operation x1 -> x0, local copies, waits for them, and re-layouts: 7.9 us -> none  [experts_dense(): grad_gate_in, grad_up_in, weighted = acts.reshape(3, -1, wide)]
    pallas_call x1, Pallas kernels: 190 us -> 183 us  [line_sum(): pl.pallas_call(functools.partial(line_sum_kernel, nz, counts), out_shape=...]
    unnamed x113 -> x161, local copies, waits for them, and re-layouts: 22.5 us -> 17.2 us
  transfers between devices with their start and end apart: 1 -> 1, of which waited for: 1 -> 0; matrix products, arithmetic and copies ran while one was open for 4% -> 4% of each run, Pallas kernels for 9% -> 27%
where the time goes in v4:
time: 649 us; the launch traced here: 639 us
  Pallas kernels  526 us (81%)
  matrix products  39.6 us (6%)
  other arithmetic  33.4 us (5%)
  local copies, waits for them, and re-layouts  23.9 us (4%)
  between operations  15.6 us (2%)
    pallas_call x1, Pallas kernels, line_sum(): pl.pallas_call(functools.partial(line_sum_kernel, nz, counts), out_shape=...  183 us
    pallas_call x1, Pallas kernels, scatter_act(): pl.pallas_call(functools.partial(scatter_act_kernel, nz), out_shape=(jax....  125 us
    pallas_call x1, Pallas kernels, gather_act(): pl.pallas_call(functools.partial(gather_act_kernel, nz), out_shape=(jax.S...  108 us
    pallas_call x2, Pallas kernels, square_gather(): pl.pallas_call(square_gather_kernel, out_shape=(jax.ShapeDtypeStruct((4,...  49.3 us
    pallas_call x2, Pallas kernels, square_scatter(): pl.pallas_call(square_scatter_kernel, out_shape=jax.ShapeDtypeStruct((r,...  48.3 us
    unnamed x161, local copies, waits for them, and re-layouts  17.2 us
  transfers between devices with their start and end apart: 1, of which 0 were waited for; matrix products, arithmetic and copies ran while one was open for 4% of the time, Pallas kernels for 27%

profile of v4, /device:TPU:0, one launch (start us, length us, event | category | flops | bytes accessed | tf_op | source)
XLA Modules:
  0.0 639.3 jit_solution(15978382740637888138)
XLA Ops:
  7.9 1.2 fusion.18
  9.7 2.0 fusion.11.own
  11.7 1.2 tile.5.ids
  13.0 28.2 %square_gather.2 = (bf16[4,128,2048]{2,1,0:T(8,128)(2,1)}, s32[4,8,128]{2,1,0:T(8,128)}) custom-call(bf16[128,2048]{1,0:T(8,128)(2,1)} %fusion.11.own, s32[8,128]{1,0:T(8,128)} %tile.5.ids), custom_call_target="tpu_custom_call" | custom-call | bytes 62914560 | tf_op jit(solution)/shard_map/square_gather/pallas_call | solution.py:804
  42.1 3.7 multiply_reduce_fusion.6
  45.8 1.3 multiply_reduce_fusion.7
  47.8 6.2 square_sum.2
  54.1 1.7 broadcast_multiply_fusion.3
  55.8 0.8 rsqrt_bitcast_fusion
  58.0 1.0 fusion
  59.0 0.9 exponential_reduce_fusion
  60.0 2.1 copy-done.72
  62.1 1.3 convolution_convert_fusion.4
  63.5 1.4 convolution_convert_fusion.6
  65.3 2.6 convolution_convert_fusion.2
  67.9 30.6 %square_scatter.2 = f32[128,2048]{1,0:T(8,128)} custom-call(bf16[4,128,2048]{2,1,0:T(8,128)(2,1)} %bitcast.177), custom_call_target="tpu_custom_call" | custom-call | bytes 62914560 | tf_op jit(solution)/shard_map/square_scatter/pallas_call | solution.py:864
  98.7 1.4 multiply_reduce_fusion.5
  101.1 108.1 %gather_act.1 = (bf16[4,8,128,2048]{3,2,1,0:T(8,128)(2,1)}, f32[2,4,8,128,512]{4,3,2,1,0:T(8,128)}, f32[2,4,4,16,128]{4,3,2,1,0:T(8,128)S(1)}) custom-call(bf16[128,2048]{1,0:T(8,128)(2,1)S(1)} %multiply_convert_fusion.3.own, f32[16,128]{1,0:T(8,128)S(1)} %get-tuple-element.97.own_small, bf16[2,2048,256]{2,1,0:T(8,128)(2,1)S(1)} %copy-done.2, ...), custom_call_target="tpu_custom_call" | custom-call | bytes 251658240 | tf_op jit(solution)/shard_map/gather_act/pallas_call | solution.py:360
  210.5 125.3 %scatter_act.1 = (f32[128,2048]{1,0:T(8,128)}, f32[16,128]{1,0:T(8,128)}, bf16[3,4,8,128,512]{4,3,2,1,0:T(8,128)(2,1)}, bf16[4,8,128,2048]{3,2,1,0:T(8,128)(2,1)}) custom-call(f32[2,4,8,128,512]{4,3,2,1,0:T(8,128)} %get-tuple-element.33.pre, bf16[4,8,128,2048]{3,2,1,0:T(8,128)(2,1)} %bitcast.164, f32[2,4,4,16,128]{4,3,2,1,0:T(8,128)} %copy-done.3, ...), custom_call_target="tpu_custom_call" | custom-call | bytes 314572800 | tf_op jit(solution)/shard_map/scatter_act/pallas_call | solution.py:730
  336.6 2.8 multiply_reduce_fusion.1
  339.4 0.9 copy-done.12
  340.4 2.2 fusion.41.own
  342.6 21.1 %square_gather.3 = (bf16[4,128,2048]{2,1,0:T(8,128)(2,1)}, s32[4,8,128]{2,1,0:T(8,128)}) custom-call(bf16[128,2048]{1,0:T(8,128)(2,1)} %fusion.41.own, s32[8,128]{1,0:T(8,128)} %tile.5.ids), custom_call_target="tpu_custom_call" | custom-call | bytes 62914560 | tf_op jit(solution)/shard_map/square_gather/pallas_call | solution.py:804
  363.7 3.7 convolution_convert_fusion.3
  367.4 1.6 multiply_reduce_fusion
  369.1 2.2 convolution_convert_fusion.5
  371.3 2.6 convolution_convert_fusion.1
  374.3 1.3 multiply_convert_fusion
  375.6 0.8 convolution_bitcast_fusion
  380.0 5.9 square_sum.3
  386.6 1.6 multiply_convert_fusion.2
  388.2 3.1 fusion.46
  391.8 1.3 fusion.47
  393.5 6.4 %convolution_convert_fusion = bf16[2048,1536]{1,0:T(8,128)(2,1)} fusion(bf16[512,2048]{1,0:T(8,128)(2,1)S(1)} %bitcast.207, bf16[512,512]{0,1:T(8,128)(2,1)S(1)} %bitcast.181, bf16[512,512]{0,1:T(8,128)(2,1)S(1)} %multiply_convert_fusion.1, bf16[512,512]{0,1:T(8,128)(2,1)S(1)} %multiply_convert_fusion.2), kind=kOutput, calls=%fused_computation | convolution fusion | flops 3229089792 | bytes 9961472 | tf_op jit(solution)/shard_map/td,ti->di/dot_general | solution.py:1636
  399.9 2.7 add_convert_fusion
  402.7 17.7 %square_scatter.3 = f32[128,2048]{1,0:T(8,128)} custom-call(bf16[4,128,2048]{2,1,0:T(8,128)(2,1)} %bitcast.172), custom_call_target="tpu_custom_call" | custom-call | bytes 62914560 | tf_op jit(solution)/shard_map/square_scatter/pallas_call | solution.py:864
  420.4 1.6 fusion.13
  423.0 182.9 %line_sum.1 = (bf16[16,2,4,16,1536]{4,3,2,1,0:T(8,128)(2,1)}, bf16[4,2,4,16,2048]{4,3,2,1,0:T(8,128)(2,1)}, f32[2,4,4,16,128]{4,3,2,1,0:T(8,128)}, f32[128,2048]...) custom-call(bf16[16,2,4,16,1536]{4,3,2,1,0:T(8,128)(2,1)} %bitcast.173, ...), custom_call_target="tpu_custom_call" | custom-call | bytes 314572800 | tf_op jit(solution)/shard_map/line_sum/pallas_call | solution.py:1215
  605.8 1.0 copy.59
  607.6 8.3 %slice_convert_fusion = (f32[2048,512]{1,0:T(8,128)}, f32[2048,512]{1,0:T(8,128)}, f32[2048,512]{1,0:T(8,128)}) fusion(bf16[2048,1536]{1,0:T(8,128)(2,1)} %bitcast.174), kind=kLoop, calls=%fused_computation.12 | loop fusion | flops 3145728 | bytes 18874368 | tf_op jit(solution)/shard_map/convert_element_type | solution.py:1669
  615.9 2.8 bitcast_convert_fusion
  618.7 1.5 fusion.44
  620.2 1.7 fusion.17
  622.6 2.1 copy.63
  624.7 1.6 copy-done.24
  626.3 2.1 copy.64
  628.4 1.6 copy-done.23
  630.0 2.0 copy.65
  (201 shorter events, 15.5 us)
Async XLA Ops:
  7.2 93.1 %copy-start = (bf16[2048,16]{0,1:T(8,128)(2,1)S(1)}, bf16[2048,16]{0,1:T(8,128)(2,1)}, u32[]{:S(2)}) copy-start(bf16[2048,16]{0,1:T(8,128)(2,1)} %param.27) | copy-start | bytes 196612
  7.2 203.3 %all-gather.3.cloned.1.call-start = ((), (), s32[]{:S(2)}) async-start(), calls=%async_computation | async-start | bytes 17301504 | tf_op jit(solution)/shard_map/all_gather | solution.py:1453
  42.1 3.7 copy-start.29
  42.1 3.7 copy-start.71
  45.8 11.0 %copy-start.14 = (f32[512,512]{0,1:T(8,128)}, f32[512,512]{0,1:T(8,128)S(1)}, u32[]{:S(2)}) copy-start(f32[512,512]{0,1:T(8,128)S(1)} %get-tuple-element.90) | copy-start | bytes 3145732
  45.8 11.0 %copy-start.56 = (f32[512]{0:T(512)S(1)}, f32[512]{0:T(512)}, u32[]{:S(2)}) copy-start(f32[512]{0:T(512)} %param.24) | copy-start | bytes 6148
  47.1 12.8 %copy-start.16 = (f32[512,512]{0,1:T(8,128)}, f32[512,512]{0,1:T(8,128)S(1)}, u32[]{:S(2)}) copy-start(f32[512,512]{0,1:T(8,128)S(1)} %get-tuple-element.92) | copy-start | bytes 3145732
  47.2 9.9 %copy-start.54 = (f32[512]{0:T(512)S(1)}, f32[512]{0:T(512)}, u32[]{:S(2)}) copy-start(f32[512]{0:T(512)} %param.23) | copy-start | bytes 6148
  58.0 4.1 copy-start.72
  59.0 4.4 copy-start.4
  62.1 306.9 %copy-start.45 = (f32[4,512]{1,0:T(4,128)}, f32[4,512]{1,0:T(4,128)S(1)}, u32[]{:S(2)}) copy-start(f32[4,512]{1,0:T(4,128)S(1)} %log_add_fusion) | copy-start | bytes 24580
  63.4 4.5 copy-start.35
  64.8 3.1 copy-start.76
  65.3 33.3 %copy-start.75 = (s32[16]{0:T(128)S(1)}, s32[16]{0:T(128)}, u32[]{:S(2)}) copy-start(s32[16]{0:T(128)} %param.33) | copy-start | bytes 196
  65.3 33.3 %copy-start.66 = (s32[1,128,8]{1,2,0:T(8,128)S(1)}, s32[1,128,8]{1,2,0:T(8,128)}, u32[]{:S(2)}) copy-start(s32[1,128,8]{1,2,0:T(8,128)} %param.32) | copy-start | bytes 12292
  65.3 33.3 %copy-start.9 = (bf16[1,128,2048]{2,1,0:T(8,128)(2,1)S(1)}, bf16[1,128,2048]{2,1,0:T(8,128)(2,1)}, u32[]{:S(2)}) copy-start(bf16[1,128,2048]{2,1,0:T(8,128)(2,1)} %param.17) | copy-start | bytes 1572868
  67.9 32.2 %copy-start.39 = (f32[2048]{0:T(1024)S(1)}, f32[2048]{0:T(1024)}, u32[]{:S(2)}) copy-start(f32[2048]{0:T(1024)} %param.26) | copy-start | bytes 24580
  67.9 33.1 %copy-start.2 = (bf16[2,2048,256]{2,1,0:T(8,128)(2,1)S(1)}, bf16[2,2048,256]{2,1,0:T(8,128)(2,1)}, u32[]{:S(2)}) copy-start(bf16[2,2048,256]{2,1,0:T(8,128)(2,1)} %w_gate.3) | copy-start | bytes 6291460
  98.6 237.9 %copy-start.43 = (pred[128,16]{0,1:T(8,128)(4,1)}, pred[128,16]{0,1:T(8,128)(4,1)S(1)}, u32[]{:S(2)}) copy-start(pred[128,16]{0,1:T(8,128)(4,1)S(1)} %fusion.30) | copy-start | bytes 6148
  100.1 239.3 %copy-start.60 = (f32[128]{0:T(128)}, f32[128]{0:T(128)S(1)}, u32[]{:S(2)}) copy-start(f32[128]{0:T(128)S(1)} %add_rsqrt_fusion) | copy-start | bytes 1540
  100.6 236.0 %copy-start.37 = (f32[128,16]{0,1:T(8,128)}, f32[128,16]{0,1:T(8,128)S(1)}, u32[]{:S(2)}) copy-start(f32[128,16]{0,1:T(8,128)S(1)} %get-tuple-element.96) | copy-start | bytes 24580
  100.6 236.0 %copy-start.58 = (f32[128]{0:T(128)}, f32[128]{0:T(128)S(1)}, u32[]{:S(2)}) copy-start(f32[128]{0:T(128)S(1)} %get-tuple-element.95) | copy-start | bytes 1540
  100.6 236.0 %copy-start.62 = (f32[128]{0:T(128)}, f32[128]{0:T(128)S(1)}, u32[]{:S(2)}) copy-start(f32[128]{0:T(128)S(1)} %fusion.36) | copy-start | bytes 1540
  101.1 235.5 %copy-start.52 = (pred[128,16]{0,1:T(8,128)(4,1)}, pred[128,16]{0,1:T(8,128)(4,1)S(1)}, u32[]{:S(2)}) copy-start(pred[128,16]{0,1:T(8,128)(4,1)S(1)} %get-tuple-element.98) | copy-start | bytes 6148
  210.5 126.1 %copy-start.7 = (f32[128,2048]{1,0:T(8,128)S(1)}, f32[128,2048]{1,0:T(8,128)}, u32[]{:S(2)}) copy-start(f32[128,2048]{1,0:T(8,128)} %copy-done.6) | copy-start | bytes 3145732
  339.4 28.0 %copy-start.67 = (f32[128]{0:T(128)}, f32[128]{0:T(128)S(1)}, u32[]{:S(2)}) copy-start(f32[128]{0:T(128)S(1)} %broadcast_multiply_fusion.6) | copy-start | bytes 1540
  342.6 24.8 %copy-start.36 = (bf16[512,512]{0,1:T(8,128)(2,1)S(1)}, bf16[512,512]{0,1:T(8,128)(2,1)}, u32[]{:S(2)}) copy-start(bf16[512,512]{0,1:T(8,128)(2,1)} %copy-done.35) | copy-start | bytes 1572868
  363.7 3.7 copy-start.5
  388.2 3.5 copy-start.30
  393.5 6.4 %copy-start.27 = (bf16[2048,512]{1,0:T(8,128)(2,1)S(1)}, bf16[2048,512]{1,0:T(8,128)(2,1)}, u32[]{:S(2)}) copy-start(bf16[2048,512]{1,0:T(8,128)(2,1)} %param.21) | copy-start | bytes 6291460
  399.9 20.5 %copy-start.10 = (bf16[1,128,2048]{2,1,0:T(8,128)(2,1)S(1)}, bf16[1,128,2048]{2,1,0:T(8,128)(2,1)}, u32[]{:S(2)}) copy-start(bf16[1,128,2048]{2,1,0:T(8,128)(2,1)} %param.17) | copy-start | bytes 1572868
  399.9 20.5 %copy-start.41 = (f32[2048]{0:T(1024)S(1)}, f32[2048]{0:T(1024)}, u32[]{:S(2)}) copy-start(f32[2048]{0:T(1024)} %param.25) | copy-start | bytes 24580
  399.9 20.5 %copy-start.65 = (f32[128]{0:T(128)S(1)}, f32[128]{0:T(128)}, u32[]{:S(2)}) copy-start(f32[128]{0:T(128)} %copy-done.64) | copy-start | bytes 1540
  402.7 19.4 %copy-start.69 = (pred[4]{0:T(512)(128)(4,1)S(1)}, pred[4]{0:T(512)(128)(4,1)}, u32[]{:S(2)}) copy-start(pred[4]{0:T(512)(128)(4,1)} %iota_compare_fusion.5) | copy-start | bytes 16
  402.7 19.5 %copy-start.47 = (f32[2048]{0:T(1024)S(1)}, f32[2048]{0:T(1024)}, u32[]{:S(2)}) copy-start(f32[2048]{0:T(1024)} %get-tuple-element.48) | copy-start | bytes 24580
  607.6 8.3 %copy-start.28 = (bf16[4,2,4,16,2048]{4,3,2,1,0:T(8,128)(2,1)S(1)}, bf16[4,2,4,16,2048]{4,3,2,1,0:T(8,128)(2,1)}, u32[]{:S(2)}) copy-start(bf16[4,2,4,16,2048]{4,3,2,1,0:T(8,128)(2,1)} %get-tuple-element.43) | copy-start | bytes 6291460
  615.8 4.3 copy-start.8
  615.8 4.3 copy-start.11
  615.9 4.3 copy-start.13
  615.9 4.3 copy-start.18
  615.9 4.3 copy-start.32
  615.9 4.3 copy-start.40
  615.9 4.3 copy-start.61
  615.9 4.3 copy-start.68
  618.7 3.8 copy-start.25
  622.6 3.7 copy-start.24
  626.3 3.7 copy-start.23
  626.3 5.7 copy-start.1
  (31 other events, 54.4 us)
Sparse Core Ops, SparseCore 0:
  11.0 139.4 all-gather.2

commit v5 on v4

--- a/solution.py
+++ b/solution.py
@@ -193,6 +193,23 @@
 TN = (((0,), (0,)), ((), ()))
 
 
+def halves_of(x):
+    high = x.astype(jnp.bfloat16)
+    return high, (x - high.astype(jnp.float32)).astype(jnp.bfloat16)
+
+
+def spread(blocks, first, hidden, wide):
+    experts = blocks[0].shape[0]
+    high, low = halves_of(jnp.concatenate(blocks, axis=1))
+    row = lax.broadcasted_iota(jnp.int32, (2 * experts, wide), 0) % experts
+    col = lax.broadcasted_iota(jnp.int32, (2 * experts, wide), 1) // hidden
+    pick = (row == first + col).astype(jnp.float32).astype(jnp.bfloat16)
+    both = jnp.concatenate([high.astype(jnp.float32), low.astype(jnp.float32)], axis=0)
+    return lax.dot_general(
+        both.astype(jnp.bfloat16), pick, TN, preferred_element_type=jnp.float32
+    )
+
+
 def above(a, b):
     return (a - b + 63) // 64
 
@@ -205,7 +222,7 @@
     return turn + above(s, 2 * alternate) * (rest - turn)
 
 
-def gather_act_kernel(nz, own, own_small, w_gate, w_up, out, acts, gates, xb, ab, load_x, store, own_sem, zr, zs, xr, xs, yr, ys, dr, xf, yf, pr, ps, *small_sems):
+def gather_act_kernel(nz, own, own_small, w_gate, w_up, w_down, out, acts, weighted, forward, gates, xb, ab, hb, fb, load_x, store, own_sem, zr, zs, xr, xs, yr, ys, dr, xf, yf, pr, ps, *small_sems):
     at = Place()
     rows, width = own.shape
     local, _, hidden = w_gate.shape
@@ -217,6 +234,7 @@
     keep.start()
     small.stage(0)
     places = (at.f, at.fx, at.fy, at.fd)
+    first = at.e * w_gate.shape[0]
 
     def up(z):
         ref = out.at[at.f, 2 * z + at.c]
@@ -279,11 +297,14 @@
         return pltpu.make_async_copy(out.at[places[q], pl.ds(2 * z, 2)], xb.at[q], load_x.at[q])
 
     def stores(q, z):
+        pair, f = pl.ds(2 * z, 2), places[q]
         return [
-            pltpu.make_async_copy(
-                ab.at[q, k], acts.at[k, places[q], pl.ds(2 * z, 2)], store.at[q, k]
-            )
-            for k in range(2)
+            *(
+                pltpu.make_async_copy(ab.at[q, k], acts.at[k, f, pair], store.at[q, k])
+                for k in range(3)
+            ),
+            pltpu.make_async_copy(hb.at[q], weighted.at[f, pair], store.at[q, 3]),
+            pltpu.make_async_copy(fb.at[q], forward.at[f, pair], store.at[q, 4]),
         ]
 
     def fetch(q, z):
@@ -293,11 +314,32 @@
 
     def work(q, z):
         load(q, z).wait()
+        f = places[q]
         x = xb[q].reshape(2 * rows, width)
+        gate_all = spread([gates[0, f, z], gates[1, f, z]], first, hidden, local * hidden)
         for j in range(local):
-            for k, w in enumerate((w_gate, w_up)):
-                g = jnp.dot(x, w[j], preferred_element_type=jnp.float32)
-                ab[q, k, :, :, pl.ds(j * hidden, hidden)] = g.reshape(2, rows, hidden)
+            cols = pl.ds(j * hidden, hidden)
+            g_all = jnp.dot(x, w_gate[j], preferred_element_type=jnp.float32)
+            u_all = jnp.dot(x, w_up[j], preferred_element_type=jnp.float32)
+            for h in range(2):
+                g, u = g_all[h * rows : (h + 1) * rows], u_all[h * rows : (h + 1) * rows]
+                gate = gate_all[h * rows : (h + 1) * rows, j * hidden : (j + 1) * hidden]
+                sig = 1.0 / (1.0 + jnp.exp(-g))
+                silu = g * sig
+                hid = silu * u
+                ab[q, 0, h, :, cols] = u * sig * (1.0 + g * (1.0 - sig))
+                ab[q, 1, h, :, cols] = silu
+                ab[q, 2, h, :, cols] = hid
+                hb[q, h, :, cols] = (hid * gate).astype(jnp.bfloat16)
+        a = hb[q].reshape(2 * rows, local * hidden)
+
+        def body(t, carry):
+            cols = pl.ds(pl.multiple_of(t * 512, 512), 512)
+            total = jnp.dot(a, w_down[:, cols], preferred_element_type=jnp.float32)
+            fb[q, :, :, cols] = total.astype(jnp.bfloat16).reshape(2, rows, 512)
+            return carry
+
+        lax.fori_loop(0, width // 512, body, 0)
         for copy in stores(q, z):
             copy.start()
 
@@ -351,7 +393,7 @@
     lax.fori_loop(0, nz, finish, 0)
 
 
-def gather_act(rows, small, w_gate, w_up, nz, cid):
+def gather_act(rows, small, w_gate, w_up, w_down, nz, cid):
     r, c = rows.shape
     local, _, hidden = w_gate.shape
     wide = local * hidden
@@ -361,15 +403,19 @@
         functools.partial(gather_act_kernel, nz),
         out_shape=(
             jax.ShapeDtypeStruct((4, 2 * nz, r, c), bf16),
-            jax.ShapeDtypeStruct((2, 4, 2 * nz, r, wide), jnp.float32),
+            jax.ShapeDtypeStruct((3, 4, 2 * nz, r, wide), jnp.float32),
+            jax.ShapeDtypeStruct((4, 2 * nz, r, wide), bf16),
+            jax.ShapeDtypeStruct((4, 2 * nz, r, c), bf16),
             jax.ShapeDtypeStruct((2, 4, nz, *small.shape), jnp.float32),
         ),
-        in_specs=[vmem] * 4,
-        out_specs=(hbm, hbm, vmem),
+        in_specs=[vmem] * 5,
+        out_specs=(hbm, hbm, hbm, hbm, vmem),
         scratch_shapes=[
             pltpu.VMEM((4, 2, r, c), bf16),
-            pltpu.VMEM((4, 2, 2, r, wide), jnp.float32),
-            DMA((4,)), DMA((4, 2)),
+            pltpu.VMEM((4, 3, 2, r, wide), jnp.float32),
+            pltpu.VMEM((4, 2, r, wide), bf16),
+            pltpu.VMEM((4, 2, r, c), bf16),
+            DMA((4,)), DMA((4, 5)),
             DMA(()), DMA((nz,)), DMA((2, nz)), DMA((2, nz)), DMA((2, nz)), DMA((2, nz)), DMA((2, nz)),
             DMA((2, nz)), DMA((nz,)), DMA((nz,)), DMA((4, nz, 2)), DMA((4, nz, 2)),
             *SmallGather.sems(nz),
@@ -379,7 +425,7 @@
         ),
         cost_estimate=pl.CostEstimate(flops=0, bytes_accessed=240 << 20, transcendentals=0),
         name="gather_act",
-    )(rows, small, w_gate, w_up)
+    )(rows, small, w_gate, w_up, w_down.reshape(wide, c))
 
 
 def add_rows(dst, dst_rows, parts):
@@ -397,7 +443,7 @@
     lax.fori_loop(0, count // 16, body, 0)
 
 
-def scatter_plan(at, nz, part, out, refs, staged=None):
+def scatter_plan(at, nz, part, out, refs, staged=None, split=1):
     acc, pb, xh, yh, xf, yf, zu, zd, ls, pr, ps, xhs, xhr, yhs, yhr, xs, xr, ys, yr, us, ur, ds_, dr = refs
     rows = out.shape[0]
     half = rows // 2
@@ -439,11 +485,15 @@
     def full_y(z):
         return send(acc.at[at.fy, z], yf.at[z], ys.at[z], yr.at[z], at.fy, at.e)
 
-    def go_up(z):
-        return send(acc.at[at.f, z], zu.at[z], us.at[z], ur.at[z], at.f, at.e + 2)
-
-    def go_down(z):
-        return send(acc.at[at.f, z], zd.at[z], ds_.at[z], dr.at[z], at.f, at.e - 2)
+    count = rows // split
+
+    def go_up(z, k):
+        cut = pl.ds(k * count, count)
+        return send(acc.at[at.f, z, cut], zu.at[z, cut], us.at[z, k], ur.at[z, k], at.f, at.e + 2)
+
+    def go_down(z, k):
+        cut = pl.ds(k * count, count)
+        return send(acc.at[at.f, z, cut], zd.at[z, cut], ds_.at[z, k], dr.at[z, k], at.f, at.e - 2)
 
     def diag_step(s):
         z = place(s)
@@ -469,47 +519,49 @@
         add_rows(a, (half, half), [(a, half), (b, half)])
         full_y(z).start()
 
-    def line_step(s):
+    def line_step(s, k=0):
         z = place(s)
-        ready(3, z)
-        full_x(z).wait_recv()
-        full_y(z).wait_recv()
+        if k == 0:
+            ready(3, z)
+            full_x(z).wait_recv()
+            full_y(z).wait_recv()
+        r = k * count
         a = acc.at[at.f, z]
-        four = [(a, 0), (pb.at[at.f, z], 0), (xf.at[z], 0), (yf.at[z], 0)]
+        four = [(a, r), (pb.at[at.f, z], r), (xf.at[z], r), (yf.at[z], r)]
 
         @pl.when(z > at.z)
         def _():
             @pl.when(at.z > 0)
             def _():
-                go_up(z).wait_recv()
-                add_rows(a, (0, rows), four + [(zu.at[z], 0)])
-
-            pl.when(at.z == 0)(lambda: add_rows(a, (0, rows), four))
-            go_up(z).start()
+                go_up(z, k).wait_recv()
+                add_rows(a, (r, count), four + [(zu.at[z], r)])
+
+            pl.when(at.z == 0)(lambda: add_rows(a, (r, count), four))
+            go_up(z, k).start()
 
         @pl.when(z < at.z)
         def _():
             @pl.when(at.z < nz - 1)
             def _():
-                go_down(z).wait_recv()
-                add_rows(a, (0, rows), four + [(zd.at[z], 0)])
-
-            pl.when(at.z == nz - 1)(lambda: add_rows(a, (0, rows), four))
-            go_down(z).start()
+                go_down(z, k).wait_recv()
+                add_rows(a, (r, count), four + [(zd.at[z], r)])
+
+            pl.when(at.z == nz - 1)(lambda: add_rows(a, (r, count), four))
+            go_down(z, k).start()
 
         @pl.when(z == at.z)
         def _():
-            add_rows(out, (0, rows), four)
+            add_rows(out, (r, count), four)
 
             @pl.when(at.z > 0)
             def _():
-                go_up(z).wait_recv()
-                add_rows(out, (0, rows), [(out, 0), (zu.at[z], 0)])
+                go_up(z, k).wait_recv()
+                add_rows(out, (r, count), [(out, r), (zu.at[z], r)])
 
             @pl.when(at.z < nz - 1)
             def _():
-                go_down(z).wait_recv()
-                add_rows(out, (0, rows), [(out, 0), (zd.at[z], 0)])
+                go_down(z, k).wait_recv()
+                add_rows(out, (r, count), [(out, r), (zd.at[z], r)])
 
     def finish():
         def body(z, carry):
@@ -520,8 +572,9 @@
             half_y(z).wait_send()
             full_x(z).wait_send()
             full_y(z).wait_send()
-            pl.when(z > at.z)(lambda: go_up(z).wait_send())
-            pl.when(z < at.z)(lambda: go_down(z).wait_send())
+            for k in range(split):
+                pl.when(z > at.z)(functools.partial(lambda k: go_up(z, k).wait_send(), k))
+                pl.when(z < at.z)(functools.partial(lambda k: go_down(z, k).wait_send(), k))
             return carry
 
         lax.fori_loop(0, nz, body, 0)
@@ -542,16 +595,17 @@
         buf(4, nz, r), buf(4, nz, r), buf(nz, r // 2), buf(nz, r // 2),
         buf(nz, r), buf(nz, r), buf(nz, r), buf(nz, r),
         DMA((4, nz)), DMA((4, nz)), DMA((4, nz)),
-        *[DMA((nz,))] * 12,
+        *[DMA((nz,))] * 8,
+        *[DMA((nz, 4))] * 4,
     ]
 
 
-def scatter_act_kernel(nz, pre, grads, gates, w_gate, w_up, w_down, out, out_small, acts, forward, *refs):
+def scatter_act_kernel(nz, pre, grads, gates, w_gate, w_up, w_down, out, out_small, acts, *refs):
     at = Place()
     refs = iter(refs)
     moved = take(refs, 23)
     acc = moved[0]
-    pb_, cb, ab, sb, fb, terms, load_sem, store_sem, forward_sem = take(refs, 9)
+    pb_, cb, ab, sb, terms, load_sem, store_sem = take(refs, 7)
     _, diag, plane, line, close, place, to_p = scatter_plan(at, nz, None, out, moved, sb)
     small = SmallScatter(at, nz, terms, out_small, take(refs, 4), take(refs, 4))
     greet([(at.fx, at.e), (at.fy, at.e), (at.f, at.pe)], (at, nz))
@@ -569,11 +623,11 @@
         copies = []
         for h, core in enumerate(cores):
             slot = 2 * z + core
-            for k in range(2):
+            for k in range(3):
                 copies.append(
                     pltpu.make_async_copy(pre.at[k, f, slot], pb_.at[q, k, h], load_sem.at[q, h, k])
                 )
-            copies.append(pltpu.make_async_copy(grads.at[f, slot], cb.at[q, h], load_sem.at[q, h, 2]))
+            copies.append(pltpu.make_async_copy(grads.at[f, slot], cb.at[q, h], load_sem.at[q, h, 3]))
         return copies
 
     def stores(q, s):
@@ -583,14 +637,7 @@
                 ab.at[q, k, h], acts.at[k, f, 2 * z + core], store_sem.at[q, h, k]
             )
             for h, core in enumerate(cores)
-            for k in range(3)
-        ]
-
-    def sends(q, s):
-        z, f = place(s), fs[q]
-        return [
-            pltpu.make_async_copy(fb.at[q, h], forward.at[f, 2 * z + core], forward_sem.at[q, h])
-            for h, core in enumerate(cores)
+            for k in range(2)
         ]
 
     def act(q, s):
@@ -604,28 +651,21 @@
                 copy.wait()
 
         c = cb[q].reshape(2 * rows, width)
+        gate_all = spread([gates[core, f, z] for core in cores], first, hidden, local * hidden)
         sums = [None, None]
         for j in range(local):
-            pick = (expert_row == first + j).astype(jnp.float32)
+            pick = (expert_row == first + j).astype(jnp.float32).astype(jnp.bfloat16)
             cols = pl.ds(j * hidden, hidden)
             dh = lax.dot_general(c, w_down[j], NT, preferred_element_type=jnp.float32)
             for h, core in enumerate(cores):
-                g, u = pb_[q, 0, h, :, cols], pb_[q, 1, h, :, cols]
                 d = dh[h * rows : (h + 1) * rows]
-                sig = 1.0 / (1.0 + jnp.exp(-g))
-                silu = g * sig
-                hid = silu * u
-                gate = lax.dot_general(
-                    gates[core, f, z], pick, TN, precision=precise, preferred_element_type=jnp.float32
-                )
-                mine = lax.dot_general(
-                    pick, hid * d, NT, precision=precise, preferred_element_type=jnp.float32
-                )
-                sums[h] = mine if sums[h] is None else sums[h] + mine
+                gate = gate_all[h * rows : (h + 1) * rows, j * hidden : (j + 1) * hidden]
+                for part in halves_of(pb_[q, 2, h, :, cols] * d):
+                    mine = lax.dot_general(pick, part, NT, preferred_element_type=jnp.float32)
+                    sums[h] = mine if sums[h] is None else sums[h] + mine
                 d = d * gate
-                ab[q, 0, h, :, cols] = (d * u * sig * (1.0 + g * (1.0 - sig))).astype(jnp.bfloat16)
-                ab[q, 1, h, :, cols] = (d * silu).astype(jnp.bfloat16)
-                ab[q, 2, h, :, cols] = (hid * gate).astype(jnp.bfloat16)
+                ab[q, 0, h, :, cols] = (d * pb_[q, 0, h, :, cols]).astype(jnp.bfloat16)
+                ab[q, 1, h, :, cols] = (d * pb_[q, 1, h, :, cols]).astype(jnp.bfloat16)
         for h, core in enumerate(cores):
             terms[core, f, z] = sums[h]
         for copy in stores(q, s):
@@ -658,33 +698,6 @@
 
         lax.fori_loop(0, width // tile, body, 0)
         to_p(q, z).start()
-
-    def ahead(q, s):
-        @pl.when(s > 0)
-        def _():
-            for copy in sends(q, s - 1):
-                copy.wait()
-
-        a = ab[q, 2].reshape(2 * rows, local * hidden)
-
-        def body(t, carry):
-            cols = pl.ds(pl.multiple_of(t * tile, tile), tile)
-            total = None
-            for j in range(local):
-                term = jnp.dot(
-                    a[:, j * hidden : (j + 1) * hidden],
-                    w_down[j, :, cols],
-                    preferred_element_type=jnp.float32,
-                )
-                total = term if total is None else total + term
-            total = total.astype(jnp.bfloat16)
-            fb[q, 0, :, cols] = total[:rows]
-            fb[q, 1, :, cols] = total[rows:]
-            return carry
-
-        lax.fori_loop(0, width // tile, body, 0)
-        for copy in sends(q, s):
-            copy.start()
 
     for q in range(4):
         for copy in loads(q, 0):
@@ -703,8 +716,6 @@
             act(3, s)
             pl.when(last)(lambda: small.stage(0))
             back(3, s)
-            for q in range(4):
-                ahead(q, s)
             pl.when(last)(lambda: small.stage(1))
             plane(s)
             pl.when(last)(lambda: small.stage(2))
@@ -716,7 +727,7 @@
     lax.fori_loop(0, nz + 1, body, 0)
     small.stage(4)
     for q in range(4):
-        for copy in stores(q, nz - 1) + sends(q, nz - 1):
+        for copy in stores(q, nz - 1):
             copy.wait()
     close()
 
@@ -732,20 +743,18 @@
         out_shape=(
             jax.ShapeDtypeStruct((r, c), jnp.float32),
             jax.ShapeDtypeStruct(small, jnp.float32),
-            jax.ShapeDtypeStruct((3, 4, 2 * nz, r, wide), bf16),
-            jax.ShapeDtypeStruct((4, 2 * nz, r, c), bf16),
+            jax.ShapeDtypeStruct((2, 4, 2 * nz, r, wide), bf16),
         ),
         in_specs=[hbm, hbm, vmem, vmem, vmem, vmem],
-        out_specs=(vmem, vmem, hbm, hbm),
+        out_specs=(vmem, vmem, hbm),
         scratch_shapes=[
             *scatter_scratch(grads, nz),
-            pltpu.VMEM((4, 2, 2, r, wide), jnp.float32),
+            pltpu.VMEM((4, 3, 2, r, wide), jnp.float32),
             pltpu.VMEM((4, 2, r, c), bf16),
-            pltpu.VMEM((4, 3, 2, r, wide), bf16),
+            pltpu.VMEM((4, 2, 2, r, wide), bf16),
             pltpu.VMEM((4, r, c), bf16),
-            pltpu.VMEM((4, 2, r, c), bf16),
             pltpu.VMEM((2, 4, nz, *small), jnp.float32),
-            DMA((4, 2, 3)), DMA((4, 2, 3)), DMA((4, 2)),
+            DMA((4, 2, 4)), DMA((4, 2, 2)),
             *SmallScatter.scratch(nz, small),
             *SmallScatter.sems(nz),
         ],
@@ -902,9 +911,10 @@
 
 class product_plan:
     def __init__(self, inputs, outs, refs):
-        self.rows, self.acts, self.grads = inputs
+        self.rows, self.acts, self.weighted, self.grads = inputs
         self.outs = outs
-        self.wide_acc, self.down_acc, self.xw, self.aw, self.load_sem, self.store_sem = refs
+        self.acc, self.xw, self.aw, self.load_sem, self.store_sem = refs
+        self.tile = self.acc.shape[2]
         self.units = self.rows.shape[0]
         self.local = self.outs[0].shape[0]
         self.per_pass = self.units // 2
@@ -917,7 +927,7 @@
         if p == self.local:
             return [
                 pltpu.make_async_copy(self.grads.at[u], self.xw.at[k], sem.at[0]),
-                pltpu.make_async_copy(self.acts.at[2, u], self.aw.at[k], sem.at[1]),
+                pltpu.make_async_copy(self.weighted.at[u], self.aw.at[k], sem.at[1]),
             ]
         cols = pl.ds(p * hidden, hidden)
         return [
@@ -937,17 +947,28 @@
             for copy in self.loads(0, k, 0):
                 copy.start()
 
-        for acc in (*[self.wide_acc.at[p] for p in range(self.local)], self.down_acc):
-            def body(r, carry, acc=acc):
-                acc[pl.ds(r * 8, 8), :] = jnp.zeros((8, acc.shape[1]), jnp.float32)
-                return carry
-
-            lax.fori_loop(0, acc.shape[0] // 8, body, 0)
+        for p in range(self.local):
+            self.clear(p)
+
+    def clear(self, p):
+        def body(r, carry):
+            self.acc[p, pl.ds(r * 8, 8), :] = jnp.zeros((8, self.tile), jnp.float32)
+            return carry
+
+        lax.fori_loop(0, self.acc.shape[1] // 8, body, 0)
 
     def step(self, i):
-        tile = 512
+        tile = self.tile
 
         def run(p):
+            if p == self.local:
+
+                @pl.when(i == p * self.per_pass)
+                def _():
+                    for copy in self.stores(0):
+                        copy.wait()
+                    self.clear(0)
+
             for k in range(2):
                 for copy in self.loads(i, k, p):
                     copy.wait()
@@ -956,11 +977,11 @@
                     cols = pl.ds(t * tile, tile)
                     x = self.xw[k, :, cols]
                     if p == self.local:
-                        self.down_acc[:, cols] += lax.dot_general(
+                        self.acc[0, cols, :] += lax.dot_general(
                             a, x, TN, preferred_element_type=jnp.float32
                         )
                     else:
-                        self.wide_acc[p, cols, :] += lax.dot_general(
+                        self.acc[p, cols, :] += lax.dot_general(
                             x, a, TN, preferred_element_type=jnp.float32
                         )
 
@@ -980,8 +1001,14 @@
     def stores(self, p):
         hidden = self.outs[0].shape[2]
         if p == self.local:
-            return [pltpu.make_async_copy(self.down_acc, self.outs[2], self.store_sem.at[p, 0])]
-        acc = self.wide_acc.at[p]
+            cuts = [pl.ds(k * self.tile, self.tile) for k in range(self.outs[2].shape[1] // self.tile)]
+            return [
+                pltpu.make_async_copy(
+                    self.acc.at[0, cut], self.outs[2].at[:, cut], self.store_sem.at[p, k]
+                )
+                for k, cut in enumerate(cuts)
+            ]
+        acc = self.acc.at[p]
         return [
             pltpu.make_async_copy(
                 acc.at[:, pl.ds(k * hidden, hidden)], self.outs[k].at[p], self.store_sem.at[p, k]
@@ -990,26 +1017,91 @@
         ]
 
     def finish(self):
-        for p in range(self.local + 1):
+        for p in range(1, self.local + 1):
             for copy in self.stores(p):
                 copy.wait()
+
+
+class SquareScatter:
+    def __init__(self, at, part, normed, out, table, refs):
+        self.part, self.normed, self.out, self.table = part, normed, out, table
+        self.xh, self.yh, self.xf, self.yf, self.px, self.py, self.pf, ss, rs, ls = refs
+        half = self.xh.shape[0]
+        lo, hi = pl.ds(0, half), pl.ds(half, half)
+
+        def to_x(k, src, dst):
+            return send(src, dst, ss.at[k], rs.at[k], at.fx, at.e)
+
+        def to_y(k, src, dst):
+            return send(src, dst, ss.at[k], rs.at[k], at.fy, at.e)
+
+        self.copies = [
+            to_x(0, part.at[at.fd, lo], self.xh),
+            to_y(1, part.at[at.fd, hi], self.yh),
+            to_x(2, part.at[at.fx, lo], self.xf.at[lo]),
+            to_y(3, part.at[at.fy, hi], self.yf.at[hi]),
+            to_x(4, self.yh, self.xf.at[hi]),
+            to_y(5, self.xh, self.yf.at[lo]),
+        ]
+        self.loads = [
+            pltpu.make_async_copy(part.at[at.fx, hi], self.px, ls.at[0]),
+            pltpu.make_async_copy(part.at[at.fy, lo], self.py, ls.at[1]),
+            pltpu.make_async_copy(part.at[at.f], self.pf, ls.at[2]),
+        ]
+
+    def stage(self, i):
+        copies, half, rows = self.copies, self.xh.shape[0], self.out.shape[0]
+        if i == 0:
+            for copy in copies[:4] + self.loads:
+                copy.start()
+        elif i == 1:
+            for copy in self.loads:
+                copy.wait()
+            copies[1].wait_recv()
+            add_rows(self.yh, (0, half), [(self.yh, 0), (self.px, 0)])
+            copies[4].start()
+            copies[0].wait_recv()
+            add_rows(self.xh, (0, half), [(self.xh, 0), (self.py, 0)])
+            copies[5].start()
+        elif i == 2:
+            for copy in copies[2:]:
+                copy.wait_recv()
+            add_rows(self.out, (0, rows), [(self.pf, 0), (self.xf, 0), (self.yf, 0)])
+
+            def body(r, total):
+                cut = pl.ds(pl.multiple_of(r * 16, 16), 16)
+                both = self.out[cut, :] * self.normed[cut, :].astype(jnp.float32)
+                return total + both[:8] + both[8:]
+
+            total = lax.fori_loop(0, rows // 16, body, jnp.zeros((8, self.out.shape[1]), jnp.float32))
+            total = jnp.sum(total, axis=0, keepdims=True)
+            for k in range(self.table.shape[3]):
+                self.table[0, 0, 0, k : k + 1, :] = total[:, k * 128 : (k + 1) * 128]
+            for copy in copies:
+                copy.wait_send()
 
 
 def line_sum_kernel(nz, counts, *refs):
     at = Place()
     refs = iter(refs)
     n = len(counts)
-    parts, part_small, rows_part, inputs = take(refs, n), next(refs), next(refs), take(refs, 3)
+    parts, table_in, rows_part, inputs = take(refs, n), next(refs), next(refs), take(refs, 4)
+    first_part, normed = take(refs, 2)
     outs, out_small, rows_out, grads = take(refs, n), next(refs), next(refs), take(refs, 3)
-    begin, diag, plane, line, close, _, _ = scatter_plan(at, nz, rows_part, rows_out, take(refs, 23))
-    product = product_plan(inputs, grads, take(refs, 6))
+    first_out, part_small = take(refs, 2)
+    square = SquareScatter(at, first_part, normed, first_out, part_small, take(refs, 10))
+    begin, diag, plane, line, close, _, _ = scatter_plan(
+        at, nz, rows_part, rows_out, take(refs, 23), split=2
+    )
+    product = product_plan(inputs, grads, take(refs, 5))
     bufs = [take(refs, 5) for _ in range(n)]
     sems = [take(refs, 12) for _ in range(n)]
     own_small = next(refs)
     scatter_small = SmallScatter(at, nz, part_small, own_small, take(refs, 4), take(refs, 4))
     gather_small = SmallGather(at, nz, own_small, out_small, take(refs, 4))
     greet([(at.fx, at.e), (at.fy, at.e), (at.f, at.pe)], (at, nz))
-    scatter_small.stage(0)
+    square.stage(0)
+    part_small[...] = table_in[...]
     total = sum(counts)
     last = nz - 1
     lag, per = 2, 5
@@ -1155,7 +1247,8 @@
         pl.when((turn == 0) & (s + 1 < nz))(lambda: begin(s + 1))
         pl.when((turn == 0) & (s < nz))(lambda: diag(s))
         pl.when((turn == 2) & (s < nz))(lambda: plane(s))
-        pl.when((turn == 3) & (s >= 1) & (s < nz + 1))(lambda: line(s - 1))
+        pl.when((turn == 3) & (s >= 1) & (s < nz + 1))(lambda: line(s - 1, 0))
+        pl.when((turn == 0) & (s >= 2) & (s < nz + 2))(lambda: line(s - 2, 1))
         piece(i, halve)
         piece(i - lag * at.z, rise, at.z < last)
         piece(i - lag * (last - at.z), sink, at.z > 0)
@@ -1164,14 +1257,15 @@
         for d in range(1, nz):
             piece(i - lag * (nz + d), functools.partial(pass_up, z=at.z - d), at.z >= d)
             piece(i - lag * (nz + d), functools.partial(pass_down, z=at.z + d), at.z + d <= last)
-        for s in range(1, 5):
-            pl.when(i == s)(functools.partial(scatter_small.stage, s))
-        for s in range(5):
-            pl.when(i == 5 + s)(functools.partial(gather_small.stage, s))
+        for k, at_step in ((1, 1), (2, 5)):
+            pl.when(i == at_step)(functools.partial(square.stage, k))
+        for k in range(5):
+            pl.when(i == 6 + k)(functools.partial(scatter_small.stage, k))
+            pl.when(i == 11 + k)(functools.partial(gather_small.stage, k))
         product.step(i)
         return carry
 
-    steps = max(total + lag * (2 * nz - 1), per * (nz + 1), product.steps)
+    steps = max(total + lag * (2 * nz - 1), per * (nz + 2), product.steps)
     lax.fori_loop(0, steps, body, 0)
     product.finish()
 
@@ -1197,7 +1291,7 @@
     close()
 
 
-def line_sum(parts, small, rows, inputs, local, nz, cid):
+def line_sum(parts, small, rows, inputs, first, normed, local, nz, cid):
     counts = tuple(p.shape[0] for p in parts)
     units, unit, width = inputs[0].shape
     wide = inputs[1].shape[3]
@@ -1212,6 +1306,9 @@
         each, line = DMA((n,)), DMA((n, nz))
         sems += [each, each, each, line, line, line, line, DMA((2, n, nz)), line, line, line, each]
     hbm, vmem = pl.BlockSpec(memory_space=pl.ANY), pl.BlockSpec(memory_space=pltpu.VMEM)
+    _, r, c = first.shape
+    bf16 = jnp.bfloat16
+    assert small.shape[3] * small.shape[4] == c
     return pl.pallas_call(
         functools.partial(line_sum_kernel, nz, counts),
         out_shape=(
@@ -1221,16 +1318,21 @@
             jax.ShapeDtypeStruct((local, width, wide // local), jnp.float32),
             jax.ShapeDtypeStruct((local, width, wide // local), jnp.float32),
             jax.ShapeDtypeStruct((wide, width), jnp.float32),
+            jax.ShapeDtypeStruct(first.shape[1:], jnp.float32),
         ),
-        in_specs=[hbm] * len(parts) + [vmem, hbm] + [hbm] * 3,
-        out_specs=(*[hbm] * len(parts), vmem, vmem, *[hbm] * 3),
+        in_specs=[hbm] * len(parts) + [vmem, hbm] + [hbm] * len(inputs) + [hbm, vmem],
+        out_specs=(*[hbm] * len(parts), vmem, vmem, *[hbm] * 3, vmem),
         scratch_shapes=[
+            pltpu.VMEM(small.shape, jnp.float32),
+            pltpu.VMEM((r // 2, c), bf16), pltpu.VMEM((r // 2, c), bf16),
+            pltpu.VMEM((r, c), bf16), pltpu.VMEM((r, c), bf16),
+            pltpu.VMEM((r // 2, c), bf16), pltpu.VMEM((r // 2, c), bf16), pltpu.VMEM((r, c), bf16),
+            DMA((6,)), DMA((6,)), DMA((3,)),
             *scatter_scratch(rows, nz),
             pltpu.VMEM((local, width, 2 * wide // local), jnp.float32),
-            pltpu.VMEM((wide, width), jnp.float32),
             pltpu.VMEM((2, unit, width), rows.dtype),
             pltpu.VMEM((2, unit, wide), rows.dtype),
-            DMA((2, 3)), DMA((local + 1, 2)),
+            DMA((2, 3)), DMA((local + 1, 4)),
             *scratch, *sems, pltpu.VMEM(small.shape[-2:], jnp.float32),
             *SmallScatter.scratch(nz, small.shape[-2:]), *SmallScatter.sems(nz), *SmallGather.sems(nz),
         ],
@@ -1239,7 +1341,7 @@
         ),
         cost_estimate=pl.CostEstimate(flops=0, bytes_accessed=300 << 20, transcendentals=0),
         name="line_sum",
-    )(*parts, small, rows, *inputs)
+    )(*parts, small, rows, *inputs, first, normed)
 
 
 def rope_tables(seg_ids, head_dim):
@@ -1280,7 +1382,7 @@
     return lax.psum((pair_sums[0], pair_sums[1]), "fsdp")
 
 
-def share_rows(kernel, term_fn, own_rows):
+def share_rows(term_fn, own_rows, kernel=0):
     if kernel:
         parts = term_fn(jnp.int32(0), own_rows * lax.axis_size("fsdp"))
         return square_scatter(parts.reshape(-1, own_rows, parts.shape[1]), kernel)
@@ -1453,10 +1555,10 @@
     grad_all = lax.all_gather(cotangent, ("fsdp", "expert"), axis=0, tiled=True)
     nz = owners // 2
     grad_all = grad_all.reshape(shards, owners, tok_count, model_width)
-    rows_all, pre, gates = gather_act(second_rows, gate_kept.T, w_gate, w_up, nz, 7)
-    back_rows, terms, acts, forward = scatter_act(
-        pre, grad_all, gates, w_gate, w_up, w_down, nz, 8
-    )
+    rows_all, pre, weighted, forward, gates = gather_act(
+        second_rows, gate_kept.T, w_gate, w_up, w_down, nz, 7
+    )
+    back_rows, terms, acts = scatter_act(pre, grad_all, gates, w_gate, w_up, w_down, nz, 8)
     grad_gate_k = terms.T * kept_mask
     grad_logits = gate_wts * (grad_gate_k - jnp.sum(gate_wts * grad_gate_k, axis=1, keepdims=True))
     router_grad = jnp.dot(grad_logits.T, second_rows.astype(jnp.float32), precision=precise)
@@ -1466,13 +1568,14 @@
     units = shards * nz
     inputs = (
         rows_all.reshape(units, -1, model_width),
-        acts.reshape(3, units, -1, wide),
+        acts.reshape(2, units, -1, wide),
+        weighted.reshape(units, -1, wide),
         grad_all.reshape(units, -1, model_width),
     )
     return forward, grad_second, router_grad, inputs
 
 
-def sum_grads(narrow, gains, head_gains, rows, inputs, local, nz):
+def sum_grads(narrow, gains, head_gains, rows, inputs, first, normed, local, nz):
     shards, width = lax.axis_size("fsdp"), gains.shape[1]
     mine = lax.iota(jnp.int32, shards) == lax.axis_index("fsdp")
     heads_flat = jnp.pad(head_gains.reshape(-1), (0, width - head_gains.size))
@@ -1481,12 +1584,15 @@
     small = jnp.pad(table.reshape(-1), (0, 2 * shards * nz * share * 128 - table.size))
     small = small.reshape(2, shards, nz, share, 128)
     parts = [g.reshape(-1, 2, nz, 16, g.shape[1]) for g in narrow]
-    *sums, small, rows, gate, up, down = line_sum(parts, small, rows, inputs, local, nz, 9)
+    first = first.reshape(shards, -1, width)
+    *sums, small, rows, gate, up, down, first = line_sum(
+        parts, small, rows, inputs, first, normed.astype(jnp.bfloat16), local, nz, 9
+    )
     expert_grads = (gate, up, down.reshape(local, -1, width))
     small = small.reshape(-1)[: table.size].reshape(table.shape)
     own = lax.dynamic_slice_in_dim(small, gains.shape[0] + lax.axis_index("fsdp"), 1, axis=0)
     head_gains = own[0, : head_gains.size].reshape(head_gains.shape)
-    return [s.reshape(g.shape) for s, g in zip(sums, narrow)], small[: gains.shape[0]], head_gains, rows, expert_grads
+    return [s.reshape(g.shape) for s, g in zip(sums, narrow)], small[: gains.shape[0]], head_gains, rows, expert_grads, first
 
 
 def on_device(
@@ -1565,7 +1671,7 @@
     def mixed_term(start, length):
         return jnp.dot(attn_rows, w_output, preferred_element_type=jnp.float32).astype(jnp.bfloat16)
 
-    mixed_rows = share_rows(dense and 4, mixed_term, tok_count).astype(jnp.float32)
+    mixed_rows = share_rows(mixed_term, tok_count, dense and 4).astype(jnp.float32)
     second_in = flat_in + mixed_rows
     scale_two = lax.rsqrt(jnp.mean(second_in * second_in, axis=1, keepdims=True) + epsilon)
     normed_two = second_in * scale_two
@@ -1647,24 +1753,28 @@
         )
         return (from_q + from_k + from_v).astype(jnp.bfloat16)
 
-    grad_first = share_rows(dense and 5, input_term, tok_count).astype(jnp.float32)
-    attn_gain_grad = jnp.sum(grad_first * normed_one, axis=0)
-    grad_normed_one = grad_first * attn_gain
-    grad_x = grad_mid + scale_one * (
-        grad_normed_one - normed_one * jnp.mean(grad_normed_one * normed_one, axis=1, keepdims=True)
-    )
+    if dense:
+        attn_gain_grad = jnp.zeros_like(mlp_gain_grad)
+    else:
+        grad_first = share_rows(input_term, tok_count).astype(jnp.float32)
+        attn_gain_grad = jnp.sum(grad_first * normed_one, axis=0)
     narrow = (mixer_grad, out_grad.astype(jnp.bfloat16))
     gains = jnp.concatenate([attn_gain_grad[None], mlp_gain_grad[None], router_grad], axis=0)
     head_gains = jnp.stack([q_gain_grad, k_gain_grad])
     if dense:
-        narrow, gains, head_gains, forward, expert_grads = sum_grads(
-            narrow, gains, head_gains, block_output, expert_grads, w_gate.shape[0], nz
+        first = input_term(jnp.int32(0), group_len)
+        narrow, gains, head_gains, forward, expert_grads, grad_first = sum_grads(
+            narrow, gains, head_gains, block_output, expert_grads, first, normed_one, w_gate.shape[0], nz
         )
         block_output = (second_in + forward).astype(jnp.bfloat16)[None]
     else:
         narrow = lax.psum(narrow, "expert")
         head_gains = lax.psum(head_gains, "expert")
         gains = lax.psum(gains, ("fsdp", "expert"))
+    grad_normed_one = grad_first * attn_gain
+    grad_x = grad_mid + scale_one * (
+        grad_normed_one - normed_one * jnp.mean(grad_normed_one * normed_one, axis=1, keepdims=True)
+    )
     wide = tuple(jnp.split(narrow[0], 3, axis=1)) + (narrow[1],)
     mixer = tuple(g.astype(jnp.float32) for g in wide) + (head_gains[0], head_gains[1])
     return (

time: 649 us -> 629 us (0.969)
  Pallas kernels: 526 us -> 500 us
    pallas_call x1, Pallas kernels: 125 us -> 102 us  [scatter_act(): pl.pallas_call(functools.partial(scatter_act_kernel, nz), out_shape=(jax....]
    pallas_call x2 -> x1, Pallas kernels: 48.3 us -> 31 us  [square_scatter(): pl.pallas_call(square_scatter_kernel, out_shape=jax.ShapeDtypeStruct((r,...]
    pallas_call x1, Pallas kernels: 108 us -> 116 us  [gather_act(): pl.pallas_call(functools.partial(gather_act_kernel, nz), out_shape=(jax.S...]
    pallas_call x1, Pallas kernels: 183 us -> 190 us  [line_sum(): pl.pallas_call(functools.partial(line_sum_kernel, nz, counts), out_shape=...]
    unnamed x161 -> x169, local copies, waits for them, and re-layouts: 17.2 us -> 16.8 us
  transfers between devices with their start and end apart: 1 -> 1, of which waited for: 0 -> 0; matrix products, arithmetic and copies ran while one was open for 4% -> 4% of each run, Pallas kernels for 27% -> 29%
where the time goes in v5:
time: 629 us; the launch traced here: 618 us
  Pallas kernels  500 us (79%)
  matrix products  45.6 us (7%)
  other arithmetic  32.1 us (5%)
  local copies, waits for them, and re-layouts  24.2 us (4%)
  between operations  15.6 us (2%)
    pallas_call x1, Pallas kernels, line_sum(): pl.pallas_call(functools.partial(line_sum_kernel, nz, counts), out_shape=...  190 us
    pallas_call x1, Pallas kernels, gather_act(): pl.pallas_call(functools.partial(gather_act_kernel, nz), out_shape=(jax.S...  116 us
    pallas_call x1, Pallas kernels, scatter_act(): pl.pallas_call(functools.partial(scatter_act_kernel, nz), out_shape=(jax....  102 us
    pallas_call x2, Pallas kernels, square_gather(): pl.pallas_call(square_gather_kernel, out_shape=(jax.ShapeDtypeStruct((4,...  48.6 us
    pallas_call x1, Pallas kernels, square_scatter(): pl.pallas_call(square_scatter_kernel, out_shape=jax.ShapeDtypeStruct((r,...  31 us
    unnamed x169, local copies, waits for them, and re-layouts  16.8 us
  transfers between devices with their start and end apart: 1, of which 0 were waited for; matrix products, arithmetic and copies ran while one was open for 4% of the time, Pallas kernels for 29%

profile of v5, /device:TPU:0, one launch (start us, length us, event | category | flops | bytes accessed | tf_op | source)
XLA Modules:
  0.0 617.9 jit_solution(13492850127364826033)
XLA Ops:
  7.9 1.2 fusion.17
  9.7 2.2 fusion.9
  11.9 1.2 tile.5.ids
  13.2 28.2 %square_gather.2 = (bf16[4,128,2048]{2,1,0:T(8,128)(2,1)}, s32[4,8,128]{2,1,0:T(8,128)}) custom-call(bf16[128,2048]{1,0:T(8,128)(2,1)} %get-tuple-element.74.own, s32[8,128]{1,0:T(8,128)} %tile.5.ids), custom_call_target="tpu_custom_call" | custom-call | bytes 62914560 | tf_op jit(solution)/shard_map/square_gather/pallas_call | solution.py:813
  41.4 3.7 multiply_reduce_fusion.7
  45.1 1.3 multiply_reduce_fusion.6
  47.1 6.2 %square_sum.2 = f32[8,128]{1,0:T(8,128)} custom-call(f32[8,128]{1,0:T(8,128)} %reshape.348.own), custom_call_target="tpu_custom_call" | custom-call | bytes 10485760 | tf_op jit(solution)/shard_map/square_sum/pallas_call | solution.py:900
  54.3 1.8 broadcast_multiply_fusion.3
  56.0 0.8 rsqrt_bitcast_fusion
  58.3 1.0 fusion
  59.3 0.9 exponential_reduce_fusion
  60.3 2.1 copy-done.77
  62.4 1.3 convolution_convert_fusion.4
  63.7 1.4 convolution_convert_fusion.6
  65.6 2.6 convolution_convert_fusion.2
  68.2 31.0 %square_scatter.1 = f32[128,2048]{1,0:T(8,128)} custom-call(bf16[4,128,2048]{2,1,0:T(8,128)(2,1)} %bitcast.181), custom_call_target="tpu_custom_call" | custom-call | bytes 62914560 | tf_op jit(solution)/shard_map/square_scatter/pallas_call | solution.py:873
  99.8 1.4 multiply_reduce_fusion.5
  102.2 115.7 %gather_act.1 = (bf16[4,8,128,2048]{3,2,1,0:T(8,128)(2,1)}, f32[3,4,8,128,512]{4,3,2,1,0:T(8,128)}, bf16[4,8,128,512]{3,2,1,0:T(8,128)(2,1)}, bf16[4,8,128,2048]{3,2,1,0:T(8,128)(2,1)}, f32[2,4,4,16,128]{4,3,2,1,0:T(8,128)S(1)}) custom-call(bf16[128,2048]{1,0:T(8,128)(2,1)S(1)} %multiply_convert_fusion.3.own, f32[16,128]{1,0:T(8,128)S(1)} %get-tuple-element.101.own_small, ...), custom_call_target="tpu_custom_call" | custom-call | bytes 251658240 | tf_op jit(solution)/shard_map/gather_act/pallas_call | solution.py:402
  219.2 102.1 %scatter_act.1 = (f32[128,2048]{1,0:T(8,128)}, f32[16,128]{1,0:T(8,128)}, bf16[2,4,8,128,512]{4,3,2,1,0:T(8,128)(2,1)}) custom-call(f32[3,4,8,128,512]{4,3,2,1,0:T(8,128)} %get-tuple-element.35.pre, bf16[4,8,128,2048]{3,2,1,0:T(8,128)(2,1)} %bitcast.166, f32[2,4,4,16,128]{4,3,2,1,0:T(8,128)} %copy-done.3, bf16[2,2048,256]{2,1,0:T(8,128)(2,1)} %w_gate.3, ...), custom_call_target="tpu_custom_call" | custom-call | bytes 314572800 | tf_op jit(solution)/shard_map/scatter_act/pallas_call | solution.py:741
  321.3 0.7 multiply_reduce_fusion.8
  322.1 2.8 multiply_reduce_fusion.1
  324.9 1.0 copy-done.13
  325.9 2.2 fusion.40.own
  328.1 20.4 %square_gather.3 = (bf16[4,128,2048]{2,1,0:T(8,128)(2,1)}, s32[4,8,128]{2,1,0:T(8,128)}) custom-call(bf16[128,2048]{1,0:T(8,128)(2,1)} %fusion.40.own, s32[8,128]{1,0:T(8,128)} %tile.5.ids), custom_call_target="tpu_custom_call" | custom-call | bytes 62914560 | tf_op jit(solution)/shard_map/square_gather/pallas_call | solution.py:813
  348.4 3.7 convolution_convert_fusion.3
  352.1 1.6 multiply_reduce_fusion
  353.8 2.2 convolution_convert_fusion.5
  356.4 2.6 convolution_convert_fusion.1
  359.0 1.3 multiply_convert_fusion
  360.3 0.8 convolution_bitcast_fusion
  364.7 5.9 square_sum.3
  370.5 0.8 multiply_bitcast_fusion.1
  371.3 1.6 multiply_convert_fusion.2
  372.9 5.3 fusion.45
  378.5 3.3 fusion.46
  382.9 8.1 %convolution_convert_fusion = bf16[2048,1536]{1,0:T(8,128)(2,1)} fusion(bf16[512,2048]{1,0:T(8,128)(2,1)} %bitcast.208, bf16[512,512]{0,1:T(8,128)(2,1)S(1)} %bitcast.185, bf16[512,512]{0,1:T(8,128)(2,1)S(1)} %multiply_convert_fusion.1, bf16[512,512]{0,1:T(8,128)(2,1)S(1)} %copy-done.29), kind=kOutput, calls=%fused_computation | convolution fusion | flops 3229089792 | bytes 9961472 | tf_op jit(solution)/shard_map/td,ti->di/dot_general | solution.py:1742
  391.0 2.7 add_convert_fusion
  393.7 190.2 %line_sum.1 = (bf16[16,2,4,16,1536]{4,3,2,1,0:T(8,128)(2,1)}, bf16[4,2,4,16,2048]{4,3,2,1,0:T(8,128)(2,1)}, f32[2,4,4,16,128]{4,3,2,1,0:T(8,128)}, f32[128,2048]...) custom-call(bf16[16,2,4,16,1536]{4,3,2,1,0:T(8,128)(2,1)} %bitcast.1, ...), custom_call_target="tpu_custom_call" | custom-call | bytes 314572800 | tf_op jit(solution)/shard_map/line_sum/pallas_call | solution.py:1312
  584.0 1.0 copy.59
  585.7 8.3 %slice_convert_fusion = (f32[2048,512]{1,0:T(8,128)}, f32[2048,512]{1,0:T(8,128)}, f32[2048,512]{1,0:T(8,128)}) fusion(bf16[2048,1536]{1,0:T(8,128)(2,1)} %bitcast.177), kind=kLoop, calls=%fused_computation.12 | loop fusion | flops 3145728 | bytes 18874368 | tf_op jit(solution)/shard_map/convert_element_type | solution.py:1779
  594.1 2.8 bitcast_convert_fusion
  597.2 1.7 fusion.43
  598.9 1.6 fusion.16
  601.2 2.1 copy.63
  603.4 1.6 copy-done.26
  604.9 2.1 copy.64
  607.1 1.6 copy-done.25
  608.6 2.0 copy.65
  (209 shorter events, 14.3 us)
Async XLA Ops:
  7.2 94.2 %copy-start = (bf16[2048,16]{0,1:T(8,128)(2,1)S(1)}, bf16[2048,16]{0,1:T(8,128)(2,1)}, u32[]{:S(2)}) copy-start(bf16[2048,16]{0,1:T(8,128)(2,1)} %param.27) | copy-start | bytes 196612
  7.2 212.0 %all-gather.3.cloned.1.call-start = ((), (), s32[]{:S(2)}) async-start(), calls=%async_computation | async-start | bytes 17301504 | tf_op jit(solution)/shard_map/all_gather | solution.py:1555
  41.4 3.7 copy-start.33
  41.4 3.7 copy-start.76
  45.1 13.1 %copy-start.17 = (f32[512,512]{0,1:T(8,128)}, f32[512,512]{0,1:T(8,128)S(1)}, u32[]{:S(2)}) copy-start(f32[512,512]{0,1:T(8,128)S(1)} %get-tuple-element.96) | copy-start | bytes 3145732
  45.1 11.9 %copy-start.58 = (f32[512]{0:T(512)S(1)}, f32[512]{0:T(512)}, u32[]{:S(2)}) copy-start(f32[512]{0:T(512)} %param.23) | copy-start | bytes 6148
  46.5 11.1 %copy-start.15 = (f32[512,512]{0,1:T(8,128)}, f32[512,512]{0,1:T(8,128)S(1)}, u32[]{:S(2)}) copy-start(f32[512,512]{0,1:T(8,128)S(1)} %get-tuple-element.94) | copy-start | bytes 3145732
  46.5 10.8 %copy-start.60 = (f32[512]{0:T(512)S(1)}, f32[512]{0:T(512)}, u32[]{:S(2)}) copy-start(f32[512]{0:T(512)} %param.24) | copy-start | bytes 6148
  58.3 4.1 copy-start.77
  59.3 4.4 copy-start.4
  62.4 291.4 %copy-start.49 = (f32[4,512]{1,0:T(4,128)}, f32[4,512]{1,0:T(4,128)S(1)}, u32[]{:S(2)}) copy-start(f32[4,512]{1,0:T(4,128)S(1)} %log_add_fusion) | copy-start | bytes 24580
  63.7 4.5 copy-start.39
  65.6 33.6 %copy-start.79 = (s32[16]{0:T(128)S(1)}, s32[16]{0:T(128)}, u32[]{:S(2)}) copy-start(s32[16]{0:T(128)} %param.33) | copy-start | bytes 196
  65.6 34.2 %copy-start.70 = (s32[1,128,8]{1,2,0:T(8,128)S(1)}, s32[1,128,8]{1,2,0:T(8,128)}, u32[]{:S(2)}) copy-start(s32[1,128,8]{1,2,0:T(8,128)} %param.32) | copy-start | bytes 12292
  65.6 34.2 %copy-start.11 = (bf16[1,128,2048]{2,1,0:T(8,128)(2,1)S(1)}, bf16[1,128,2048]{2,1,0:T(8,128)(2,1)}, u32[]{:S(2)}) copy-start(bf16[1,128,2048]{2,1,0:T(8,128)(2,1)} %param.17) | copy-start | bytes 1572868
  68.2 33.1 %copy-start.43 = (f32[2048]{0:T(1024)S(1)}, f32[2048]{0:T(1024)}, u32[]{:S(2)}) copy-start(f32[2048]{0:T(1024)} %param.26) | copy-start | bytes 24580
  68.2 34.0 %copy-start.2 = (bf16[2,2048,256]{2,1,0:T(8,128)(2,1)S(1)}, bf16[2,2048,256]{2,1,0:T(8,128)(2,1)}, u32[]{:S(2)}) copy-start(bf16[2,2048,256]{2,1,0:T(8,128)(2,1)} %w_gate.3) | copy-start | bytes 6291460
  99.8 222.3 %copy-start.47 = (pred[128,16]{0,1:T(8,128)(4,1)}, pred[128,16]{0,1:T(8,128)(4,1)S(1)}, u32[]{:S(2)}) copy-start(pred[128,16]{0,1:T(8,128)(4,1)S(1)} %fusion.29) | copy-start | bytes 6148
  101.2 223.6 %copy-start.64 = (f32[128]{0:T(128)}, f32[128]{0:T(128)S(1)}, u32[]{:S(2)}) copy-start(f32[128]{0:T(128)S(1)} %add_rsqrt_fusion) | copy-start | bytes 1540
  101.7 220.3 %copy-start.41 = (f32[128,16]{0,1:T(8,128)}, f32[128,16]{0,1:T(8,128)S(1)}, u32[]{:S(2)}) copy-start(f32[128,16]{0,1:T(8,128)S(1)} %get-tuple-element.100) | copy-start | bytes 24580
  101.7 220.3 %copy-start.62 = (f32[128]{0:T(128)}, f32[128]{0:T(128)S(1)}, u32[]{:S(2)}) copy-start(f32[128]{0:T(128)S(1)} %get-tuple-element.99) | copy-start | bytes 1540
  101.7 220.3 %copy-start.66 = (f32[128]{0:T(128)}, f32[128]{0:T(128)S(1)}, u32[]{:S(2)}) copy-start(f32[128]{0:T(128)S(1)} %fusion.35) | copy-start | bytes 1540
  101.9 220.2 %copy-start.56 = (pred[128,16]{0,1:T(8,128)(4,1)}, pred[128,16]{0,1:T(8,128)(4,1)S(1)}, u32[]{:S(2)}) copy-start(pred[128,16]{0,1:T(8,128)(4,1)S(1)} %get-tuple-element.102) | copy-start | bytes 6148
  219.2 102.9 %copy-start.9 = (f32[128,2048]{1,0:T(8,128)S(1)}, f32[128,2048]{1,0:T(8,128)}, u32[]{:S(2)}) copy-start(f32[128,2048]{1,0:T(8,128)} %copy-done.8) | copy-start | bytes 3145732
  324.9 27.2 %copy-start.71 = (f32[128]{0:T(128)}, f32[128]{0:T(128)S(1)}, u32[]{:S(2)}) copy-start(f32[128]{0:T(128)S(1)} %broadcast_multiply_fusion.6) | copy-start | bytes 1540
  328.1 24.1 %copy-start.40 = (bf16[512,512]{0,1:T(8,128)(2,1)S(1)}, bf16[512,512]{0,1:T(8,128)(2,1)}, u32[]{:S(2)}) copy-start(bf16[512,512]{0,1:T(8,128)(2,1)} %copy-done.39) | copy-start | bytes 1572868
  348.4 3.7 copy-start.5
  372.9 5.4 copy-start.28
  372.9 5.6 copy-start.34
  378.5 3.5 copy-start.51
  378.5 3.5 copy-start.73
  378.5 4.3 copy-start.29
  378.5 4.3 copy-start.38
  382.9 8.1 %copy-start.6 = (f32[512,2048]{1,0:T(8,128)S(1)}, f32[512,2048]{1,0:T(8,128)}, u32[]{:S(2)}) copy-start(f32[512,2048]{1,0:T(8,128)} %fusion.45) | copy-start | bytes 12582916
  382.9 8.1 %copy-start.7 = (f32[512,2048]{1,0:T(8,128)S(1)}, f32[512,2048]{1,0:T(8,128)}, u32[]{:S(2)}) copy-start(f32[512,2048]{1,0:T(8,128)} %fusion.46) | copy-start | bytes 12582916
  382.9 8.1 %copy-start.31 = (bf16[2048,512]{1,0:T(8,128)(2,1)S(1)}, bf16[2048,512]{1,0:T(8,128)(2,1)}, u32[]{:S(2)}) copy-start(bf16[2048,512]{1,0:T(8,128)(2,1)} %param.21) | copy-start | bytes 6291460
  585.7 8.4 %copy-start.32 = (bf16[4,2,4,16,2048]{4,3,2,1,0:T(8,128)(2,1)S(1)}, bf16[4,2,4,16,2048]{4,3,2,1,0:T(8,128)(2,1)}, u32[]{:S(2)}) copy-start(bf16[4,2,4,16,2048]{4,3,2,1,0:T(8,128)(2,1)} %get-tuple-element.47) | copy-start | bytes 6291460
  594.0 4.9 copy-start.10
  594.0 4.9 copy-start.14
  594.0 4.9 copy-start.19
  594.0 4.9 copy-start.36
  594.0 4.9 copy-start.44
  594.0 4.9 copy-start.65
  594.0 4.9 copy-start.72
  596.9 4.4 copy-start.27
  601.2 3.7 copy-start.26
  604.9 3.7 copy-start.25
  604.9 5.7 copy-start.1
  (35 other events, 67.0 us)
Sparse Core Ops, SparseCore 0:
  11.0 136.6 all-gather.2

commit v6 on v5

--- a/solution.py
+++ b/solution.py
@@ -1104,7 +1104,7 @@
     part_small[...] = table_in[...]
     total = sum(counts)
     last = nz - 1
-    lag, per = 2, 5
+    lag, per = 1, 5
 
     class Piece:
         def __init__(self, k, p):
@@ -1583,7 +1583,7 @@
     share = -(-table.size // (2 * shards * nz * 1024)) * 8
     small = jnp.pad(table.reshape(-1), (0, 2 * shards * nz * share * 128 - table.size))
     small = small.reshape(2, shards, nz, share, 128)
-    parts = [g.reshape(-1, 2, nz, 16, g.shape[1]) for g in narrow]
+    parts = [g.reshape(-1, 2, nz, 32, g.shape[1]) for g in narrow]
     first = first.reshape(shards, -1, width)
     *sums, small, rows, gate, up, down, first = line_sum(
         parts, small, rows, inputs, first, normed.astype(jnp.bfloat16), local, nz, 9

time: 629 us -> 620 us (0.986)
  Pallas kernels: 500 us -> 490 us
    pallas_call x1, Pallas kernels: 190 us -> 181 us  [line_sum(): pl.pallas_call(functools.partial(line_sum_kernel, nz, counts), out_shape=...]
  transfers between devices with their start and end apart: 1 -> 1, of which waited for: 0 -> 0; matrix products, arithmetic and copies ran while one was open for 4% -> 4% of each run, Pallas kernels for 29% -> 30%
where the time goes in v6:
time: 620 us; the launch traced here: 608 us
  Pallas kernels  490 us (79%)
  matrix products  45.6 us (7%)
  other arithmetic  32.1 us (5%)
  local copies, waits for them, and re-layouts  24.2 us (4%)
  between operations  15.6 us (3%)
    pallas_call x1, Pallas kernels, line_sum(): pl.pallas_call(functools.partial(line_sum_kernel, nz, counts), out_shape=...  181 us
    pallas_call x1, Pallas kernels, gather_act(): pl.pallas_call(functools.partial(gather_act_kernel, nz), out_shape=(jax.S...  116 us
    pallas_call x1, Pallas kernels, scatter_act(): pl.pallas_call(functools.partial(scatter_act_kernel, nz), out_shape=(jax....  102 us
    pallas_call x2, Pallas kernels, square_gather(): pl.pallas_call(square_gather_kernel, out_shape=(jax.ShapeDtypeStruct((4,...  48.6 us
    pallas_call x1, Pallas kernels, square_scatter(): pl.pallas_call(square_scatter_kernel, out_shape=jax.ShapeDtypeStruct((r,...  31 us
    unnamed x169, local copies, waits for them, and re-layouts  16.8 us
  transfers between devices with their start and end apart: 1, of which 0 were waited for; matrix products, arithmetic and copies ran while one was open for 4% of the time, Pallas kernels for 30%

profile of v6, /device:TPU:0, one launch (start us, length us, event | category | flops | bytes accessed | tf_op | source)
XLA Modules:
  0.0 608.4 jit_solution(14995311166983023378)
XLA Ops:
  7.9 1.2 fusion.17
  9.7 2.2 fusion.9
  11.9 1.2 tile.5.ids
  13.2 28.2 %square_gather.2 = (bf16[4,128,2048]{2,1,0:T(8,128)(2,1)}, s32[4,8,128]{2,1,0:T(8,128)}) custom-call(bf16[128,2048]{1,0:T(8,128)(2,1)} %get-tuple-element.74.own, s32[8,128]{1,0:T(8,128)} %tile.5.ids), custom_call_target="tpu_custom_call" | custom-call | bytes 62914560 | tf_op jit(solution)/shard_map/square_gather/pallas_call | solution.py:813
  41.4 3.7 multiply_reduce_fusion.7
  45.1 1.3 multiply_reduce_fusion.6
  47.1 6.2 %square_sum.2 = f32[8,128]{1,0:T(8,128)} custom-call(f32[8,128]{1,0:T(8,128)} %reshape.348.own), custom_call_target="tpu_custom_call" | custom-call | bytes 10485760 | tf_op jit(solution)/shard_map/square_sum/pallas_call | solution.py:900
  54.3 1.8 broadcast_multiply_fusion.3
  56.0 0.8 rsqrt_bitcast_fusion
  58.3 1.0 fusion
  59.3 0.9 exponential_reduce_fusion
  60.3 2.1 copy-done.77
  62.4 1.3 convolution_convert_fusion.4
  63.7 1.4 convolution_convert_fusion.6
  65.6 2.6 convolution_convert_fusion.2
  68.2 31.0 %square_scatter.1 = f32[128,2048]{1,0:T(8,128)} custom-call(bf16[4,128,2048]{2,1,0:T(8,128)(2,1)} %bitcast.181), custom_call_target="tpu_custom_call" | custom-call | bytes 62914560 | tf_op jit(solution)/shard_map/square_scatter/pallas_call | solution.py:873
  99.8 1.4 multiply_reduce_fusion.5
  102.2 115.7 %gather_act.1 = (bf16[4,8,128,2048]{3,2,1,0:T(8,128)(2,1)}, f32[3,4,8,128,512]{4,3,2,1,0:T(8,128)}, bf16[4,8,128,512]{3,2,1,0:T(8,128)(2,1)}, bf16[4,8,128,2048]{3,2,1,0:T(8,128)(2,1)}, f32[2,4,4,16,128]{4,3,2,1,0:T(8,128)S(1)}) custom-call(bf16[128,2048]{1,0:T(8,128)(2,1)S(1)} %multiply_convert_fusion.3.own, f32[16,128]{1,0:T(8,128)S(1)} %get-tuple-element.101.own_small, ...), custom_call_target="tpu_custom_call" | custom-call | bytes 251658240 | tf_op jit(solution)/shard_map/gather_act/pallas_call | solution.py:402
  219.2 102.1 %scatter_act.1 = (f32[128,2048]{1,0:T(8,128)}, f32[16,128]{1,0:T(8,128)}, bf16[2,4,8,128,512]{4,3,2,1,0:T(8,128)(2,1)}) custom-call(f32[3,4,8,128,512]{4,3,2,1,0:T(8,128)} %get-tuple-element.35.pre, bf16[4,8,128,2048]{3,2,1,0:T(8,128)(2,1)} %bitcast.166, f32[2,4,4,16,128]{4,3,2,1,0:T(8,128)} %copy-done.3, bf16[2,2048,256]{2,1,0:T(8,128)(2,1)} %w_gate.3, ...), custom_call_target="tpu_custom_call" | custom-call | bytes 314572800 | tf_op jit(solution)/shard_map/scatter_act/pallas_call | solution.py:741
  321.3 0.7 multiply_reduce_fusion.8
  322.1 2.8 multiply_reduce_fusion.1
  324.9 1.0 copy-done.13
  325.9 2.2 fusion.40.own
  328.1 20.4 %square_gather.3 = (bf16[4,128,2048]{2,1,0:T(8,128)(2,1)}, s32[4,8,128]{2,1,0:T(8,128)}) custom-call(bf16[128,2048]{1,0:T(8,128)(2,1)} %fusion.40.own, s32[8,128]{1,0:T(8,128)} %tile.5.ids), custom_call_target="tpu_custom_call" | custom-call | bytes 62914560 | tf_op jit(solution)/shard_map/square_gather/pallas_call | solution.py:813
  348.4 3.7 convolution_convert_fusion.3
  352.1 1.6 multiply_reduce_fusion
  353.8 2.2 convolution_convert_fusion.5
  356.4 2.6 convolution_convert_fusion.1
  359.0 1.3 multiply_convert_fusion
  360.3 0.8 convolution_bitcast_fusion
  364.7 5.9 square_sum.3
  370.5 0.8 multiply_bitcast_fusion.1
  371.3 1.6 multiply_convert_fusion.2
  372.9 5.3 fusion.45
  378.5 3.3 fusion.46
  382.9 8.1 %convolution_convert_fusion = bf16[2048,1536]{1,0:T(8,128)(2,1)} fusion(bf16[512,2048]{1,0:T(8,128)(2,1)} %bitcast.208, bf16[512,512]{0,1:T(8,128)(2,1)S(1)} %bitcast.185, bf16[512,512]{0,1:T(8,128)(2,1)S(1)} %multiply_convert_fusion.1, bf16[512,512]{0,1:T(8,128)(2,1)S(1)} %copy-done.29), kind=kOutput, calls=%fused_computation | convolution fusion | flops 3229089792 | bytes 9961472 | tf_op jit(solution)/shard_map/td,ti->di/dot_general | solution.py:1742
  391.0 2.7 add_convert_fusion
  393.7 180.7 %line_sum.1 = (bf16[8,2,4,32,1536]{4,3,2,1,0:T(8,128)(2,1)}, bf16[2,2,4,32,2048]{4,3,2,1,0:T(8,128)(2,1)}, f32[2,4,4,16,128]{4,3,2,1,0:T(8,128)}, f32[128,2048]{...) custom-call(bf16[8,2,4,32,1536]{4,3,2,1,0:T(8,128)(2,1)} %bitcast.17, ...), custom_call_target="tpu_custom_call" | custom-call | bytes 314572800 | tf_op jit(solution)/shard_map/line_sum/pallas_call | solution.py:1312
  574.4 1.0 copy.59
  576.2 8.3 %slice_convert_fusion = (f32[2048,512]{1,0:T(8,128)}, f32[2048,512]{1,0:T(8,128)}, f32[2048,512]{1,0:T(8,128)}) fusion(bf16[2048,1536]{1,0:T(8,128)(2,1)} %bitcast.177), kind=kLoop, calls=%fused_computation.12 | loop fusion | flops 3145728 | bytes 18874368 | tf_op jit(solution)/shard_map/convert_element_type | solution.py:1779
  584.5 2.8 bitcast_convert_fusion
  587.7 1.7 fusion.43
  589.4 1.6 fusion.16
  591.7 2.1 copy.63
  593.8 1.6 copy-done.26
  595.4 2.1 copy.64
  597.6 1.6 copy-done.25
  599.1 2.0 copy.65
  (209 shorter events, 14.3 us)
Async XLA Ops:
  7.2 94.2 %copy-start = (bf16[2048,16]{0,1:T(8,128)(2,1)S(1)}, bf16[2048,16]{0,1:T(8,128)(2,1)}, u32[]{:S(2)}) copy-start(bf16[2048,16]{0,1:T(8,128)(2,1)} %param.27) | copy-start | bytes 196612
  7.2 212.0 %all-gather.3.cloned.1.call-start = ((), (), s32[]{:S(2)}) async-start(), calls=%async_computation | async-start | bytes 17301504 | tf_op jit(solution)/shard_map/all_gather | solution.py:1555
  41.4 3.7 copy-start.33
  41.4 3.7 copy-start.76
  45.1 13.1 %copy-start.17 = (f32[512,512]{0,1:T(8,128)}, f32[512,512]{0,1:T(8,128)S(1)}, u32[]{:S(2)}) copy-start(f32[512,512]{0,1:T(8,128)S(1)} %get-tuple-element.96) | copy-start | bytes 3145732
  45.1 11.9 %copy-start.58 = (f32[512]{0:T(512)S(1)}, f32[512]{0:T(512)}, u32[]{:S(2)}) copy-start(f32[512]{0:T(512)} %param.23) | copy-start | bytes 6148
  46.5 11.1 %copy-start.15 = (f32[512,512]{0,1:T(8,128)}, f32[512,512]{0,1:T(8,128)S(1)}, u32[]{:S(2)}) copy-start(f32[512,512]{0,1:T(8,128)S(1)} %get-tuple-element.94) | copy-start | bytes 3145732
  46.5 10.8 %copy-start.60 = (f32[512]{0:T(512)S(1)}, f32[512]{0:T(512)}, u32[]{:S(2)}) copy-start(f32[512]{0:T(512)} %param.24) | copy-start | bytes 6148
  58.3 4.1 copy-start.77
  59.3 4.4 copy-start.4
  62.4 291.4 %copy-start.49 = (f32[4,512]{1,0:T(4,128)}, f32[4,512]{1,0:T(4,128)S(1)}, u32[]{:S(2)}) copy-start(f32[4,512]{1,0:T(4,128)S(1)} %log_add_fusion) | copy-start | bytes 24580
  63.7 4.5 copy-start.39
  65.6 33.6 %copy-start.79 = (s32[16]{0:T(128)S(1)}, s32[16]{0:T(128)}, u32[]{:S(2)}) copy-start(s32[16]{0:T(128)} %param.33) | copy-start | bytes 196
  65.6 34.2 %copy-start.70 = (s32[1,128,8]{1,2,0:T(8,128)S(1)}, s32[1,128,8]{1,2,0:T(8,128)}, u32[]{:S(2)}) copy-start(s32[1,128,8]{1,2,0:T(8,128)} %param.32) | copy-start | bytes 12292
  65.6 34.2 %copy-start.11 = (bf16[1,128,2048]{2,1,0:T(8,128)(2,1)S(1)}, bf16[1,128,2048]{2,1,0:T(8,128)(2,1)}, u32[]{:S(2)}) copy-start(bf16[1,128,2048]{2,1,0:T(8,128)(2,1)} %param.17) | copy-start | bytes 1572868
  68.2 33.1 %copy-start.43 = (f32[2048]{0:T(1024)S(1)}, f32[2048]{0:T(1024)}, u32[]{:S(2)}) copy-start(f32[2048]{0:T(1024)} %param.26) | copy-start | bytes 24580
  68.2 34.0 %copy-start.2 = (bf16[2,2048,256]{2,1,0:T(8,128)(2,1)S(1)}, bf16[2,2048,256]{2,1,0:T(8,128)(2,1)}, u32[]{:S(2)}) copy-start(bf16[2,2048,256]{2,1,0:T(8,128)(2,1)} %w_gate.3) | copy-start | bytes 6291460
  99.8 222.3 %copy-start.47 = (pred[128,16]{0,1:T(8,128)(4,1)}, pred[128,16]{0,1:T(8,128)(4,1)S(1)}, u32[]{:S(2)}) copy-start(pred[128,16]{0,1:T(8,128)(4,1)S(1)} %fusion.29) | copy-start | bytes 6148
  101.2 223.6 %copy-start.64 = (f32[128]{0:T(128)}, f32[128]{0:T(128)S(1)}, u32[]{:S(2)}) copy-start(f32[128]{0:T(128)S(1)} %add_rsqrt_fusion) | copy-start | bytes 1540
  101.7 220.3 %copy-start.41 = (f32[128,16]{0,1:T(8,128)}, f32[128,16]{0,1:T(8,128)S(1)}, u32[]{:S(2)}) copy-start(f32[128,16]{0,1:T(8,128)S(1)} %get-tuple-element.100) | copy-start | bytes 24580
  101.7 220.3 %copy-start.62 = (f32[128]{0:T(128)}, f32[128]{0:T(128)S(1)}, u32[]{:S(2)}) copy-start(f32[128]{0:T(128)S(1)} %get-tuple-element.99) | copy-start | bytes 1540
  101.7 220.3 %copy-start.66 = (f32[128]{0:T(128)}, f32[128]{0:T(128)S(1)}, u32[]{:S(2)}) copy-start(f32[128]{0:T(128)S(1)} %fusion.35) | copy-start | bytes 1540
  101.9 220.2 %copy-start.56 = (pred[128,16]{0,1:T(8,128)(4,1)}, pred[128,16]{0,1:T(8,128)(4,1)S(1)}, u32[]{:S(2)}) copy-start(pred[128,16]{0,1:T(8,128)(4,1)S(1)} %get-tuple-element.102) | copy-start | bytes 6148
  219.2 102.9 %copy-start.9 = (f32[128,2048]{1,0:T(8,128)S(1)}, f32[128,2048]{1,0:T(8,128)}, u32[]{:S(2)}) copy-start(f32[128,2048]{1,0:T(8,128)} %copy-done.8) | copy-start | bytes 3145732
  324.9 27.2 %copy-start.71 = (f32[128]{0:T(128)}, f32[128]{0:T(128)S(1)}, u32[]{:S(2)}) copy-start(f32[128]{0:T(128)S(1)} %broadcast_multiply_fusion.6) | copy-start | bytes 1540
  328.1 24.1 %copy-start.40 = (bf16[512,512]{0,1:T(8,128)(2,1)S(1)}, bf16[512,512]{0,1:T(8,128)(2,1)}, u32[]{:S(2)}) copy-start(bf16[512,512]{0,1:T(8,128)(2,1)} %copy-done.39) | copy-start | bytes 1572868
  348.4 3.7 copy-start.5
  372.9 5.4 copy-start.28
  372.9 5.6 copy-start.34
  378.5 3.5 copy-start.51
  378.5 3.5 copy-start.73
  378.5 4.3 copy-start.29
  378.5 4.3 copy-start.38
  382.9 8.1 %copy-start.6 = (f32[512,2048]{1,0:T(8,128)S(1)}, f32[512,2048]{1,0:T(8,128)}, u32[]{:S(2)}) copy-start(f32[512,2048]{1,0:T(8,128)} %fusion.45) | copy-start | bytes 12582916
  382.9 8.1 %copy-start.7 = (f32[512,2048]{1,0:T(8,128)S(1)}, f32[512,2048]{1,0:T(8,128)}, u32[]{:S(2)}) copy-start(f32[512,2048]{1,0:T(8,128)} %fusion.46) | copy-start | bytes 12582916
  382.9 8.1 %copy-start.31 = (bf16[2048,512]{1,0:T(8,128)(2,1)S(1)}, bf16[2048,512]{1,0:T(8,128)(2,1)}, u32[]{:S(2)}) copy-start(bf16[2048,512]{1,0:T(8,128)(2,1)} %param.21) | copy-start | bytes 6291460
  576.2 8.4 %copy-start.32 = (bf16[2,2,4,32,2048]{4,3,2,1,0:T(8,128)(2,1)S(1)}, bf16[2,2,4,32,2048]{4,3,2,1,0:T(8,128)(2,1)}, u32[]{:S(2)}) copy-start(bf16[2,2,4,32,2048]{4,3,2,1,0:T(8,128)(2,1)} %get-tuple-element.47) | copy-start | bytes 6291460
  584.5 4.9 copy-start.10
  584.5 4.9 copy-start.14
  584.5 4.9 copy-start.19
  584.5 4.9 copy-start.36
  584.5 4.9 copy-start.44
  584.5 4.9 copy-start.65
  584.5 4.9 copy-start.72
  587.4 4.4 copy-start.27
  591.7 3.7 copy-start.26
  595.4 3.7 copy-start.25
  595.4 5.7 copy-start.1
  (35 other events, 67.0 us)
Sparse Core Ops, SparseCore 0:
  11.0 136.6 all-gather.2

commit v7 on v6

--- a/solution.py
+++ b/solution.py
@@ -1744,14 +1744,10 @@
     ).astype(jnp.bfloat16)
 
     def input_term(start, length):
-        from_q = jnp.einsum(
-            "ti,di->td", grad_query_rows, w_query, preferred_element_type=jnp.float32
-        )
-        from_k = jnp.einsum("ti,di->td", grad_key_rows, w_key, preferred_element_type=jnp.float32)
-        from_v = jnp.einsum(
-            "ti,di->td", grad_value_rows, w_value, preferred_element_type=jnp.float32
-        )
-        return (from_q + from_k + from_v).astype(jnp.bfloat16)
+        head_w = jnp.concatenate([w_query, w_key, w_value], axis=1)
+        return jnp.einsum(
+            "ti,di->td", head_grads, head_w, preferred_element_type=jnp.float32
+        ).astype(jnp.bfloat16)
 
     if dense:
         attn_gain_grad = jnp.zeros_like(mlp_gain_grad)

time: 620 us -> 615 us (level)
  matrix products: 45.6 us -> 39.3 us
    unnamed x169 -> x161, local copies, waits for them, and re-layouts: 16.8 us -> 16.7 us
where the time goes in v7:
time: 615 us; the launch traced here: 604 us
  Pallas kernels  490 us (80%)
  matrix products  39.3 us (6%)
  other arithmetic  33.4 us (5%)
  local copies, waits for them, and re-layouts  24.3 us (4%)
  between operations  15.6 us (3%)
    pallas_call x1, Pallas kernels, line_sum(): pl.pallas_call(functools.partial(line_sum_kernel, nz, counts), out_shape=...  181 us
    pallas_call x1, Pallas kernels, gather_act(): pl.pallas_call(functools.partial(gather_act_kernel, nz), out_shape=(jax.S...  116 us
    pallas_call x1, Pallas kernels, scatter_act(): pl.pallas_call(functools.partial(scatter_act_kernel, nz), out_shape=(jax....  102 us
    pallas_call x2, Pallas kernels, square_gather(): pl.pallas_call(square_gather_kernel, out_shape=(jax.ShapeDtypeStruct((4,...  48.7 us
    pallas_call x1, Pallas kernels, square_scatter(): pl.pallas_call(square_scatter_kernel, out_shape=jax.ShapeDtypeStruct((r,...  30.9 us
    unnamed x161, local copies, waits for them, and re-layouts  16.7 us
  transfers between devices with their start and end apart: 1, of which 0 were waited for; matrix products, arithmetic and copies ran while one was open for 4% of the time, Pallas kernels for 30%

profile of v7, /device:TPU:0, one launch (start us, length us, event | category | flops | bytes accessed | tf_op | source)
XLA Modules:
  0.0 603.6 jit_solution(3855937848776114523)
XLA Ops:
  7.9 1.2 fusion.21
  9.7 2.2 fusion.13
  11.9 1.2 tile.5.ids
  13.2 28.2 %square_gather.2 = (bf16[4,128,2048]{2,1,0:T(8,128)(2,1)}, s32[4,8,128]{2,1,0:T(8,128)}) custom-call(bf16[128,2048]{1,0:T(8,128)(2,1)} %get-tuple-element.74.own, s32[8,128]{1,0:T(8,128)} %tile.5.ids), custom_call_target="tpu_custom_call" | custom-call | bytes 62914560 | tf_op jit(solution)/shard_map/square_gather/pallas_call | solution.py:813
  41.4 3.7 multiply_reduce_fusion.7
  45.1 1.3 multiply_reduce_fusion.6
  47.1 6.2 %square_sum.2 = f32[8,128]{1,0:T(8,128)} custom-call(f32[8,128]{1,0:T(8,128)} %reshape.348.own), custom_call_target="tpu_custom_call" | custom-call | bytes 10485760 | tf_op jit(solution)/shard_map/square_sum/pallas_call | solution.py:900
  53.3 0.7 slice.80
  54.3 1.7 broadcast_multiply_fusion.3
  56.0 0.8 rsqrt_bitcast_fusion
  58.3 1.0 fusion.6
  59.3 0.9 exponential_reduce_fusion
  60.2 2.1 copy-done.71
  62.4 1.3 convolution_convert_fusion.4
  63.7 1.4 convolution_convert_fusion.6
  65.5 2.6 convolution_convert_fusion.2
  68.2 30.9 %square_scatter.1 = f32[128,2048]{1,0:T(8,128)} custom-call(bf16[4,128,2048]{2,1,0:T(8,128)(2,1)} %bitcast.175), custom_call_target="tpu_custom_call" | custom-call | bytes 62914560 | tf_op jit(solution)/shard_map/square_scatter/pallas_call | solution.py:873
  99.7 1.4 multiply_reduce_fusion.5
  102.1 115.7 %gather_act.1 = (bf16[4,8,128,2048]{3,2,1,0:T(8,128)(2,1)}, f32[3,4,8,128,512]{4,3,2,1,0:T(8,128)}, bf16[4,8,128,512]{3,2,1,0:T(8,128)(2,1)}, bf16[4,8,128,2048]{3,2,1,0:T(8,128)(2,1)}, f32[2,4,4,16,128]{4,3,2,1,0:T(8,128)S(1)}) custom-call(bf16[128,2048]{1,0:T(8,128)(2,1)S(1)} %multiply_convert_fusion.3.own, f32[16,128]{1,0:T(8,128)S(1)} %get-tuple-element.101.own_small, ...), custom_call_target="tpu_custom_call" | custom-call | bytes 251658240 | tf_op jit(solution)/shard_map/gather_act/pallas_call | solution.py:402
  219.1 102.2 %scatter_act.1 = (f32[128,2048]{1,0:T(8,128)}, f32[16,128]{1,0:T(8,128)}, bf16[2,4,8,128,512]{4,3,2,1,0:T(8,128)(2,1)}) custom-call(f32[3,4,8,128,512]{4,3,2,1,0:T(8,128)} %get-tuple-element.35.pre, bf16[4,8,128,2048]{3,2,1,0:T(8,128)(2,1)} %bitcast.160, f32[2,4,4,16,128]{4,3,2,1,0:T(8,128)} %copy-done.3, bf16[2,2048,256]{2,1,0:T(8,128)(2,1)} %w_gate.3, ...), custom_call_target="tpu_custom_call" | custom-call | bytes 314572800 | tf_op jit(solution)/shard_map/scatter_act/pallas_call | solution.py:741
  321.3 0.7 multiply_reduce_fusion.8
  322.0 2.8 multiply_reduce_fusion.1
  324.8 1.0 copy-done.11
  325.8 2.2 fusion.45.own
  328.0 20.5 %square_gather.3 = (bf16[4,128,2048]{2,1,0:T(8,128)(2,1)}, s32[4,8,128]{2,1,0:T(8,128)}) custom-call(bf16[128,2048]{1,0:T(8,128)(2,1)} %fusion.45.own, s32[8,128]{1,0:T(8,128)} %tile.5.ids), custom_call_target="tpu_custom_call" | custom-call | bytes 62914560 | tf_op jit(solution)/shard_map/square_gather/pallas_call | solution.py:813
  348.5 3.7 convolution_convert_fusion.3
  352.2 1.6 multiply_reduce_fusion
  353.9 2.2 convolution_convert_fusion.5
  356.4 2.1 multiply_convert_fusion
  358.5 0.8 convolution_bitcast_fusion
  362.9 5.9 square_sum.3
  368.8 0.8 multiply_bitcast_fusion.1
  369.6 2.0 multiply_convert_fusion.2
  371.9 6.8 %fusion.7 = bf16[512,2048]{1,0:T(8,128)(2,1)} fusion(bf16[2048,512]{1,0:T(8,128)(2,1)S(1)} %copy-done.67, bf16[2048,512]{1,0:T(8,128)(2,1)S(1)} %copy-done.69, bf16[2048,512]{1,0:T(8,128)(2,1)} %param.19, bf16[512,512]{0,1:T(8,128)(2,1)S(1)} %bitcast.207, bf16[512,512]{0,1:T(8,128)(2,1)S(1)} %multiply_convert_fusion.1, ...), kind=kOutput, calls=%fused_computation.13 | convolution fusion | flops 3245867008 | bytes 9961472 | tf_op jit(solution)/shard_map/ti,di->td/dot_general | solution.py:1748
  378.8 6.4 %convolution_convert_fusion = bf16[2048,1536]{1,0:T(8,128)(2,1)} fusion(bf16[512,2048]{1,0:T(8,128)(2,1)S(1)} %bitcast.202, bf16[512,512]{0,1:T(8,128)(2,1)S(1)} %bitcast.208, bf16[512,512]{0,1:T(8,128)(2,1)S(1)} %multiply_convert_fusion.1, bf16[512,512]{0,1:T(8,128)(2,1)S(1)} %multiply_convert_fusion.2), kind=kOutput, calls=%fused_computation | convolution fusion | flops 3229089792 | bytes 9961472 | tf_op jit(solution)/shard_map/td,ti->di/dot_general | solution.py:1742
  385.2 2.6 convolution_convert_fusion.1
  388.0 0.7 pad.9
  388.8 180.8 %line_sum.1 = (bf16[8,2,4,32,1536]{4,3,2,1,0:T(8,128)(2,1)}, bf16[2,2,4,32,2048]{4,3,2,1,0:T(8,128)(2,1)}, f32[2,4,4,16,128]{4,3,2,1,0:T(8,128)}, f32[128,2048]{...) custom-call(bf16[8,2,4,32,1536]{4,3,2,1,0:T(8,128)(2,1)} %bitcast.16, ...), custom_call_target="tpu_custom_call" | custom-call | bytes 314572800 | tf_op jit(solution)/shard_map/line_sum/pallas_call | solution.py:1312
  569.6 1.0 copy.59
  571.3 8.3 %slice_convert_fusion = (f32[2048,512]{1,0:T(8,128)}, f32[2048,512]{1,0:T(8,128)}, f32[2048,512]{1,0:T(8,128)}) fusion(bf16[2048,1536]{1,0:T(8,128)(2,1)} %bitcast.170), kind=kLoop, calls=%fused_computation.18 | loop fusion | flops 3145728 | bytes 18874368 | tf_op jit(solution)/shard_map/convert_element_type | solution.py:1775
  579.7 2.8 bitcast_convert_fusion
  582.8 1.7 fusion.48
  584.6 1.6 fusion.20
  586.9 2.1 copy.63
  589.0 1.6 copy-done.24
  590.6 2.1 copy.64
  592.7 1.6 copy-done.23
  594.3 2.0 copy.65
  (199 shorter events, 12.9 us)
Async XLA Ops:
  7.2 94.2 %copy-start = (bf16[2048,16]{0,1:T(8,128)(2,1)S(1)}, bf16[2048,16]{0,1:T(8,128)(2,1)}, u32[]{:S(2)}) copy-start(bf16[2048,16]{0,1:T(8,128)(2,1)} %param.27) | copy-start | bytes 196612
  7.2 211.9 %all-gather.3.cloned.1.call-start = ((), (), s32[]{:S(2)}) async-start(), calls=%async_computation | async-start | bytes 17301504 | tf_op jit(solution)/shard_map/all_gather | solution.py:1555
  41.4 3.7 copy-start.68
  41.4 3.7 copy-start.70
  45.1 13.1 %copy-start.15 = (f32[512,512]{0,1:T(8,128)}, f32[512,512]{0,1:T(8,128)S(1)}, u32[]{:S(2)}) copy-start(f32[512,512]{0,1:T(8,128)S(1)} %get-tuple-element.96) | copy-start | bytes 3145732
  45.1 11.9 %copy-start.48 = (f32[512]{0:T(512)S(1)}, f32[512]{0:T(512)}, u32[]{:S(2)}) copy-start(f32[512]{0:T(512)} %param.23) | copy-start | bytes 6148
  46.5 11.1 %copy-start.13 = (f32[512,512]{0,1:T(8,128)}, f32[512,512]{0,1:T(8,128)S(1)}, u32[]{:S(2)}) copy-start(f32[512,512]{0,1:T(8,128)S(1)} %get-tuple-element.94) | copy-start | bytes 3145732
  46.5 10.8 %copy-start.50 = (f32[512]{0:T(512)S(1)}, f32[512]{0:T(512)}, u32[]{:S(2)}) copy-start(f32[512]{0:T(512)} %param.24) | copy-start | bytes 6148
  58.3 4.1 copy-start.71
  59.3 4.4 copy-start.4
  62.4 291.4 %copy-start.40 = (f32[4,512]{1,0:T(4,128)}, f32[4,512]{1,0:T(4,128)S(1)}, u32[]{:S(2)}) copy-start(f32[4,512]{1,0:T(4,128)S(1)} %log_add_fusion) | copy-start | bytes 24580
  65.1 3.1 copy-start.75
  65.5 33.5 %copy-start.74 = (s32[16]{0:T(128)S(1)}, s32[16]{0:T(128)}, u32[]{:S(2)}) copy-start(s32[16]{0:T(128)} %param.33) | copy-start | bytes 196
  65.5 34.1 %copy-start.60 = (s32[1,128,8]{1,2,0:T(8,128)S(1)}, s32[1,128,8]{1,2,0:T(8,128)}, u32[]{:S(2)}) copy-start(s32[1,128,8]{1,2,0:T(8,128)} %param.32) | copy-start | bytes 12292
  65.5 34.1 %copy-start.9 = (bf16[1,128,2048]{2,1,0:T(8,128)(2,1)S(1)}, bf16[1,128,2048]{2,1,0:T(8,128)(2,1)}, u32[]{:S(2)}) copy-start(bf16[1,128,2048]{2,1,0:T(8,128)(2,1)} %param.17) | copy-start | bytes 1572868
  68.1 33.0 %copy-start.34 = (f32[2048]{0:T(1024)S(1)}, f32[2048]{0:T(1024)}, u32[]{:S(2)}) copy-start(f32[2048]{0:T(1024)} %param.26) | copy-start | bytes 24580
  68.2 34.0 %copy-start.2 = (bf16[2,2048,256]{2,1,0:T(8,128)(2,1)S(1)}, bf16[2,2048,256]{2,1,0:T(8,128)(2,1)}, u32[]{:S(2)}) copy-start(bf16[2,2048,256]{2,1,0:T(8,128)(2,1)} %w_gate.3) | copy-start | bytes 6291460
  99.7 222.3 %copy-start.38 = (pred[128,16]{0,1:T(8,128)(4,1)}, pred[128,16]{0,1:T(8,128)(4,1)S(1)}, u32[]{:S(2)}) copy-start(pred[128,16]{0,1:T(8,128)(4,1)S(1)} %fusion.33) | copy-start | bytes 6148
  101.2 223.7 %copy-start.54 = (f32[128]{0:T(128)}, f32[128]{0:T(128)S(1)}, u32[]{:S(2)}) copy-start(f32[128]{0:T(128)S(1)} %add_rsqrt_fusion) | copy-start | bytes 1540
  101.6 220.4 %copy-start.32 = (f32[128,16]{0,1:T(8,128)}, f32[128,16]{0,1:T(8,128)S(1)}, u32[]{:S(2)}) copy-start(f32[128,16]{0,1:T(8,128)S(1)} %get-tuple-element.100) | copy-start | bytes 24580
  101.6 220.4 %copy-start.52 = (f32[128]{0:T(128)}, f32[128]{0:T(128)S(1)}, u32[]{:S(2)}) copy-start(f32[128]{0:T(128)S(1)} %get-tuple-element.99) | copy-start | bytes 1540
  101.7 220.3 %copy-start.56 = (f32[128]{0:T(128)}, f32[128]{0:T(128)S(1)}, u32[]{:S(2)}) copy-start(f32[128]{0:T(128)S(1)} %fusion.39) | copy-start | bytes 1540
  101.8 220.2 %copy-start.46 = (pred[128,16]{0,1:T(8,128)(4,1)}, pred[128,16]{0,1:T(8,128)(4,1)S(1)}, u32[]{:S(2)}) copy-start(pred[128,16]{0,1:T(8,128)(4,1)S(1)} %get-tuple-element.102) | copy-start | bytes 6148
  219.1 102.9 %copy-start.7 = (f32[128,2048]{1,0:T(8,128)S(1)}, f32[128,2048]{1,0:T(8,128)}, u32[]{:S(2)}) copy-start(f32[128,2048]{1,0:T(8,128)} %copy-done.6) | copy-start | bytes 3145732
  324.8 27.3 %copy-start.61 = (f32[128]{0:T(128)}, f32[128]{0:T(128)S(1)}, u32[]{:S(2)}) copy-start(f32[128]{0:T(128)S(1)} %broadcast_multiply_fusion.6) | copy-start | bytes 1540
  328.0 24.2 %copy-start.31 = (bf16[512,512]{0,1:T(8,128)(2,1)S(1)}, bf16[512,512]{0,1:T(8,128)(2,1)}, u32[]{:S(2)}) copy-start(bf16[512,512]{0,1:T(8,128)(2,1)} %copy-done.30) | copy-start | bytes 1572868
  348.5 3.7 copy-start.5
  356.4 2.9 copy-start.19
  356.4 2.9 copy-start.27
  368.8 3.1 copy-start.67
  368.8 3.1 copy-start.69
  368.8 3.1 copy-start.77
  371.9 6.8 %copy-start.72 = (bf16[4,128,2048]{2,1,0:T(8,128)(2,1)S(1)}, bf16[4,128,2048]{2,1,0:T(8,128)(2,1)}, u32[]{:S(2)}) copy-start(bf16[4,128,2048]{2,1,0:T(8,128)(2,1)} %get-tuple-element.33) | copy-start | bytes 6291460
  378.7 6.4 %copy-start.73 = (bf16[4,128,2048]{2,1,0:T(8,128)(2,1)S(1)}, bf16[4,128,2048]{2,1,0:T(8,128)(2,1)}, u32[]{:S(2)}) copy-start(bf16[4,128,2048]{2,1,0:T(8,128)(2,1)} %get-tuple-element.39) | copy-start | bytes 6291460
  378.7 6.4 %copy-start.76 = (bf16[4,128,512]{2,1,0:T(8,128)(2,1)S(1)}, bf16[4,128,512]{2,1,0:T(8,128)(2,1)}, u32[]{:S(2)}) copy-start(bf16[4,128,512]{2,1,0:T(8,128)(2,1)} %copy-done.75) | copy-start | bytes 1572868
  571.3 8.4 %copy-start.26 = (bf16[2,2,4,32,2048]{4,3,2,1,0:T(8,128)(2,1)S(1)}, bf16[2,2,4,32,2048]{4,3,2,1,0:T(8,128)(2,1)}, u32[]{:S(2)}) copy-start(bf16[2,2,4,32,2048]{4,3,2,1,0:T(8,128)(2,1)} %get-tuple-element.47) | copy-start | bytes 6291460
  579.6 2.9 copy-start.59
  579.6 4.9 copy-start.8
  579.6 4.9 copy-start.12
  579.6 4.9 copy-start.17
  579.6 4.9 copy-start.28
  579.6 4.9 copy-start.35
  579.7 4.9 copy-start.55
  579.7 4.9 copy-start.62
  582.5 4.4 copy-start.25
  586.9 3.7 copy-start.24
  590.6 3.7 copy-start.23
  590.6 5.7 copy-start.1
  (31 other events, 56.0 us)
Sparse Core Ops, SparseCore 0:
  11.0 136.6 all-gather.2
